TPU v7x, 16 devices: a 4x2x1 block of a 4x4x8 slice. The times are simulated.
16 devices in a mesh: replica: 2 (over y, z), model: 8 (over x, core).
Axes of the slice: x: 4, y: 2, z: 1, core: 2. Of those that a mesh axis runs over, the one named last changes fastest.
The devices are a block of a 4x4x8 slice.
Arguments:
- prompt: bfloat16 [32, 768, 2048], P('replica', 'model'), parts along dimension 0
- lengths: int32 [32], P('replica'), parts along dimension 0
- new_tok: bfloat16 [32, 2048], P('replica'), parts along dimension 0
- norm_attn: bfloat16 [1, 2048], replicated
- w_q: bfloat16 [1, 2048, 2048], P(None, None, 'model')
- w_k: bfloat16 [1, 2048, 2048], P(None, None, 'model')
- w_v: bfloat16 [1, 2048, 2048], P(None, None, 'model')
- w_o: bfloat16 [1, 2048, 2048], P(None, 'model')
- norm_mlp: bfloat16 [1, 2048], replicated
- w_gate: bfloat16 [1, 2048, 8192], P(None, None, 'model')
- w_up: bfloat16 [1, 2048, 8192], P(None, None, 'model')
- w_down: bfloat16 [1, 8192, 2048], P(None, 'model')
Outputs:
- output 1: bfloat16 [32, 2048], P('replica'), parts along dimension 0
- output 2: bfloat16 [32, 2048], P('replica'), parts along dimension 0
- output 3: bfloat16 [1, 32, 769, 16, 128], P(None, 'replica', None, 'model'), parts along dimension 1
- output 4: bfloat16 [1, 32, 769, 16, 128], P(None, 'replica', None, 'model'), parts along dimension 1
There are 2 independent parts. A program takes and returns all parts, laid end to end along the dimension named above; an argument that names none is the same for every part.
All inputs are finite; a program needn't handle non-finite values.
Results may differ from a plain program's by a relative error of at most 0.0109685.
Values are sent between devices in bfloat16 or wider.
A program may use at most 768 MiB of HBM per device.

v0:
```python
import jax
import jax.numpy as jnp
from jax import lax
from jax.sharding import PartitionSpec as P

HEAD_DIM = 128
NEG_BIG = -1e30


def rms_norm(hidden, gain_vec):
    hid_f32 = hidden.astype(jnp.float32)
    inv_rms = lax.rsqrt(jnp.mean(hid_f32 * hid_f32, axis=-1, keepdims=True) + 1e-5)
    return (hid_f32 * inv_rms * gain_vec.astype(jnp.float32)).astype(jnp.bfloat16)


def rotary(heads_f32, positions):
    half_dim = HEAD_DIM // 2
    inv_freq = 10000.0 ** (-2.0 * jnp.arange(half_dim, dtype=jnp.float32) / HEAD_DIM)
    angles = positions.astype(jnp.float32)[..., None] * inv_freq
    cos_tab = jnp.cos(angles)[..., None, :]
    sin_tab = jnp.sin(angles)[..., None, :]
    lo_half = heads_f32[..., :half_dim]
    hi_half = heads_f32[..., half_dim:]
    return jnp.concatenate([lo_half * cos_tab - hi_half * sin_tab, hi_half * cos_tab + lo_half * sin_tab], axis=-1)


def block_attention(q_block, key_blocks, val_blocks, lengths, q_start, n_used):
    n_batch, blk_len, n_heads, _ = q_block.shape
    kv_heads = key_blocks.shape[3]
    n_group = n_heads // kv_heads
    q_grouped = q_block.reshape(n_batch, blk_len, kv_heads, n_group, HEAD_DIM)
    q_pos = q_start + jnp.arange(blk_len)
    score_scale = HEAD_DIM ** -0.5

    def step_fn(blk_idx, loop_state):
        run_max, run_sum, run_acc = loop_state
        key_blk = lax.dynamic_index_in_dim(key_blocks, blk_idx, axis=0, keepdims=False)
        val_blk = lax.dynamic_index_in_dim(val_blocks, blk_idx, axis=0, keepdims=False)
        k_pos = blk_idx * blk_len + jnp.arange(blk_len)
        scores = jnp.einsum('bqhgd,bkhd->bqhgk', q_grouped, key_blk, preferred_element_type=jnp.float32) * score_scale
        visible = (k_pos[None, None, :] <= q_pos[None, :, None]) & (k_pos[None, None, :] < lengths[:, None, None])
        scores = jnp.where(visible[:, :, None, None, :], scores, NEG_BIG)
        new_max = jnp.maximum(run_max, jnp.max(scores, axis=-1))
        rescale = jnp.exp(run_max - new_max)
        attn_prob = jnp.exp(scores - new_max[..., None])
        run_sum = run_sum * rescale + jnp.sum(attn_prob, axis=-1)
        run_acc = run_acc * rescale[..., None] + jnp.einsum('bqhgk,bkhd->bqhgd', attn_prob.astype(jnp.bfloat16), val_blk, preferred_element_type=jnp.float32)
        return new_max, run_sum, run_acc

    stat_shape = (n_batch, blk_len, kv_heads, n_group)
    init_state = (jnp.full(stat_shape, NEG_BIG, jnp.float32), jnp.zeros(stat_shape, jnp.float32), jnp.zeros(stat_shape + (HEAD_DIM,), jnp.float32))
    run_max, run_sum, run_acc = lax.fori_loop(0, n_used, step_fn, init_state)
    return (run_acc / run_sum[..., None]).reshape(n_batch, blk_len, n_heads * HEAD_DIM).astype(jnp.bfloat16)


def decode_attention(q_new, key_cache, val_cache, lengths):
    n_batch, n_heads, _ = q_new.shape
    kv_heads = key_cache.shape[2]
    cache_len = key_cache.shape[1]
    q_grouped = q_new.reshape(n_batch, kv_heads, n_heads // kv_heads, HEAD_DIM)
    scores = jnp.einsum('bhgd,bkhd->bhgk', q_grouped, key_cache, preferred_element_type=jnp.float32) * (HEAD_DIM ** -0.5)
    cache_pos = jnp.arange(cache_len)
    visible = (cache_pos[None, :] < lengths[:, None]) | (cache_pos[None, :] == cache_len - 1)
    scores = jnp.where(visible[:, None, None, :], scores, NEG_BIG)
    attn_prob = jax.nn.softmax(scores, axis=-1)
    out_f32 = jnp.einsum('bhgk,bkhd->bhgd', attn_prob.astype(jnp.bfloat16), val_cache, preferred_element_type=jnp.float32)
    return out_f32.reshape(n_batch, n_heads * HEAD_DIM).astype(jnp.bfloat16)


def decode_layer(dec_hidden, key_mine, val_mine, lengths, gain_attn, wq_loc, wk_loc, wv_loc, wo_loc, gain_mlp, wg_loc, wu_loc, wd_loc):
    n_batch = dec_hidden.shape[0]
    heads_loc = wq_loc.shape[1] // HEAD_DIM
    kv_loc = wk_loc.shape[1] // HEAD_DIM
    tok_norm = rms_norm(dec_hidden, gain_attn)
    q_new = rotary(jnp.dot(tok_norm, wq_loc, preferred_element_type=jnp.float32).reshape(n_batch, heads_loc, HEAD_DIM), lengths).astype(jnp.bfloat16)
    k_new = rotary(jnp.dot(tok_norm, wk_loc, preferred_element_type=jnp.float32).reshape(n_batch, kv_loc, HEAD_DIM), lengths).astype(jnp.bfloat16)
    v_new = jnp.dot(tok_norm, wv_loc, preferred_element_type=jnp.float32).astype(jnp.bfloat16).reshape(n_batch, kv_loc, HEAD_DIM)
    key_cache = jnp.concatenate([key_mine, k_new[:, None]], axis=1)
    val_cache = jnp.concatenate([val_mine, v_new[:, None]], axis=1)
    tok_attn = decode_attention(q_new, key_cache, val_cache, lengths)
    attn_part = jnp.dot(tok_attn, wo_loc, preferred_element_type=jnp.float32)
    dec_hidden = (dec_hidden.astype(jnp.float32) + lax.psum(attn_part, 'model')).astype(jnp.bfloat16)
    tok_norm = rms_norm(dec_hidden, gain_mlp)
    tok_mid = (jax.nn.silu(jnp.dot(tok_norm, wg_loc, preferred_element_type=jnp.float32)) * jnp.dot(tok_norm, wu_loc, preferred_element_type=jnp.float32)).astype(jnp.bfloat16)
    mlp_part = jnp.dot(tok_mid, wd_loc, preferred_element_type=jnp.float32)
    dec_hidden = (dec_hidden.astype(jnp.float32) + lax.psum(mlp_part, 'model')).astype(jnp.bfloat16)
    return dec_hidden, key_cache, val_cache


def solution(mesh):
    n_dev = mesh.shape['model']
    seq_spec = P('replica', 'model', None)
    col_spec = P(None, None, 'model')
    row_spec = P(None, 'model', None)
    gain_spec = P(None, None)
    tok_spec = P('replica', None)
    cache_spec = P(None, 'replica', None, 'model', None)
    in_specs = (seq_spec, P('replica'), tok_spec, gain_spec, col_spec, col_spec, col_spec, row_spec, gain_spec, col_spec, col_spec, row_spec)
    out_specs = (tok_spec, tok_spec, cache_spec, cache_spec)

    def per_device(prompt, lengths, new_tok, norm_attn, w_q, w_k, w_v, w_o, norm_mlp, w_gate, w_up, w_down):
        my_idx = lax.axis_index('model')
        n_batch, seq_loc, d_model = prompt.shape
        n_tok = n_batch * seq_loc
        kv_loc = w_k.shape[2] // HEAD_DIM
        n_heads = (w_q.shape[2] // HEAD_DIM) * n_dev
        kv_heads = kv_loc * n_dev
        seq_len = seq_loc * n_dev
        seq_pos = my_idx * seq_loc + jnp.arange(seq_loc)
        hidden = prompt
        dec_hidden = new_tok
        key_layers = []
        val_layers = []
        for layer_idx in range(w_q.shape[0]):
            wq_full = lax.all_gather(w_q[layer_idx], 'model', axis=1, tiled=True)
            wk_full = lax.all_gather(w_k[layer_idx], 'model', axis=1, tiled=True)
            wv_full = lax.all_gather(w_v[layer_idx], 'model', axis=1, tiled=True)
            wo_full = lax.all_gather(w_o[layer_idx], 'model', axis=0, tiled=True)
            wg_full = lax.all_gather(w_gate[layer_idx], 'model', axis=1, tiled=True)
            wu_full = lax.all_gather(w_up[layer_idx], 'model', axis=1, tiled=True)
            wd_full = lax.all_gather(w_down[layer_idx], 'model', axis=0, tiled=True)
            normed = rms_norm(hidden, norm_attn[layer_idx]).reshape(n_tok, d_model)
            q_rot = rotary(jnp.dot(normed, wq_full, preferred_element_type=jnp.float32).reshape(n_batch, seq_loc, n_heads, HEAD_DIM), seq_pos).astype(jnp.bfloat16)
            k_rot = rotary(jnp.dot(normed, wk_full, preferred_element_type=jnp.float32).reshape(n_batch, seq_loc, kv_heads, HEAD_DIM), seq_pos).astype(jnp.bfloat16)
            v_proj = jnp.dot(normed, wv_full, preferred_element_type=jnp.float32).astype(jnp.bfloat16).reshape(n_batch, seq_loc, kv_heads, HEAD_DIM)
            key_blocks = lax.all_gather(k_rot, 'model', axis=0)
            val_blocks = lax.all_gather(v_proj, 'model', axis=0)
            attn_out = block_attention(q_rot, key_blocks, val_blocks, lengths, my_idx * seq_loc, my_idx + 1).reshape(n_tok, n_heads * HEAD_DIM)
            hidden = (hidden.astype(jnp.float32) + jnp.dot(attn_out, wo_full, preferred_element_type=jnp.float32).reshape(n_batch, seq_loc, d_model)).astype(jnp.bfloat16)
            normed = rms_norm(hidden, norm_mlp[layer_idx]).reshape(n_tok, d_model)
            mlp_mid = (jax.nn.silu(jnp.dot(normed, wg_full, preferred_element_type=jnp.float32)) * jnp.dot(normed, wu_full, preferred_element_type=jnp.float32)).astype(jnp.bfloat16)
            hidden = (hidden.astype(jnp.float32) + jnp.dot(mlp_mid, wd_full, preferred_element_type=jnp.float32).reshape(n_batch, seq_loc, d_model)).astype(jnp.bfloat16)
            key_mine = jnp.moveaxis(lax.dynamic_slice_in_dim(key_blocks, my_idx * kv_loc, kv_loc, axis=3), 0, 1).reshape(n_batch, seq_len, kv_loc, HEAD_DIM)
            val_mine = jnp.moveaxis(lax.dynamic_slice_in_dim(val_blocks, my_idx * kv_loc, kv_loc, axis=3), 0, 1).reshape(n_batch, seq_len, kv_loc, HEAD_DIM)
            dec_hidden, key_cache, val_cache = decode_layer(dec_hidden, key_mine, val_mine, lengths, norm_attn[layer_idx], w_q[layer_idx], w_k[layer_idx], w_v[layer_idx], w_o[layer_idx], norm_mlp[layer_idx], w_gate[layer_idx], w_up[layer_idx], w_down[layer_idx])
            key_layers.append(key_cache)
            val_layers.append(val_cache)
        last_sel = (seq_pos[None, :] == (lengths - 1)[:, None]).astype(jnp.bfloat16)
        last_part = jnp.einsum('bs,bsd->bd', last_sel, hidden, preferred_element_type=jnp.float32)
        last_hidden = lax.psum(last_part, 'model').astype(jnp.bfloat16)
        return dec_hidden, last_hidden, jnp.stack(key_layers), jnp.stack(val_layers)

    return jax.shard_map(per_device, mesh=mesh, in_specs=in_specs, out_specs=out_specs, check_vma=False)
```

profile of v0, /device:TPU:113, one launch (start us, length us, event | category | flops | bytes accessed | tf_op | source)
XLA Modules:
  0.0 1409.4 jit_solution(6268706973719453212)
XLA Ops:
  19.0 42.7 %all-gather.23.cloned.1.call-done = bf16[1,2048,2048]{2,1,0:T(8,128)(2,1)} async-done(((bf16[1,2048,256]{2,1,0:T(8,128)(2,1)}), bf16[1,2048,2048]{2,1,0:T(8,128)(2,1)}) %all-gather.23.cloned.1.call-update) | async-done | bytes 8388624 | tf_op jit(solution)/shard_map/all_gather | solution.py:117
  61.7 17.3 %fusion.65 = bf16[192,8,16,128]{3,1,2,0:T(8,128)(2,1)S(1)} fusion(bf16[1536,2048]{1,0:T(8,128)(2,1)} %bitcast.241, bf16[1,2048,2048]{2,1,0:T(8,128)(2,1)} %all-gather.23.cloned.1.call-done), kind=kOutput, calls=%fused_computation.85 | convolution fusion | flops 12888047616 | bytes 20971520 | tf_op jit(solution)/shard_map/dot_general | solution.py:125
  84.6 28.4 %all-gather.25.cloned.1.call-done = bf16[1,2048,2048]{2,1,0:T(8,128)(2,1)} async-done(((bf16[1,2048,256]{2,1,0:T(8,128)(2,1)}), bf16[1,2048,2048]{2,1,0:T(8,128)(2,1)}) %all-gather.25.cloned.1.call-update) | async-done | bytes 8388624 | tf_op jit(solution)/shard_map/all_gather | solution.py:115
  113.0 12.3 copy.74
  125.4 39.0 %all-gather.21.cloned.1.call-done = bf16[1,2048,2048]{2,1,0:T(8,128)(2,1)} async-done(((bf16[1,2048,256]{2,1,0:T(8,128)(2,1)}), bf16[1,2048,2048]{2,1,0:T(8,128)(2,1)}) %all-gather.21.cloned.1.call-update) | async-done | bytes 8388624 | tf_op jit(solution)/shard_map/all_gather | solution.py:116
  164.4 12.4 copy.67
  176.8 19.7 %fusion.49 = f32[16,96,16,128]{3,1,2,0:T(8,128)} fusion(bf16[16,128,2048,1]{2,1,0,3:T(8,128)(2,1)} %bitcast.238, bf16[16,96,2048]{2,1,0:T(8,128)(2,1)} %fusion.30), kind=kOutput, calls=%fused_computation.71 | convolution fusion | flops 12884901888 | bytes 27262976 | tf_op jit(solution)/shard_map/dot_general | solution.py:123
  196.5 15.7 %fusion.51 = f32[16,96,16,128]{3,1,2,0:T(8,128)} fusion(bf16[16,128,2048,1]{2,1,0,3:T(8,128)(2,1)S(1)} %bitcast.239, bf16[16,96,2048]{2,1,0:T(8,128)(2,1)S(1)} %bitcast.243), kind=kOutput, calls=%fused_computation.73 | convolution fusion | flops 12884901888 | bytes 27262976 | tf_op jit(solution)/shard_map/dot_general | solution.py:124
  212.2 27.9 %fusion.45 = (bf16[16,96,16,1,64]{4,1,2,0,3:T(8,128)(2,1)}, bf16[16,96,16,1,64]{4,1,2,0,3:T(8,128)(2,1)}, bf16[1,16,96,16,64]{4,2,3,1,0:T(8,128)(2,1)}, bf16[1,16,96,16,64]{4,2,3,1,0:T(8,128)(2,1)}) fusion(f32[16,96,16,128]{3,1,2,0:T(8,128)} %fusion.49, f32[96,64]{1,0:T(8,128)S(1)} %get-tuple-element.173, f32[96,64]{1,0:T(8,128)S(1)} %get-tuple-element.172, ...), kind=kLoop, calls=%fused_computation.66 | loop fusion | flops 25165824 | bytes 37797888 | tf_op jit(solution)/shard_map/concatenate | solution.py:24
  262.1 9.8 pad_maximum_fusion.3
  271.9 119.3 %all-gather.19.cloned.1.call-done = bf16[8,16,96,16,128]{4,3,2,1,0:T(8,128)(2,1)} async-done(((bf16[1,16,96,16,128]{4,3,2,1,0:T(8,128)(2,1)}), bf16[8,16,96,16,128]{4,3,2,1,0:T(8,128)(2,1)}) %all-gather.19.cloned.1.call-update) | async-done | bytes 50331664 | tf_op jit(solution)/shard_map/all_gather | solution.py:127
  391.2 225.0 %all-gather.17.cloned.1.call-done = bf16[8,16,96,16,128]{4,3,2,1,0:T(8,128)(2,1)} async-done(((bf16[1,16,96,16,128]{4,3,2,1,0:T(8,128)(2,1)}), bf16[8,16,96,16,128]{4,3,2,1,0:T(8,128)(2,1)}) %all-gather.17.cloned.1.call-update) | async-done | bytes 50331664 | tf_op jit(solution)/shard_map/all_gather | solution.py:126
  616.2 27.7 %constant_dynamic-slice_fusion.2 = (bf16[8,16,96,2,128]{4,3,2,1,0:T(2,128)(2,1)}, bf16[8,16,96,2,128]{4,3,2,1,0:T(2,128)(2,1)}) fusion(bf16[8,16,96,16,128]{4,3,2,1,0:T(8,128)(2,1)} %all-gather.19.cloned.1.call-done, s32[]{:T(128)S(6)} %select_n.18, bf16[8,16,96,16,128]{4,3,2,1,0:T(8,128)(2,1)} %all-gather.17.cloned.1.call-done), kind=kLoop, calls=%fused_computation.152 | loop fusion | bytes 25165828 | tf_op jit(solution)/shard_map/dynamic_slice | solution.py:134
  667.6 100.3 %while.15 = (s32[]{:T(128)}, f32[16,96,16,1]{1,2,0,3:T(8,128)S(1)}, f32[16,96,16,1]{1,2,0,3:T(8,128)S(1)}, f32[16,96,16,1,128]{4,1,2,0,3:T(8,128)}, s32[]{:T(128...) while((s32[]{:T(128)}, f32[16,96,16,1]{1,2,0,3:T(8,128)S(1)}, ...), condition=%wide.region_10.11_spmd.clone, body=%wide.region_7.10_spmd.clone.sunk | while | flops 1240435456 | bytes 137452704 | solution.py:52
  668.5 12.8 constant_dynamic-slice_fusion.5
  681.4 13.5 fusion.153
  694.9 8.6 fusion.155
  703.6 14.3 %bitcast_add_fusion.5 = f32[16,96,16,1,128]{4,1,2,0,3:T(8,128)} fusion(f32[16,96,16,1,128]{4,1,2,0,3:T(8,128)} %get-tuple-element.277, f32[16,96,16]{1,2,0:T(8,128)S(1)} %get-tuple-element.258, f32[16,16,96,96]{3,2,1,0:T(8,128)S(1)} %copy-done, f32[16,96,16]{1,2,0:T(8,128)S(1)} %bitcast.225, pred[16,96,96]{1,2,0:T(8,128)(4,1)S(1)} %broadcast_and_fusion.2, ...), kind=kOutput, calls=%fused_computation.1.clone.1 | convolution fusion | flops 619708416 | bytes 41238528 | tf_op jit(solution)/shard_map/while/body/bqhgk,bkhd->bqhgd/dot_general | solution.py:47
  718.4 12.8 constant_dynamic-slice_fusion.5
  731.2 13.5 fusion.153
  744.8 8.6 fusion.155
  753.5 14.3 %bitcast_add_fusion.5 = f32[16,96,16,1,128]{4,1,2,0,3:T(8,128)} fusion(f32[16,96,16,1,128]{4,1,2,0,3:T(8,128)} %get-tuple-element.277, f32[16,96,16]{1,2,0:T(8,128)S(1)} %get-tuple-element.258, f32[16,16,96,96]{3,2,1,0:T(8,128)S(1)} %copy-done, f32[16,96,16]{1,2,0:T(8,128)S(1)} %bitcast.225, pred[16,96,96]{1,2,0:T(8,128)(4,1)S(1)} %broadcast_and_fusion.2, ...), kind=kOutput, calls=%fused_computation.1.clone.1 | convolution fusion | flops 619708416 | bytes 41238528 | tf_op jit(solution)/shard_map/while/body/bqhgk,bkhd->bqhgd/dot_general | solution.py:47
  781.0 10.3 convert_element_type.149
  791.3 20.9 %fusion.32 = (f32[16,96]{1,0:T(8,128)S(1)}, bf16[16,96,2048]{2,1,0:T(8,128)(2,1)}) fusion(bf16[16,96,2048]{2,1,0:T(8,128)(2,1)} %convert_element_type.149, bf16[1,2048,2048]{2,1,0:T(8,128)(2,1)} %all-gather.27.cloned.1.call-done, bf16[16,96,2048]{2,1,0:T(8,128)(2,1)} %param.14), kind=kOutput, calls=%fused_computation.48 | convolution fusion | flops 12903774208 | bytes 27269120 | tf_op jit(solution)/shard_map/dot_general | solution.py:129
  826.1 60.6 %fusion.24 = f32[1536,8192]{1,0:T(8,128)} fusion(bf16[1536,2048]{1,0:T(8,128)(2,1)} %bitcast.244, bf16[1,2048,8192]{2,1,0:T(8,128)(2,1)} %all-gather.29.cloned.1.call-done), kind=kOutput, calls=%fused_computation.36 | convolution fusion | flops 51539607552 | bytes 90177536 | tf_op jit(solution)/shard_map/dot_general | solution.py:131
  886.7 85.8 %all-gather.31.cloned.1.call-done = bf16[1,2048,8192]{2,1,0:T(8,128)(2,1)} async-done(((bf16[1,2048,1024]{2,1,0:T(8,128)(2,1)}), bf16[1,2048,8192]{2,1,0:T(8,128)(2,1)}) %all-gather.31.cloned.1.call-update) | async-done | bytes 33554448 | tf_op jit(solution)/shard_map/all_gather | solution.py:120
  972.5 67.0 %multiply_convert_fusion.clone.4 = bf16[1536,8192]{1,0:T(8,128)(2,1)} fusion(f32[1536,8192]{1,0:T(8,128)} %fusion.24, bf16[1536,2048]{1,0:T(8,128)(2,1)} %bitcast.245, bf16[1,2048,8192]{2,1,0:T(8,128)(2,1)} %all-gather.31.cloned.1.call-done), kind=kOutput, calls=%fused_computation.32.clone.clone.clone.1 | convolution fusion | flops 51615105024 | bytes 115343360 | tf_op jit(solution)/shard_map/dot_general | solution.py:131
  1039.4 88.3 %all-gather.33.cloned.1.call-done = bf16[1,8192,2048]{2,1,0:T(8,128)(2,1)} async-done(((bf16[1,1024,2048]{2,1,0:T(8,128)(2,1)}), bf16[1,8192,2048]{2,1,0:T(8,128)(2,1)}) %all-gather.33.cloned.1.call-update) | async-done | bytes 33554448 | tf_op jit(solution)/shard_map/all_gather | solution.py:121
  1127.7 61.0 %fusion.21 = f32[1536,2048]{1,0:T(8,128)} fusion(bf16[1,8192,2048]{2,1,0:T(8,128)(2,1)} %all-gather.33.cloned.1.call-done, bf16[1536,8192]{1,0:T(8,128)(2,1)} %multiply_convert_fusion.clone.4), kind=kOutput, calls=%fused_computation.33 | convolution fusion | flops 51539607552 | bytes 71303168 | tf_op jit(solution)/shard_map/dot_general | solution.py:132
  1207.8 148.3 %all-reduce.7 = bf16[16,2048]{1,0:T(8,128)(2,1)} all-reduce(f32[16,2048]{1,0:T(8,128)S(1)} %bitcast.250), channel_id=1, replica_groups=mesh['replica'=2,'model'=8] {'model'}, use_global_device_ids=true, to_apply=%region_12.13 | all-reduce | flops 32768 | bytes 196608 | tf_op jit(solution)/shard_map/psum | solution.py:140
  1356.1 25.1 %copy.78 = bf16[1,16,769,2,128]{4,3,2,1,0:T(2,128)(2,1)} copy(bf16[1,16,769,2,128]{4,2,3,1,0:T(8,128)(2,1)} %fusion.61) | data formatting | bytes 12599296
  1381.3 19.8 %copy.79 = bf16[1,16,769,2,128]{4,3,2,1,0:T(2,128)(2,1)} copy(bf16[1,16,769,2,128]{4,2,3,1,0:T(8,128)(2,1)S(1)} %bitcast.227) | data formatting | bytes 12599296
  (153 shorter events, 111.4 us)
Async XLA Ops:
  7.2 54.5 %all-gather.23.cloned.1.call-start = ((), (), s32[]{:S(2)}) async-start(), calls=%async_computation.5 | async-start | bytes 9437184 | tf_op jit(solution)/shard_map/all_gather | solution.py:117
  8.0 105.1 %all-gather.25.cloned.1.call-start = ((), (), s32[]{:S(2)}) async-start(), calls=%async_computation.6 | async-start | bytes 9437184 | tf_op jit(solution)/shard_map/all_gather | solution.py:115
  8.8 155.6 %all-gather.21.cloned.1.call-start = ((), (), s32[]{:S(2)}) async-start(), calls=%async_computation.4 | async-start | bytes 9437184 | tf_op jit(solution)/shard_map/all_gather | solution.py:116
  9.6 381.6 %all-gather.19.cloned.1.call-start = ((), (), s32[]{:S(2)}) async-start(), calls=%async_computation.1 | async-start | bytes 56623104 | tf_op jit(solution)/shard_map/all_gather | solution.py:127
  9.6 5.1 copy-start.1
  84.1 532.1 %all-gather.17.cloned.1.call-start = ((), (), s32[]{:S(2)}) async-start(), calls=%async_computation | async-start | bytes 56623104 | tf_op jit(solution)/shard_map/all_gather | solution.py:126
  164.4 32.1 %slice-start.4 = ((s8[6291456]{0:T(1024)(128)(4,1)}), s8[2097152]{0:T(1024)(128)(4,1)S(1)}, s32[]{:S(2)}) async-start(s8[6291456]{0:T(1024)(128)(4,1)} %bitcast.242), calls=%async_computation.15 | async-start | bytes 4194304
  176.8 19.7 %copy-start.5 = (bf16[2048,2048]{1,0:T(8,128)(2,1)S(1)}, bf16[2048,2048]{1,0:T(8,128)(2,1)}, u32[]{:S(2)}) copy-start(bf16[2048,2048]{1,0:T(8,128)(2,1)} %copy.67) | copy-start | bytes 25165828
  176.8 19.7 %slice-start.5 = ((s8[6291456]{0:T(1024)(128)(4,1)}), s8[4194304]{0:T(1024)(128)(4,1)S(1)}, s32[]{:S(2)}) async-start(s8[6291456]{0:T(1024)(128)(4,1)} %bitcast.242), calls=%async_computation.16 | async-start | bytes 8388608
  252.5 538.7 %all-gather.27.cloned.1.call-start = ((), (), s32[]{:S(2)}) async-start(), calls=%async_computation.7 | async-start | bytes 9437184 | tf_op jit(solution)/shard_map/all_gather | solution.py:118
  253.2 572.9 %all-gather.29.cloned.1.call-start = ((), (), s32[]{:S(2)}) async-start(), calls=%async_computation.8 | async-start | bytes 37748736 | tf_op jit(solution)/shard_map/all_gather | solution.py:119
  254.0 6.6 copy-start.21
  254.0 718.5 %all-gather.31.cloned.1.call-start = ((), (), s32[]{:S(2)}) async-start(), calls=%async_computation.9 | async-start | bytes 37748736 | tf_op jit(solution)/shard_map/all_gather | solution.py:120
  254.8 872.9 %all-gather.33.cloned.1.call-start = ((), (), s32[]{:S(2)}) async-start(), calls=%async_computation.10 | async-start | bytes 37748736 | tf_op jit(solution)/shard_map/all_gather | solution.py:121
  255.6 942.8 %all-reduce.4.cloned.1.call-start = ((), (), s32[]{:S(2)}) async-start(), calls=%async_computation.2 | async-start | bytes 262144 | tf_op jit(solution)/shard_map/psum | solution.py:82
  256.2 400.9 %copy-start.14 = (bf16[16,1,2,128]{3,1,2,0:T(2,128)(2,1)}, bf16[16,1,2,128]{3,1,2,0:T(2,128)(2,1)S(1)}, u32[]{:S(2)}) copy-start(bf16[16,1,2,128]{3,1,2,0:T(2,128)(2,1)S(1)} %broadcast_in_dim_reshape.4) | copy-start | bytes 24580
  260.6 391.8 %copy-start.16 = (bf16[16,1,2,128]{3,1,2,0:T(2,128)(2,1)}, bf16[16,1,2,128]{3,1,2,0:T(2,128)(2,1)S(1)}, u32[]{:S(2)}) copy-start(bf16[16,1,2,128]{3,1,2,0:T(2,128)(2,1)S(1)} %copy.71) | copy-start | bytes 24580
  643.9 7.0 slice-start.2
  643.9 7.0 slice-start.3
  694.9 8.7 copy-start
  744.8 8.7 copy-start
  791.2 20.9 %copy-start.9 = (bf16[1,256,2048]{2,1,0:T(8,128)(2,1)S(1)}, bf16[1,256,2048]{2,1,0:T(8,128)(2,1)}, u32[]{:S(2)}) copy-start(bf16[1,256,2048]{2,1,0:T(8,128)(2,1)} %param.21) | copy-start | bytes 3145732
  791.2 20.9 %copy-start.19 = (bf16[16,2,128]{2,1,0:T(2,128)(2,1)S(1)}, bf16[16,2,128]{2,1,0:T(2,128)(2,1)}, u32[]{:S(2)}) copy-start(bf16[16,2,128]{2,1,0:T(2,128)(2,1)} %convert_element_type.141) | copy-start | bytes 24580
  791.2 21.9 %copy-start.17 = (bf16[16,1,2,128]{3,1,2,0:T(2,128)(2,1)S(1)}, bf16[16,1,2,128]{3,1,2,0:T(2,128)(2,1)}, u32[]{:S(2)}) copy-start(bf16[16,1,2,128]{3,1,2,0:T(2,128)(2,1)} %copy-done.16) | copy-start | bytes 24580
  812.2 7.0 copy-start.12
  819.1 582.0 %all-reduce.6.cloned.1.call-start = ((), (), s32[]{:S(2)}) async-start(), calls=%async_computation.3 | async-start | bytes 262144 | tf_op jit(solution)/shard_map/psum | solution.py:86
  1039.4 149.3 %copy-start.18 = (pred[16,96,1]{1,0,2:T(8,128)(4,1)S(1)}, pred[16,96,1]{1,0,2:T(8,128)(4,1)}, u32[]{:S(2)}) copy-start(pred[16,96,1]{1,0,2:T(8,128)(4,1)} %compare_bitcast_fusion) | copy-start | bytes 4612
  1127.7 61.1 %copy-start.4 = (bf16[16,96,2048]{2,1,0:T(8,128)(2,1)S(1)}, bf16[16,96,2048]{2,1,0:T(8,128)(2,1)}, u32[]{:S(2)}) copy-start(bf16[16,96,2048]{2,1,0:T(8,128)(2,1)} %get-tuple-element.179) | copy-start | bytes 18874372
  1188.8 6.4 copy-start.2
  1188.8 6.4 copy-start.15
  1207.7 173.5 %slice-start = ((s8[6356992]{0:T(1024)(128)(4,1)}), s8[2162688]{0:T(1024)(128)(4,1)S(1)}, s32[]{:S(2)}) async-start(s8[6356992]{0:T(1024)(128)(4,1)} %bitcast.226), calls=%async_computation.11 | async-start | bytes 4325376
  1356.1 25.1 %slice-start.1 = ((s8[6356992]{0:T(1024)(128)(4,1)}), s8[4194304]{0:T(1024)(128)(4,1)S(1)}, s32[]{:S(2)}) async-start(s8[6356992]{0:T(1024)(128)(4,1)} %bitcast.226), calls=%async_computation.12 | async-start | bytes 8388608
  (8 other events, 30.6 us)
Sparse Core Ops, SparseCore 0:
  9.6 52.1 all-gather.22
  63.3 49.7 all-gather.24
  114.6 49.7 all-gather.20
  166.4 224.8 all-gather.18
  392.6 223.5 all-gather.16
  617.7 45.0 all-gather.26
  664.4 152.8 all-gather.28
  818.9 153.5 all-gather.30
  974.1 153.5 all-gather.32
  1129.9 49.8 all-reduce.3
  1207.9 173.2 all-reduce.5
where the time goes:
time: 1420 us; the launch traced here: 1410 us
  waiting for transfers between devices  634 us (45%)
  matrix products  341 us (24%)
  local copies, waits for them, and re-layouts  169 us (12%)
  blocking collectives  148 us (10%)
  other arithmetic  102 us (7%)
  between operations  14.5 us (1%)
    all_gather x1, waiting for transfers between devices, per_device(): key_blocks = lax.all_gather(k_rot, 'model', axis=0)  225 us
    psum x1, blocking collectives, per_device(): last_hidden = lax.psum(last_part, 'model').astype(jnp.bfloat16)  148 us
    all_gather x1, waiting for transfers between devices, per_device(): val_blocks = lax.all_gather(v_proj, 'model', axis=0)  119 us
    all_gather x1, waiting for transfers between devices, per_device(): wd_full = lax.all_gather(w_down[layer_idx], 'model', axis=0, tiled=True)  88.3 us
    all_gather x1, waiting for transfers between devices, per_device(): wu_full = lax.all_gather(w_up[layer_idx], 'model', axis=1, tiled=True)  85.8 us
    dot_general x1, matrix products, per_device(): jnp.dot(normed, wu_full, preferred_element_type=jnp.float32)  67 us
    unnamed x59, local copies, waits for them, and re-layouts  61.4 us
    dot_general x1, matrix products, per_device(): jnp.dot(mlp_mid, wd_full, preferred_element_type=jnp.float32)  61 us
  transfers between devices with their start and end apart: 11, of which 7 were waited for; matrix products, arithmetic and copies ran while one was open for 42% of the time, Pallas kernels for 0%

commit v1 on v0

v1 whole, which is shorter than its diff:
```python
import jax
import jax.numpy as jnp
from jax import lax
from jax.sharding import PartitionSpec as P

HEAD_DIM = 128
NEG_BIG = -1e30
N_CHUNKS = 4


def rms_norm(hidden, gain_vec):
    hid_f32 = hidden.astype(jnp.float32)
    inv_rms = lax.rsqrt(jnp.mean(hid_f32 * hid_f32, axis=-1, keepdims=True) + 1e-5)
    return (hid_f32 * inv_rms * gain_vec.astype(jnp.float32)).astype(jnp.bfloat16)


def rotary(heads_f32, positions):
    half_dim = HEAD_DIM // 2
    inv_freq = 10000.0 ** (-2.0 * jnp.arange(half_dim, dtype=jnp.float32) / HEAD_DIM)
    angles = positions.astype(jnp.float32)[..., None] * inv_freq
    cos_tab = jnp.cos(angles)[..., None, :]
    sin_tab = jnp.sin(angles)[..., None, :]
    lo_half = heads_f32[..., :half_dim]
    hi_half = heads_f32[..., half_dim:]
    return jnp.concatenate([lo_half * cos_tab - hi_half * sin_tab, hi_half * cos_tab + lo_half * sin_tab], axis=-1)


def dot_f32(lhs, rhs):
    return jnp.dot(lhs, rhs, preferred_element_type=jnp.float32)


def solution(mesh):
    n_dev = mesh.shape['model']
    seq_spec = P('replica', 'model', None)
    col_spec = P(None, None, 'model')
    row_spec = P(None, 'model', None)
    gain_spec = P(None, None)
    tok_spec = P('replica', None)
    cache_spec = P(None, 'replica', None, 'model', None)
    in_specs = (seq_spec, P('replica'), tok_spec, gain_spec, col_spec, col_spec, col_spec, row_spec, gain_spec, col_spec, col_spec, row_spec)
    out_specs = (tok_spec, tok_spec, cache_spec, cache_spec)

    def per_device(prompt, lengths, new_tok, norm_attn, w_q, w_k, w_v, w_o, norm_mlp, w_gate, w_up, w_down):
        my_idx = lax.axis_index('model')
        n_batch, seq_loc, d_model = prompt.shape
        heads = w_q.shape[2] // HEAD_DIM
        seq_len = seq_loc * n_dev
        wq, wk, wv, wo, wg, wu, wd = w_q[0], w_k[0], w_v[0], w_o[0], w_gate[0], w_up[0], w_down[0]
        normed = rms_norm(prompt, norm_attn[0])
        last_loc = lengths - 1 - my_idx * seq_loc
        mine = (last_loc >= 0) & (last_loc < seq_loc)
        picked = jnp.take_along_axis(prompt, jnp.clip(last_loc, 0, seq_loc - 1)[:, None, None], axis=1)[:, 0]
        last_x = lax.psum(jnp.where(mine[:, None], picked, 0).astype(jnp.float32), 'model').astype(jnp.bfloat16)

        pos = jnp.arange(seq_len)
        per = n_batch // N_CHUNKS
        keys, vals = [], []
        for c in range(N_CHUNKS):
            full = lax.all_gather(normed[c * per:(c + 1) * per], 'model', axis=1, tiled=True)
            flat = full.reshape(per * seq_len, d_model)
            k_c = rotary(dot_f32(flat, wk).reshape(per, seq_len, heads, HEAD_DIM), pos).astype(jnp.bfloat16)
            v_c = dot_f32(flat, wv).astype(jnp.bfloat16).reshape(per, seq_len, heads, HEAD_DIM)
            keys.append(k_c)
            vals.append(v_c)
        key_pre = jnp.concatenate(keys, axis=0)
        val_pre = jnp.concatenate(vals, axis=0)

        rows = jnp.concatenate([new_tok, last_x], axis=0)
        rows_n = rms_norm(rows, norm_attn[0])
        row_pos = jnp.concatenate([lengths, lengths - 1], axis=0)
        q_rows = rotary(dot_f32(rows_n, wq).reshape(2 * n_batch, heads, HEAD_DIM), row_pos).astype(jnp.bfloat16)
        tok_n = rows_n[:n_batch]
        k_new = rotary(dot_f32(tok_n, wk).reshape(n_batch, heads, HEAD_DIM), lengths).astype(jnp.bfloat16)
        v_new = dot_f32(tok_n, wv).astype(jnp.bfloat16).reshape(n_batch, heads, HEAD_DIM)
        key_cache = jnp.concatenate([key_pre, k_new[:, None]], axis=1)
        val_cache = jnp.concatenate([val_pre, v_new[:, None]], axis=1)

        q2 = jnp.stack([q_rows[:n_batch], q_rows[n_batch:]], axis=1)
        scores = jnp.einsum('brhd,bkhd->bhrk', q2, key_cache, preferred_element_type=jnp.float32) * (HEAD_DIM ** -0.5)
        slot = jnp.arange(seq_len + 1)
        prefix = slot[None, :] < lengths[:, None]
        vis = jnp.stack([prefix | (slot[None, :] == seq_len), prefix], axis=1)
        scores = jnp.where(vis[:, None], scores, NEG_BIG)
        prob = jax.nn.softmax(scores, axis=-1)
        att = jnp.einsum('bhrk,bkhd->brhd', prob.astype(jnp.bfloat16), val_cache, preferred_element_type=jnp.float32)
        att = jnp.concatenate([att[:, 0], att[:, 1]], axis=0).reshape(2 * n_batch, heads * HEAD_DIM).astype(jnp.bfloat16)
        rows = (rows.astype(jnp.float32) + lax.psum(dot_f32(att, wo), 'model')).astype(jnp.bfloat16)
        rows_n = rms_norm(rows, norm_mlp[0])
        mid = (jax.nn.silu(dot_f32(rows_n, wg)) * dot_f32(rows_n, wu)).astype(jnp.bfloat16)
        rows = (rows.astype(jnp.float32) + lax.psum(dot_f32(mid, wd), 'model')).astype(jnp.bfloat16)
        return rows[:n_batch], rows[n_batch:], key_cache[None], val_cache[None]

    return jax.shard_map(per_device, mesh=mesh, in_specs=in_specs, out_specs=out_specs, check_vma=False)
```

time: 1420 us -> 460 us (0.32)
  waiting for transfers between devices: 634 us -> 219 us
  matrix products: 341 us -> 78.1 us
  blocking collectives: 148 us -> 28.5 us
  local copies, waits for them, and re-layouts: 169 us -> 77 us
  other arithmetic: 102 us -> 34.6 us
    all_gather x9 -> x4, waiting for transfers between devices: 628 us -> 177 us  [per_device(): lax.all_gather(normed[c * per:(c + 1) * per], 'model', axis=1, tiled=True)]
    dot_general x20 -> x15, matrix products: 341 us -> 73.4 us  [the longest x14 69.9 us: dot_f32(): return jnp.dot(lhs, rhs, preferred_element_type=jnp.float32)]
    psum x1, blocking collectives: 148 us -> 28.5 us  [per_device(): lax.psum(jnp.where(mine[:, None], picked, 0).astype(jnp.float32), 'model')]
    dynamic_slice x3 -> x0, local copies, waits for them, and re-layouts: 53.3 us -> none  [the longest x1 27.7 us: per_device(): lax.dynamic_slice_in_dim(val_blocks, my_idx * kv_loc, kv_loc, axis=3)]
    concatenate x5 -> x2, other arithmetic: 45 us -> 0.17 us  [rotary(): jnp.concatenate([lo_half * cos_tab - hi_half * sin_tab, hi_half * cos_tab...]
    psum x2, waiting for transfers between devices: 0.02 us -> 39.6 us  [the longest x1 38.8 us: per_device(): lax.psum(dot_f32(att, wo), 'model')]
    dot_general x5 -> x2, local copies, waits for them, and re-layouts: 26.9 us -> 2.12 us  [dot_f32(): return jnp.dot(lhs, rhs, preferred_element_type=jnp.float32)]
    reshape x0 -> x8, local copies, waits for them, and re-layouts: none -> 24.1 us  [per_device(): dot_f32(flat, wv).astype(jnp.bfloat16)]
  transfers between devices with their start and end apart: 11 -> 6, of which waited for: 7 -> 6; matrix products, arithmetic and copies ran while one was open for 42% -> 26% of each run, Pallas kernels for 0% -> 0%
where the time goes in v1:
time: 460 us; the launch traced here: 452 us
  waiting for transfers between devices  219 us (48%)
  matrix products  78.1 us (17%)
  local copies, waits for them, and re-layouts  77 us (17%)
  other arithmetic  34.6 us (8%)
  blocking collectives  28.5 us (6%)
  between operations  14.9 us (3%)
    all_gather x4, waiting for transfers between devices, per_device(): lax.all_gather(normed[c * per:(c + 1) * per], 'model', axis=1, tiled=True)  177 us
    dot_general x14, matrix products, dot_f32(): return jnp.dot(lhs, rhs, preferred_element_type=jnp.float32)  69.9 us
    unnamed x43, local copies, waits for them, and re-layouts  43.6 us
    psum x1, waiting for transfers between devices, per_device(): lax.psum(dot_f32(att, wo), 'model')  38.8 us
    psum x1, blocking collectives, per_device(): lax.psum(jnp.where(mine[:, None], picked, 0).astype(jnp.float32), 'model')  28.5 us
    reshape x8, local copies, waits for them, and re-layouts, per_device(): dot_f32(flat, wv).astype(jnp.bfloat16)  24.1 us
    broadcast_in_dim x2, other arithmetic, per_device(): return (rows[:n_batch], rows[n_batch:], key_cache[None], val_cache[None])  17.8 us
  transfers between devices with their start and end apart: 6, of which 6 were waited for; matrix products, arithmetic and copies ran while one was open for 26% of the time, Pallas kernels for 0%

profile of v1, /device:TPU:113, one launch (start us, length us, event | category | flops | bytes accessed | tf_op | source)
XLA Modules:
  0.0 452.5 jit_solution(8415766108746320543)
XLA Ops:
  8.1 4.3 fusion.1
  14.0 2.8 fusion.74
  20.9 28.5 %all-reduce.7 = bf16[16,2048]{1,0:T(8,128)(2,1)S(1)} all-reduce(f32[16,2048]{1,0:T(8,128)S(1)} %select_convert_fusion), channel_id=1, replica_groups=mesh['replica'=2,'model'=8] {'model'}, use_global_device_ids=true, to_apply=%region_0.0 | all-reduce | flops 32768 | bytes 196608 | tf_op jit(solution)/shard_map/psum | solution.py:53
  58.7 26.0 %all-gather.7.cloned.1.call-done = bf16[4,768,2048]{2,1,0:T(8,128)(2,1)} async-done(((bf16[4,96,2048]{2,1,0:T(8,128)(2,1)}), bf16[4,768,2048]{2,1,0:T(8,128)(2,1)}) %all-gather.7.cloned.1.call-update) | async-done | bytes 12582928 | tf_op jit(solution)/shard_map/all_gather | solution.py:59
  84.8 9.2 %convolution_convert_fusion.2 = bf16[3072,256]{1,0:T(8,128)(2,1)} fusion(bf16[3072,2048]{1,0:T(8,128)(2,1)} %bitcast.125, bf16[1,2048,256]{2,1,0:T(8,128)(2,1)S(1)} %copy-done), kind=kOutput, calls=%fused_computation.25 | convolution fusion | flops 3222011904 | bytes 15204352 | tf_op jit(solution)/shard_map/dot_general | solution.py:29
  93.9 3.5 reshape.388
  99.0 50.8 %all-gather.9.cloned.1.call-done = bf16[4,768,2048]{2,1,0:T(8,128)(2,1)} async-done(((bf16[4,96,2048]{2,1,0:T(8,128)(2,1)}), bf16[4,768,2048]{2,1,0:T(8,128)(2,1)}) %all-gather.9.cloned.1.call-update) | async-done | bytes 12582928 | tf_op jit(solution)/shard_map/all_gather | solution.py:59
  149.8 9.2 %convolution_convert_fusion.1 = bf16[3072,256]{1,0:T(8,128)(2,1)} fusion(bf16[3072,2048]{1,0:T(8,128)(2,1)} %bitcast.126, bf16[1,2048,256]{2,1,0:T(8,128)(2,1)S(1)} %copy-done), kind=kOutput, calls=%fused_computation.24 | convolution fusion | flops 3222011904 | bytes 15204352 | tf_op jit(solution)/shard_map/dot_general | solution.py:29
  159.0 3.6 reshape.390
  162.6 2.8 copy.72
  165.4 50.3 %all-gather.11.cloned.1.call-done = bf16[4,768,2048]{2,1,0:T(8,128)(2,1)} async-done(((bf16[4,96,2048]{2,1,0:T(8,128)(2,1)}), bf16[4,768,2048]{2,1,0:T(8,128)(2,1)}) %all-gather.11.cloned.1.call-update) | async-done | bytes 12582928 | tf_op jit(solution)/shard_map/all_gather | solution.py:59
  215.6 9.2 %convolution_convert_fusion = bf16[3072,256]{1,0:T(8,128)(2,1)} fusion(bf16[3072,2048]{1,0:T(8,128)(2,1)} %bitcast.129, bf16[1,2048,256]{2,1,0:T(8,128)(2,1)S(1)} %copy-done), kind=kOutput, calls=%fused_computation.23 | convolution fusion | flops 3222011904 | bytes 15204352 | tf_op jit(solution)/shard_map/dot_general | solution.py:29
  224.8 3.5 reshape.392
  228.3 2.8 copy.73
  231.0 50.3 %all-gather.5.cloned.1.call-done = bf16[4,768,2048]{2,1,0:T(8,128)(2,1)} async-done(((bf16[4,96,2048]{2,1,0:T(8,128)(2,1)}), bf16[4,768,2048]{2,1,0:T(8,128)(2,1)}) %all-gather.5.cloned.1.call-update) | async-done | bytes 12582928 | tf_op jit(solution)/shard_map/all_gather | solution.py:59
  281.3 9.2 %convolution_convert_fusion.3 = bf16[3072,256]{1,0:T(8,128)(2,1)} fusion(bf16[3072,2048]{1,0:T(8,128)(2,1)} %bitcast.132, bf16[1,2048,256]{2,1,0:T(8,128)(2,1)S(1)} %copy-done), kind=kOutput, calls=%fused_computation.26 | convolution fusion | flops 3222011904 | bytes 15204352 | tf_op jit(solution)/shard_map/dot_general | solution.py:29
  290.5 3.5 reshape.386
  294.0 2.9 copy.70
  296.9 8.7 %fusion.8 = f32[4,768,2,128]{1,3,2,0:T(8,128)S(1)} fusion(bf16[2,128,2048,1]{2,1,0,3:T(8,128)(2,1)} %bitcast.111, bf16[4,768,2048]{2,1,0:T(8,128)(2,1)} %all-gather.7.cloned.1.call-done), kind=kOutput, calls=%fused_computation.11 | convolution fusion | flops 3221225472 | bytes 16777216 | tf_op jit(solution)/shard_map/dot_general | solution.py:29
  305.7 3.6 fusion.6
  309.3 3.6 fusion.4
  312.9 6.5 %fusion.10 = f32[4,768,2,128]{1,3,2,0:T(8,128)S(1)} fusion(bf16[2,128,2048,1]{2,1,0,3:T(8,128)(2,1)S(1)} %bitcast.114, bf16[4,768,2048]{2,1,0:T(8,128)(2,1)} %all-gather.5.cloned.1.call-done), kind=kOutput, calls=%fused_computation.13 | convolution fusion | flops 3221225472 | bytes 16777216 | tf_op jit(solution)/shard_map/dot_general | solution.py:29
  319.4 3.9 subtract_convert_fusion.3
  323.3 4.7 %fusion.76 = (f32[16,2,2]{2,1,0:T(2,128)}, f32[16,2,2,769]{3,2,1,0:T(2,128)}) fusion(pred[16,2,769]{2,1,0:T(4,128)(4,1)} %pad_add_fusion, bf16[16,2,2,128]{3,0,2,1:T(8,128)(2,1)} %pad_maximum_fusion.3, bf16[16,1,2,128]{1,3,2,0:T(8,128)(2,1)S(1)} %copy-done.3, bf16[4,768,2,64]{1,3,2,0:T(8,128)(2,1)} %get-tuple-element.42, ...), kind=kOutput, calls=%fused_computation.130 | convolution fusion | flops 69493760 | bytes 6537760 | tf_op jit(solution)/shard_map/sub | solution.py:84
  328.0 3.5 fusion.27
  332.8 11.0 %fusion.90 = bf16[1,16,769,2,128]{2,4,3,1,0:T(8,128)(2,1)} fusion(bf16[16,1,2,128]{1,3,2,0:T(8,128)(2,1)S(1)} %copy-done.3, bf16[4,768,2,64]{1,3,2,0:T(8,128)(2,1)} %get-tuple-element.42, bf16[4,768,2,64]{1,3,2,0:T(8,128)(2,1)} %get-tuple-element.43, bf16[4,768,2,64]{1,3,2,0:T(8,128)(2,1)} %get-tuple-element.40, ...), kind=kLoop, calls=%fused_computation.131 | loop fusion | flops 56696832 | bytes 12599296 | tf_op jit(solution)/shard_map/broadcast_in_dim | solution.py:91
  343.8 38.8 %all-reduce.4.cloned.1.call-done = f32[32,2048]{1,0:T(8,128)} async-done(((f32[32,2048]{1,0:T(8,128)}), f32[32,2048]{1,0:T(8,128)}) %all-reduce.4.cloned.1.call-update) | async-done | bytes 262160 | tf_op jit(solution)/shard_map/psum | solution.py:87
  383.7 3.1 fusion.16
  386.8 5.8 %fusion.12 = f32[32,2048]{1,0:T(8,128)} fusion(bf16[1,1024,2048]{2,1,0:T(8,128)(2,1)} %param.23, bf16[1,2048,1024]{2,1,0:T(8,128)(2,1)} %param.22, f32[32,1024]{1,0:T(8,128)S(1)} %fusion.16, bf16[32,2048]{1,0:T(8,128)(2,1)S(1)} %get-tuple-element.23, f32[2048]{0:T(1024)S(1)} %bitcast.121, f32[32]{0:T(128)S(1)} %add_rsqrt_fusion.1), kind=kOutput, calls=%fused_computation.17 | convolution fusion | flops 268894208 | bytes 8921216 | tf_op jit(solution)/shard_map/dot_general | solution.py:29
  392.6 6.8 %fusion.72 = bf16[1,16,769,2,128]{4,2,3,1,0:T(8,128)(2,1)} fusion(bf16[16,1,2,128]{3,1,2,0:T(2,128)(2,1)S(1)} %copy-done.11, bf16[4,768,2,128]{3,1,2,0:T(8,128)(2,1)} %copy.73, bf16[4,768,2,128]{3,1,2,0:T(8,128)(2,1)} %copy.72, bf16[4,768,2,128]{3,1,2,0:T(8,128)(2,1)S(1)} %copy.71, bf16[4,768,2,128]{3,1,2,0:T(8,128)(2,1)} %copy.70), kind=kLoop, calls=%fused_computation.127 | loop fusion | flops 31498240 | bytes 12599296 | tf_op jit(solution)/shard_map/broadcast_in_dim | solution.py:91
  399.4 18.5 %copy.84 = bf16[1,16,769,2,128]{4,3,2,1,0:T(2,128)(2,1)} copy(bf16[1,16,769,2,128]{2,4,3,1,0:T(8,128)(2,1)} %fusion.90) | data formatting | bytes 12599296
  417.9 25.0 %copy.85 = bf16[1,16,769,2,128]{4,3,2,1,0:T(2,128)(2,1)} copy(bf16[1,16,769,2,128]{4,2,3,1,0:T(8,128)(2,1)} %fusion.72) | data formatting | bytes 12599296
  (98 shorter events, 22.2 us)
Async XLA Ops:
  7.2 42.5 %copy-start = (bf16[1,2048,256]{2,1,0:T(8,128)(2,1)S(1)}, bf16[1,2048,256]{2,1,0:T(8,128)(2,1)}, u32[]{:S(2)}) copy-start(bf16[1,2048,256]{2,1,0:T(8,128)(2,1)} %param.18) | copy-start | bytes 3145732
  7.2 77.6 %all-gather.7.cloned.1.call-start = ((), (), s32[]{:S(2)}) async-start(), calls=%async_computation.1 | async-start | bytes 14155776 | tf_op jit(solution)/shard_map/all_gather | solution.py:59
  7.3 5.2 %copy-start.2 = (bf16[16,96,2048]{2,1,0:T(8,128)(2,1)S(1)}, bf16[16,96,2048]{2,1,0:T(8,128)(2,1)}, u32[]{:S(2)}) copy-start(bf16[16,96,2048]{2,1,0:T(8,128)(2,1)} %param.12) | copy-start | bytes 18874372
  14.0 5.2 %copy-start.12 = (bf16[1,2048]{1,0:T(2,128)(2,1)S(1)}, bf16[1,2048]{1,0:T(2,128)(2,1)}, u32[]{:S(2)}) copy-start(bf16[1,2048]{1,0:T(2,128)(2,1)} %param.20) | copy-start | bytes 12292
  14.0 5.2 %copy-start.13 = (s32[16]{0:T(128)S(1)}, s32[16]{0:T(128)}, u32[]{:S(2)}) copy-start(s32[16]{0:T(128)} %param.13) | copy-start | bytes 196
  16.8 32.6 %copy-start.10 = (bf16[16,2048]{1,0:T(8,128)(2,1)S(1)}, bf16[16,2048]{1,0:T(8,128)(2,1)}, u32[]{:S(2)}) copy-start(bf16[16,2048]{1,0:T(8,128)(2,1)} %param.14) | copy-start | bytes 196612
  16.8 33.8 %copy-start.6 = (bf16[1,2048,256]{2,1,0:T(8,128)(2,1)S(1)}, bf16[1,2048,256]{2,1,0:T(8,128)(2,1)}, u32[]{:S(2)}) copy-start(bf16[1,2048,256]{2,1,0:T(8,128)(2,1)} %param.17) | copy-start | bytes 3145732
  16.9 132.9 %all-gather.9.cloned.1.call-start = ((), (), s32[]{:S(2)}) async-start(), calls=%async_computation.2 | async-start | bytes 14155776 | tf_op jit(solution)/shard_map/all_gather | solution.py:59
  17.7 197.9 %all-gather.11.cloned.1.call-start = ((), (), s32[]{:S(2)}) async-start(), calls=%async_computation.3 | async-start | bytes 14155776 | tf_op jit(solution)/shard_map/all_gather | solution.py:59
  18.5 262.8 %all-gather.5.cloned.1.call-start = ((), (), s32[]{:S(2)}) async-start(), calls=%async_computation | async-start | bytes 14155776 | tf_op jit(solution)/shard_map/all_gather | solution.py:59
  19.1 363.4 %all-reduce.4.cloned.1.call-start = ((), (), s32[]{:S(2)}) async-start(), calls=%async_computation.4 | async-start | bytes 524288 | tf_op jit(solution)/shard_map/psum | solution.py:87
  51.2 42.7 %copy-start.4 = (bf16[256,2048]{1,0:T(8,128)(2,1)}, bf16[256,2048]{1,0:T(8,128)(2,1)S(1)}, u32[]{:S(2)}) copy-start(bf16[256,2048]{1,0:T(8,128)(2,1)S(1)} %copy.92) | copy-start | bytes 3145732
  294.0 11.6 %slice-start = ((s8[12582912]{0:T(1024)(128)(4,1)}), s8[4194304]{0:T(1024)(128)(4,1)S(1)}, s32[]{:S(2)}) async-start(s8[12582912]{0:T(1024)(128)(4,1)} %bitcast.127), calls=%async_computation.6 | async-start | bytes 8388608
  296.9 8.7 %copy-start.5 = (bf16[256,2048]{1,0:T(8,128)(2,1)S(1)}, bf16[256,2048]{1,0:T(8,128)(2,1)}, u32[]{:S(2)}) copy-start(bf16[256,2048]{1,0:T(8,128)(2,1)} %copy-done.4) | copy-start | bytes 3145732
  296.9 8.8 %slice-start.1 = ((s8[12582912]{0:T(1024)(128)(4,1)}), s8[4194304]{0:T(1024)(128)(4,1)S(1)}, s32[]{:S(2)}) async-start(s8[12582912]{0:T(1024)(128)(4,1)} %bitcast.127), calls=%async_computation.7 | async-start | bytes 8388608
  296.9 8.8 %slice-start.2 = ((s8[12582912]{0:T(1024)(128)(4,1)}), s8[4194304]{0:T(1024)(128)(4,1)S(1)}, s32[]{:S(2)}) async-start(s8[12582912]{0:T(1024)(128)(4,1)} %bitcast.127), calls=%async_computation.8 | async-start | bytes 8388608
  296.9 12.4 %slice-start.3 = ((s8[12582912]{0:T(1024)(128)(4,1)}), s8[4194304]{0:T(1024)(128)(4,1)S(1)}, s32[]{:S(2)}) async-start(s8[12582912]{0:T(1024)(128)(4,1)} %bitcast.130), calls=%async_computation.9 | async-start | bytes 8388608
  296.9 12.4 %slice-start.4 = ((s8[12582912]{0:T(1024)(128)(4,1)}), s8[4194304]{0:T(1024)(128)(4,1)S(1)}, s32[]{:S(2)}) async-start(s8[12582912]{0:T(1024)(128)(4,1)} %bitcast.130), calls=%async_computation.10 | async-start | bytes 8388608
  305.6 3.6 slice-start.5
  312.9 6.5 %copy-start.8 = (f32[768,64]{0,1:T(8,128)S(1)}, f32[768,64]{0,1:T(8,128)}, u32[]{:S(2)}) copy-start(f32[768,64]{0,1:T(8,128)} %get-tuple-element.52) | copy-start | bytes 589828
  312.9 6.5 %copy-start.9 = (f32[768,64]{0,1:T(8,128)S(1)}, f32[768,64]{0,1:T(8,128)}, u32[]{:S(2)}) copy-start(f32[768,64]{0,1:T(8,128)} %get-tuple-element.53) | copy-start | bytes 589828
  319.4 3.9 copy-start.3
  328.0 3.6 copy-start.7
  332.7 111.0 %all-reduce.6.cloned.1.call-start = ((), (), s32[]{:S(2)}) async-start(), calls=%async_computation.5 | async-start | bytes 524288 | tf_op jit(solution)/shard_map/psum | solution.py:90
  383.7 8.9 %copy-start.11 = (bf16[16,1,2,128]{3,1,2,0:T(2,128)(2,1)S(1)}, bf16[16,1,2,128]{3,1,2,0:T(2,128)(2,1)}, u32[]{:S(2)}) copy-start(bf16[16,1,2,128]{3,1,2,0:T(2,128)(2,1)} %broadcast_in_dim_reshape.4) | copy-start | bytes 24580
  399.4 46.0 %copy-start.1 = (bf16[1,2048,256]{2,1,0:T(8,128)(2,1)S(1)}, bf16[1,2048,256]{2,1,0:T(8,128)(2,1)}, u32[]{:S(2)}) copy-start(bf16[1,2048,256]{2,1,0:T(8,128)(2,1)} %param.18) | copy-start | bytes 3145732
Sparse Core Ops, SparseCore 0:
  17.0 67.7 all-gather.6
  86.3 63.4 all-gather.8
  152.0 63.6 all-gather.10
  217.7 63.6 all-gather.4
  332.8 49.7 all-reduce.3
  392.7 50.9 all-reduce.5

commit v2 on v1

v2 whole, which is shorter than its diff:
```python
import functools

import numpy as np

import jax
import jax.numpy as jnp
from jax import lax
from jax.experimental import pallas as pl
from jax.experimental.pallas import tpu as pltpu
from jax.sharding import PartitionSpec as P

HEAD_DIM = 128
NEG_BIG = -1e30
MESH = pl.DeviceIdType.MESH
GROUP = 2
F32 = jnp.float32
BF16 = jnp.bfloat16


def dot_f32(lhs, rhs):
    return jnp.dot(lhs, rhs, preferred_element_type=F32)


def rms_rows(rows_f32, gain_f32):
    inv_rms = lax.rsqrt(jnp.mean(rows_f32 * rows_f32, axis=-1, keepdims=True) + 1e-5)
    return (rows_f32 * inv_rms * gain_f32).astype(BF16)


def rope_half(head_f32, cos_t, sin_t):
    return head_f32 * cos_t + pltpu.roll(head_f32, HEAD_DIM // 2, 1) * sin_t


def remote(src, dst, send_sem, recv_sem, dev):
    return pltpu.make_async_remote_copy(src_ref=src, dst_ref=dst, send_sem=send_sem, recv_sem=recv_sem,
                                        device_id={'model': dev}, device_id_type=MESH)


def wait_bytes(ref, sem):
    pltpu.make_async_copy(ref, ref, sem).wait()


def greet(me, n_dev):
    barrier = pltpu.get_barrier_semaphore()
    for off in range(1, n_dev):
        pl.semaphore_signal(barrier, inc=1, device_id={'model': lax.rem(me + off, n_dev)}, device_id_type=MESH)
    pl.semaphore_wait(barrier, n_dev - 1)


def exchange_kernel(n_dev, len_ref, x_hbm, wk_hbm, wv_hbm, wq_hbm, tok_ref, gain_ref, cos_ref, sin_ref,
                    kout, vout, q_out, rows_out, kn_out, vn_out,
                    wbuf, wq_buf, xown, xrecv, stage, ktmp, lfull, lrecv, lcols, crow, srow,
                    xcopy_sem, wcopy_sem, wrecv_sem, wsend_sem, xrecv_sem, xsend_sem,
                    kv_recv_sem, kv_send_sem, kv_local_sem, l_send_sem, l_recv_sem):
    n_batch, seq_loc, d_model = xown.shape
    n_chip = n_dev // 2
    half = n_batch // 2
    n_chunk = half // GROUP
    m_rows = GROUP * seq_loc
    me = lax.axis_index('model')
    chip, core = me // 2, lax.rem(me, 2)
    left, right = lax.rem(chip + n_chip - 1, n_chip), lax.rem(chip + 1, n_chip)
    partner = chip * 2 + 1 - core
    w_hbm = (wk_hbm, wv_hbm)
    outs = (kout, vout)

    wlocal = [pltpu.make_async_copy(w_hbm[kv], wbuf.at[0, core, kv], wcopy_sem.at[kv]) for kv in range(2)]
    for cp in wlocal:
        cp.start()

    def xcopy(ch):
        return pltpu.make_async_copy(x_hbm.at[pl.ds(ch * GROUP, GROUP)], xown.at[pl.ds(ch * GROUP, GROUP)], xcopy_sem.at[ch])

    for ch in range(2 * n_chunk):
        xcopy(ch).start()
    wq_copy = pltpu.make_async_copy(wq_hbm, wq_buf, wcopy_sem.at[2])
    wq_copy.start()

    greet(me, n_dev)

    wsends = []
    for kv in range(2):
        wsends.append(remote(w_hbm[kv], wbuf.at[1, core, kv], wsend_sem.at[0, kv], wrecv_sem.at[1, core, kv], right * 2 + core))
        wsends.append(remote(w_hbm[kv], wbuf.at[2, core, kv], wsend_sem.at[1, kv], wrecv_sem.at[2, core, kv], left * 2 + core))
        wsends.append(remote(w_hbm[kv], wbuf.at[0, core, kv], wsend_sem.at[2, kv], wrecv_sem.at[0, core, kv], partner))
    for cp in wsends:
        cp.start()
    xsends = []
    for ci in range(n_chunk):
        xsends.append(remote(x_hbm.at[pl.ds(ci * GROUP, GROUP)], xrecv.at[0, pl.ds(ci * GROUP, GROUP)],
                             xsend_sem.at[0, ci], xrecv_sem.at[0, ci], right * 2 + core))
        xsends.append(remote(x_hbm.at[pl.ds(half + ci * GROUP, GROUP)], xrecv.at[1, pl.ds(ci * GROUP, GROUP)],
                             xsend_sem.at[1, ci], xrecv_sem.at[1, ci], left * 2 + core))
    for cp in xsends:
        cp.start()

    gain = gain_ref[...].astype(F32)

    def normalize(ref):
        for g in range(GROUP):
            ref[g] = rms_rows(ref[g].astype(F32), gain)

    def make_kv(rows_ref, unit, ci, slot, kcore, owner, b0, dst, target):
        rows = rows_ref[...].reshape(m_rows, d_model)
        start = pl.multiple_of(owner * seq_loc, seq_loc)
        cos_t = jnp.concatenate([cos_ref[pl.ds(start, seq_loc), :]] * GROUP, axis=0)
        sin_t = jnp.concatenate([sin_ref[pl.ds(start, seq_loc), :]] * GROUP, axis=0)
        for kv in range(2):
            acc = dot_f32(rows, wbuf[slot, kcore, kv])
            for h in range(2):
                head = acc[:, h * HEAD_DIM:(h + 1) * HEAD_DIM]
                if kv == 0:
                    head = rope_half(head, cos_t, sin_t)
                ktmp[pl.ds(h, m_rows, stride=2), :] = head
            piece = stage.at[unit, dst, kv, pl.ds(ci * GROUP, GROUP)]
            piece.reshape(2 * m_rows, HEAD_DIM)[...] = ktmp[...].astype(BF16)
            place = outs[kv].at[pl.ds(b0, GROUP), pl.ds(start, seq_loc)]
            if target is None:
                pltpu.make_async_copy(piece, place, kv_local_sem.at[kv]).start()
            else:
                remote(piece, place, kv_send_sem, kv_recv_sem.at[kv], target).start()

    for cp in wlocal:
        cp.wait()
    base = me * seq_loc

    @pl.loop(0, 2 * n_chunk)
    def _(ch):
        xcopy(ch).wait()
        rows_ref = xown.at[pl.ds(ch * GROUP, GROUP)]
        for g in range(GROUP):
            b = ch * GROUP + g
            hit = lax.broadcasted_iota(jnp.int32, (16, seq_loc), 1) == len_ref[b] - 1 - base
            row = dot_f32(jnp.where(hit, 1.0, 0.0).astype(BF16), xown[b])
            lfull[pl.ds(b, 1), :] = row[0:1]
        normalize(rows_ref)
        make_kv(rows_ref, ch // n_chunk, lax.rem(ch, n_chunk), 0, core, me, ch * GROUP, 3, None)

    width = d_model // n_dev

    def col(j):
        return pl.ds(pl.multiple_of(j * width, width), width)

    for off in range(1, n_dev):
        peer = lax.rem(me + off, n_dev)
        remote(lfull.at[:, col(peer)], lrecv.at[me], l_send_sem.at[0], l_recv_sem.at[0], peer).start()
    lrecv[me] = lfull[:, col(me)]

    for kv in range(2):
        wait_bytes(wbuf.at[0, 1 - core, kv], wrecv_sem.at[0, 1 - core, kv])

    @pl.loop(0, 2 * n_chunk)
    def _(ch):
        make_kv(xown.at[pl.ds(ch * GROUP, GROUP)], ch // n_chunk, lax.rem(ch, n_chunk), 0, 1 - core, me, ch * GROUP, 2, partner)

    fwds = []
    for slot in (1, 2):
        for kv in range(2):
            wait_bytes(wbuf.at[slot, core, kv], wrecv_sem.at[slot, core, kv])
            fwds.append(remote(wbuf.at[slot, core, kv], wbuf.at[slot, core, kv], wsend_sem.at[2 + slot, kv],
                               wrecv_sem.at[slot, core, kv], partner))
            fwds[-1].start()
    for slot in (1, 2):
        for kv in range(2):
            wait_bytes(wbuf.at[slot, 1 - core, kv], wrecv_sem.at[slot, 1 - core, kv])

    @pl.loop(0, n_chunk)
    def _(ci):
        for kcore in range(2):
            make_kv(xown.at[pl.ds(ci * GROUP, GROUP)], 0, ci, 1, kcore, me, ci * GROUP, kcore, left * 2 + kcore)
            make_kv(xown.at[pl.ds(half + ci * GROUP, GROUP)], 1, ci, 2, kcore, me, half + ci * GROUP, kcore, right * 2 + kcore)

    wait_bytes(lrecv.at[pl.ds(0, n_dev - 1)], l_recv_sem.at[0])
    lcols[me] = jnp.sum(lrecv[...], axis=0).astype(BF16)
    for off in range(1, n_dev):
        peer = lax.rem(me + off, n_dev)
        remote(lcols.at[me], lcols.at[me], l_send_sem.at[1], l_recv_sem.at[1], peer).start()

    @pl.loop(0, n_chunk)
    def _(ci):
        for side in range(2):
            rows_ref = xrecv.at[side, pl.ds(ci * GROUP, GROUP)]
            wait_bytes(rows_ref, xrecv_sem.at[side, ci])
            normalize(rows_ref)
            owner = (left if side == 0 else right) * 2 + core
            beyond = right if side == 0 else left
            b0 = side * half + ci * GROUP
            for kcore in range(2):
                make_kv(rows_ref, 2 + side, ci, 2 - side, kcore, owner, b0, kcore, beyond * 2 + kcore)
            make_kv(rows_ref, 2 + side, ci, 0, 1 - core, owner, b0, 2, partner)
            make_kv(rows_ref, 2 + side, ci, 0, core, owner, b0, 3, None)

    wait_bytes(lcols.at[pl.ds(0, n_dev - 1)], l_recv_sem.at[1])
    wq_copy.wait()
    rows_out[0:n_batch, :] = tok_ref[...]
    for j in range(n_dev):
        rows_out[n_batch:2 * n_batch, j * width:(j + 1) * width] = lcols[j]
    for b in range(n_batch):
        for r in range(2):
            at = jnp.maximum(len_ref[b] - r, 0)
            crow[pl.ds(r * n_batch + b, 1), :] = cos_ref[pl.ds(at, 1), :]
            srow[pl.ds(r * n_batch + b, 1), :] = sin_ref[pl.ds(at, 1), :]
    rows_n = rms_rows(rows_out[...].astype(F32), gain)
    q_acc = dot_f32(rows_n, wq_buf[...])
    for h in range(2):
        q_out[:, h * HEAD_DIM:(h + 1) * HEAD_DIM] = rope_half(q_acc[:, h * HEAD_DIM:(h + 1) * HEAD_DIM], crow[...], srow[...]).astype(BF16)
    for kv, new_out in enumerate((kn_out, vn_out)):
        acc = dot_f32(rows_n[0:n_batch], wbuf[0, core, kv])
        for h in range(2):
            head = acc[:, h * HEAD_DIM:(h + 1) * HEAD_DIM]
            if kv == 0:
                head = rope_half(head, crow[0:n_batch, :], srow[0:n_batch, :])
            ktmp[pl.ds(h, n_batch, stride=2), :] = head
        new_out.reshape(2 * n_batch, HEAD_DIM)[...] = ktmp[0:2 * n_batch, :].astype(BF16)

    quarter = n_batch // 4
    seq_len = seq_loc * n_dev
    for kv in range(2):
        wait_bytes(outs[kv].at[pl.ds(0, quarter), pl.ds(0, seq_len)], kv_local_sem.at[kv])
        wait_bytes(outs[kv].at[pl.ds(0, 3 * quarter), pl.ds(0, seq_len)], kv_recv_sem.at[kv])
    for cp in wsends + fwds + xsends:
        cp.wait_send()
    wait_bytes(lrecv.at[pl.ds(0, n_dev - 1)], l_send_sem.at[0])
    wait_bytes(lcols.at[pl.ds(0, n_dev - 1)], l_send_sem.at[1])
    wait_bytes(stage.at[:, pl.ds(0, 3)], kv_send_sem)


def attention_kernel(len_ref, q_ref, kn_ref, vn_ref, k_in, v_in, k_out, v_out, att_ref):
    b = pl.program_id(0)
    n_slot = k_out.shape[1]
    k_out[0, 0:n_slot - 1] = k_in[0, 0:n_slot - 1]
    v_out[0, 0:n_slot - 1] = v_in[0, 0:n_slot - 1]
    k_out[0, n_slot - 1:n_slot] = kn_ref[...]
    v_out[0, n_slot - 1:n_slot] = vn_ref[...]
    keys = k_out.at[0].reshape(2 * n_slot, HEAD_DIM)[...]
    vals = v_out.at[0].reshape(2 * n_slot, HEAD_DIM)[...]
    scores = lax.dot_general(q_ref[0], keys, (((1,), (1,)), ((), ())), preferred_element_type=F32) * (HEAD_DIM ** -0.5)
    row = lax.broadcasted_iota(jnp.int32, scores.shape, 0)
    colm = lax.broadcasted_iota(jnp.int32, scores.shape, 1)
    slot = colm // 2
    see = (slot < len_ref[b]) | ((slot == n_slot - 1) & (row < 2))
    see = see & (lax.rem(row, 2) == lax.rem(colm, 2))
    scores = jnp.where(see, scores, NEG_BIG)
    prob = jnp.exp(scores - jnp.max(scores, axis=1, keepdims=True))
    total = jnp.sum(prob, axis=1, keepdims=True)
    att_ref[0] = dot_f32(prob.astype(BF16), vals) / total


def tail_kernel(n_dev, att_ref, rows_ref, wo_ref, gain_ref, wg_hbm, wu_hbm, wd_hbm, out_ref,
                wg, wu, wd, part, recv, hid, rows, w_sem, send_sem, recv_sem, g_send_sem, g_recv_sem):
    me = lax.axis_index('model')
    n_row, d_model = rows.shape
    width = d_model // n_dev
    copies = [pltpu.make_async_copy(src, dst, w_sem.at[i]) for i, (src, dst) in enumerate(((wg_hbm, wg), (wu_hbm, wu), (wd_hbm, wd)))]
    for cp in copies:
        cp.start()

    def col(j):
        return pl.ds(pl.multiple_of(j * width, width), width)

    def add_partials(step, residual):
        for off in range(1, n_dev):
            peer = lax.rem(me + off, n_dev)
            remote(part.at[step, :, col(peer)], recv.at[step, me], send_sem.at[step], recv_sem.at[step], peer).start()
        recv[step, me] = part[step, :, col(me)]
        wait_bytes(recv.at[step, pl.ds(0, n_dev - 1)], recv_sem.at[step])
        hid[step, me] = (residual[:, col(me)].astype(F32) + jnp.sum(recv[step], axis=0)).astype(BF16)
        for off in range(1, n_dev):
            peer = lax.rem(me + off, n_dev)
            remote(hid.at[step, me], hid.at[step, me], g_send_sem.at[step], g_recv_sem.at[step], peer).start()
        wait_bytes(hid.at[step, pl.ds(0, n_dev - 1)], g_recv_sem.at[step])

    part[0] = dot_f32(att_ref[...], wo_ref[...])
    greet(me, n_dev)
    add_partials(0, rows_ref)
    for j in range(n_dev):
        rows[:, j * width:(j + 1) * width] = hid[0, j]
    rows_n = rms_rows(rows[...].astype(F32), gain_ref[...].astype(F32))
    copies[0].wait()
    gate = dot_f32(rows_n, wg[...])
    copies[1].wait()
    up = dot_f32(rows_n, wu[...])
    mid = (gate * (1.0 / (1.0 + jnp.exp(-gate))) * up).astype(BF16)
    copies[2].wait()
    part[1] = dot_f32(mid, wd[...])
    add_partials(1, rows)
    for j in range(n_dev):
        out_ref[:, j * width:(j + 1) * width] = hid[1, j]
    for step in range(2):
        wait_bytes(recv.at[step, pl.ds(0, n_dev - 1)], send_sem.at[step])
        wait_bytes(hid.at[step, pl.ds(0, n_dev - 1)], g_send_sem.at[step])


def rotary_tables(n_pos):
    inv_freq = np.float32(10000.0) ** (-2.0 * np.arange(HEAD_DIM // 2, dtype=np.float32) / HEAD_DIM).astype(np.float32)
    angles = np.arange(n_pos, dtype=np.float32)[:, None] * inv_freq.astype(np.float32)
    cos, sin = np.cos(angles), np.sin(angles)
    return (np.concatenate([cos, cos], axis=1).astype(np.float32), np.concatenate([-sin, sin], axis=1).astype(np.float32))


def solution(mesh):
    n_dev = mesh.shape['model']
    seq_spec = P('replica', 'model', None)
    col_spec = P(None, None, 'model')
    row_spec = P(None, 'model', None)
    gain_spec = P(None, None)
    tok_spec = P('replica', None)
    cache_spec = P(None, 'replica', None, 'model', None)
    in_specs = (seq_spec, P('replica'), tok_spec, gain_spec, col_spec, col_spec, col_spec, row_spec, gain_spec, col_spec, col_spec, row_spec)
    out_specs = (tok_spec, tok_spec, cache_spec, cache_spec)
    hbm = pl.BlockSpec(memory_space=pl.ANY)
    vmem = pl.BlockSpec(memory_space=pltpu.VMEM)
    smem = pl.BlockSpec(memory_space=pltpu.SMEM)
    dma = pltpu.SemaphoreType.DMA

    def per_device(prompt, lengths, new_tok, norm_attn, w_q, w_k, w_v, w_o, norm_mlp, w_gate, w_up, w_down):
        n_batch, seq_loc, d_model = prompt.shape
        kv_width = w_k.shape[2]
        heads = kv_width // HEAD_DIM
        seq_len = seq_loc * n_dev
        half = n_batch // 2
        n_chunk = half // GROUP
        width = d_model // n_dev
        wq, wk, wv, wo, wg, wu, wd = w_q[0], w_k[0], w_v[0], w_o[0], w_gate[0], w_up[0], w_down[0]
        cos_tab, sin_tab = (jnp.asarray(t) for t in rotary_tables(seq_len + 8))

        cache = jax.ShapeDtypeStruct((n_batch, seq_len + 1, heads, HEAD_DIM), BF16)
        new_kv = jax.ShapeDtypeStruct((n_batch, heads, HEAD_DIM), BF16)
        key_buf, val_buf, q_rows, rows, k_new, v_new = pl.pallas_call(
            functools.partial(exchange_kernel, n_dev),
            out_shape=(cache, cache, jax.ShapeDtypeStruct((2 * n_batch, kv_width), BF16),
                       jax.ShapeDtypeStruct((2 * n_batch, d_model), BF16), new_kv, new_kv),
            in_specs=[smem, hbm, hbm, hbm, hbm, vmem, vmem, vmem, vmem],
            out_specs=(hbm, hbm, vmem, vmem, vmem, vmem),
            scratch_shapes=[
                pltpu.VMEM((3, 2, 2, d_model, kv_width), BF16),
                pltpu.VMEM((d_model, kv_width), BF16),
                pltpu.VMEM((n_batch, seq_loc, d_model), BF16),
                pltpu.VMEM((2, half, seq_loc, d_model), BF16),
                pltpu.VMEM((4, 4, 2, half, seq_loc, heads, HEAD_DIM), BF16),
                pltpu.VMEM((2 * GROUP * seq_loc, HEAD_DIM), F32),
                pltpu.VMEM((n_batch, d_model), F32),
                pltpu.VMEM((n_dev, n_batch, width), F32),
                pltpu.VMEM((n_dev, n_batch, width), BF16),
                pltpu.VMEM((2 * n_batch, HEAD_DIM), F32),
                pltpu.VMEM((2 * n_batch, HEAD_DIM), F32),
                dma((2 * n_chunk,)), dma((3,)), dma((3, 2, 2)), dma((5, 2)), dma((2, n_chunk)), dma((2, n_chunk)),
                dma((2,)), dma(()), dma((2,)), dma((2,)), dma((2,)),
            ],
            compiler_params=pltpu.CompilerParams(collective_id=0, has_side_effects=True, vmem_limit_bytes=60 * 2 ** 20),
            name='exchange',
        )(lengths, prompt, wk, wv, wq, new_tok, norm_attn, cos_tab, sin_tab)

        q_pairs = q_rows.reshape(2, n_batch, heads, HEAD_DIM).transpose(1, 0, 2, 3).reshape(n_batch, 2 * heads, HEAD_DIM)
        q_pairs = jnp.concatenate([q_pairs, q_pairs], axis=1)
        cache_block = pl.BlockSpec((1, seq_len + 1, heads, HEAD_DIM), lambda b, lens: (b, 0, 0, 0))
        new_block = pl.BlockSpec((1, heads, HEAD_DIM), lambda b, lens: (b, 0, 0))
        pair_block = pl.BlockSpec((1, 4 * heads, HEAD_DIM), lambda b, lens: (b, 0, 0))
        key_cache, val_cache, att = pl.pallas_call(
            attention_kernel,
            grid_spec=pltpu.PrefetchScalarGridSpec(
                num_scalar_prefetch=1, grid=(n_batch,),
                in_specs=[pair_block, new_block, new_block, cache_block, cache_block],
                out_specs=(cache_block, cache_block, pair_block)),
            out_shape=(cache, cache, jax.ShapeDtypeStruct((n_batch, 4 * heads, HEAD_DIM), F32)),
            name='attend',
        )(lengths, q_pairs, k_new, v_new, key_buf, val_buf)
        att = att[:, :2 * heads].reshape(n_batch, 2, kv_width).transpose(1, 0, 2).reshape(2 * n_batch, kv_width).astype(BF16)

        ff = wg.shape[1]
        out = pl.pallas_call(
            functools.partial(tail_kernel, n_dev),
            out_shape=jax.ShapeDtypeStruct((2 * n_batch, d_model), BF16),
            in_specs=[vmem, vmem, vmem, vmem, hbm, hbm, hbm],
            out_specs=vmem,
            scratch_shapes=[
                pltpu.VMEM((d_model, ff), BF16), pltpu.VMEM((d_model, ff), BF16), pltpu.VMEM((ff, d_model), BF16),
                pltpu.VMEM((2, 2 * n_batch, d_model), F32),
                pltpu.VMEM((2, n_dev, 2 * n_batch, width), F32),
                pltpu.VMEM((2, n_dev, 2 * n_batch, width), BF16),
                pltpu.VMEM((2 * n_batch, d_model), BF16),
                dma((3,)), dma((2,)), dma((2,)), dma((2,)), dma((2,)),
            ],
            compiler_params=pltpu.CompilerParams(collective_id=1, has_side_effects=True, vmem_limit_bytes=40 * 2 ** 20),
            name='tail',
        )(att, rows, wo, norm_mlp, wg, wu, wd)
        return out[:n_batch], out[n_batch:], key_cache[None], val_cache[None]

    return jax.shard_map(per_device, mesh=mesh, in_specs=in_specs, out_specs=out_specs, check_vma=False)
```

time: 460 us -> 243 us (0.53); the launches traced: 452 us -> 242 us
  Pallas kernels: 0 us -> 232 us
  waiting for transfers between devices: 219 us -> 0 us
  matrix products: 78.1 us -> 0 us
  local copies, waits for them, and re-layouts: 77 us -> 8.85 us
  other arithmetic: 34.6 us -> 0.63 us
  blocking collectives: 28.5 us -> 0 us
  between operations: 14.9 us -> 0.7 us
    pallas_call x0 -> x3, Pallas kernels: none -> 232 us  [the longest x1 190 us: per_device(): pl.pallas_call(functools.partial(exchange_kernel, n_dev), out_shape=(cach...]
    all_gather x4 -> x0, waiting for transfers between devices: 177 us -> none  [per_device(): lax.all_gather(normed[c * per:(c + 1) * per], 'model', axis=1, tiled=True)]
    dot_general x15 -> x0, matrix products: 73.4 us -> none  [the longest x14 69.9 us: dot_f32(): return jnp.dot(lhs, rhs, preferred_element_type=jnp.float32)]
    psum x2 -> x0, waiting for transfers between devices: 39.6 us -> none  [the longest x1 38.8 us: per_device(): lax.psum(dot_f32(att, wo), 'model')]
    unnamed x43 -> x12, local copies, waits for them, and re-layouts: 43.6 us -> 6.57 us
    psum x1 -> x0, blocking collectives: 28.5 us -> none  [per_device(): lax.psum(jnp.where(mine[:, None], picked, 0).astype(jnp.float32), 'model')]
    reshape x8 -> x2, local copies, waits for them, and re-layouts: 24.1 us -> 0.74 us  [per_device(): q_rows.reshape(2, n_batch, heads, HEAD_DIM).transpose(1, 0, 2, 3)]
    broadcast_in_dim x2 -> x0, other arithmetic: 17.8 us -> none  [per_device(): return (rows[:n_batch], rows[n_batch:], key_cache[None], val_cache[None])]
  transfers between devices with their start and end apart: 6 -> 0, of which waited for: 6 -> 0; matrix products, arithmetic and copies ran while one was open for 26% -> 0% of each run, Pallas kernels for 0% -> 0%
where the time goes in v2:
time: 243 us; the launch traced here: 242 us
  Pallas kernels  232 us (95%)
  local copies, waits for them, and re-layouts  8.85 us (4%)
    pallas_call x1, Pallas kernels, per_device(): pl.pallas_call(functools.partial(exchange_kernel, n_dev), out_shape=(cach...  190 us
    pallas_call x1, Pallas kernels, per_device(): pl.pallas_call(functools.partial(tail_kernel, n_dev), out_shape=jax.Shape...  24.5 us
    pallas_call x1, Pallas kernels, per_device(): pl.pallas_call(attention_kernel, grid_spec=pltpu.PrefetchScalarGridSpec(n...  17.1 us
    unnamed x12, local copies, waits for them, and re-layouts  6.57 us

profile of v2, /device:TPU:113, one launch (start us, length us, event | category | flops | bytes accessed | tf_op | source)
XLA Modules:
  0.0 242.2 jit_solution(12980703709195727436)
XLA Ops:
  0.6 190.4 %exchange.1 = (bf16[16,769,2,128]{3,2,1,0:T(2,128)(2,1)}, bf16[16,769,2,128]{3,2,1,0:T(2,128)(2,1)}, bf16[32,256]{1,0:T(8,128)(2,1)}, bf16[32,2048]{1,0:T(8,128)...) custom-call(s32[16]{0:T(128)} %len_ref.3, bf16[16,96,2048]{2,1,0:T(8,128)(2,1)} %x_hbm.1, ...), custom_call_target="tpu_custom_call" | custom-call | tf_op jit(solution)/shard_map/exchange/pallas_call | solution.py:328
  191.1 0.7 reshape.18
  191.8 0.6 pad_maximum_fusion.q_ref
  192.4 0.0 copy-start.3
  192.5 0.0 copy-start.4
  192.5 0.0 copy-start.5
  192.5 17.1 %attend.1 = (bf16[16,769,2,128]{3,2,1,0:T(2,128)(2,1)}, bf16[16,769,2,128]{3,2,1,0:T(2,128)(2,1)}, f32[16,8,128]{2,1,0:T(8,128)}) custom-call(s32[16]{0:T(128)} %len_ref.3, bf16[16,8,128]{2,1,0:T(8,128)(2,1)} %pad_maximum_fusion.q_ref, bf16[16,2,128]{2,1,0:T(2,128)(2,1)} %get-tuple-element.14.kn_ref, bf16[16,2,128]{2,1,0:T(2,128)(2,1)} %get-tuple-element.15.vn_ref, ...), custom_call_target="tpu_custom_call" | custom-call | tf_op jit(solution)/shard_map/attend/pallas_call | solution.py:358
  209.5 0.8 slice.15
  210.4 0.0 copy-done.3
  210.4 0.0 copy-done.4
  210.4 0.0 copy-done.5
  210.4 0.0 copy-start
  210.4 2.2 copy-done
  212.6 0.0 copy-start.1
  212.6 2.2 copy-done.1
  214.8 0.0 copy-start.2
  214.8 2.2 copy-done.2
  217.0 24.5 %tail.1 = bf16[32,2048]{1,0:T(8,128)(2,1)S(1)} custom-call(bf16[32,256]{1,0:T(8,128)(2,1)S(1)} %bitcast.19, bf16[32,2048]{1,0:T(8,128)(2,1)S(1)} %copy-done.4, bf16[256,2048]{1,0:T(8,128)(2,1)S(1)} %bitcast.18, bf16[1,2048]{1,0:T(2,128)(2,1)S(1)} %copy-done.5, bf16[2048,1024]{1,0:T(8,128)(2,1)S(1)} %bitcast.15, bf16[2048,1024]{1,0:T(8,128)(2,1)S(1)} %bitcast.16, ...), custom_call_target="tpu_custom_call" | custom-call | tf_op jit(solution)/shard_map/tail/pallas_call | solution.py:370
  241.5 0.7 fusion
  (3 shorter events, 0.0 us)
Async XLA Ops:
  192.4 17.9 %copy-start.3 = (bf16[1,256,2048]{2,1,0:T(8,128)(2,1)S(1)}, bf16[1,256,2048]{2,1,0:T(8,128)(2,1)}, u32[]{:S(2)}) copy-start(bf16[1,256,2048]{2,1,0:T(8,128)(2,1)} %param.21) | copy-start | bytes 3145732
  192.5 18.0 %copy-start.4 = (bf16[32,2048]{1,0:T(8,128)(2,1)S(1)}, bf16[32,2048]{1,0:T(8,128)(2,1)}, u32[]{:S(2)}) copy-start(bf16[32,2048]{1,0:T(8,128)(2,1)} %get-tuple-element.19.rows_ref) | copy-start | bytes 393220
  192.5 18.0 %copy-start.5 = (bf16[1,2048]{1,0:T(2,128)(2,1)S(1)}, bf16[1,2048]{1,0:T(2,128)(2,1)}, u32[]{:S(2)}) copy-start(bf16[1,2048]{1,0:T(2,128)(2,1)} %gain_ref.3) | copy-start | bytes 12292
  210.4 2.2 copy-start
  212.6 2.2 copy-start.1
  214.8 2.2 copy-start.2

commit v3 on v2

v3 whole, which is shorter than its diff:
```python
import functools

import numpy as np

import jax
import jax.numpy as jnp
from jax import lax
from jax.experimental import pallas as pl
from jax.experimental.pallas import tpu as pltpu
from jax.sharding import PartitionSpec as P

HEAD_DIM = 128
NEG_BIG = -1e30
MESH = pl.DeviceIdType.MESH
GROUP = 2
F32 = jnp.float32
BF16 = jnp.bfloat16


def dot_f32(lhs, rhs):
    return jnp.dot(lhs, rhs, preferred_element_type=F32)


def rms_rows(rows_f32, gain_f32):
    inv_rms = lax.rsqrt(jnp.mean(rows_f32 * rows_f32, axis=-1, keepdims=True) + 1e-5)
    return (rows_f32 * inv_rms * gain_f32).astype(BF16)


def rope_half(head_f32, cos_t, sin_t):
    return head_f32 * cos_t + pltpu.roll(head_f32, HEAD_DIM // 2, 1) * sin_t


def remote(src, dst, send_sem, recv_sem, dev):
    return pltpu.make_async_remote_copy(src_ref=src, dst_ref=dst, send_sem=send_sem, recv_sem=recv_sem,
                                        device_id={'model': dev}, device_id_type=MESH)


def wait_bytes(ref, sem):
    pltpu.make_async_copy(ref, ref, sem).wait()


def greet(me, n_dev):
    barrier = pltpu.get_barrier_semaphore()
    for off in range(1, n_dev):
        pl.semaphore_signal(barrier, inc=1, device_id={'model': lax.rem(me + off, n_dev)}, device_id_type=MESH)
    pl.semaphore_wait(barrier, n_dev - 1)


def layer_kernel(n_dev, len_ref, x_hbm, wk_hbm, wv_hbm, wq_hbm, wo_hbm, wg_hbm, wu_hbm, wd_hbm, tok_ref, gain_ref, gain2_ref, cos_ref, sin_ref,
                 kout, vout, out_ref,
                 wbuf, wq, wo, wg, wu, wd, xown, xrecv, stage, ktmp, lfull, lrecv, lcols, crow, srow,
                 rows, qtmp, qall, knew, vnew, kself, vself, near, psend, prec, att, part, recv, hid,
                 xcopy_sem, wcopy_sem, wrecv_sem, wsend_sem, xrecv_sem, xsend_sem,
                 kv_recv_sem, kv_send_sem, kv_local_sem, l_send_sem, l_recv_sem, q_sem, p_sem, r_send_sem, r_recv_sem, h_send_sem, h_recv_sem, new_sem):
    n_batch, seq_loc, d_model = xown.shape
    n_chip = n_dev // 2
    half = n_batch // 2
    n_chunk = half // GROUP
    m_rows = GROUP * seq_loc
    seq_len = seq_loc * n_dev
    width = d_model // n_dev
    me = lax.axis_index('model')
    chip, core = me // 2, lax.rem(me, 2)
    left, right = lax.rem(chip + n_chip - 1, n_chip), lax.rem(chip + 1, n_chip)
    partner = chip * 2 + 1 - core
    w_hbm = (wk_hbm, wv_hbm)
    outs = (kout, vout)
    owners = (me, me, left * 2 + core, right * 2 + core)
    firsts = (0, half, 0, half)
    aims = (left, right, right, left)
    slots = (1, 2, 2, 1)

    def col(j):
        return pl.ds(pl.multiple_of(j * width, width), width)

    wlocal = [pltpu.make_async_copy(w_hbm[kv], wbuf.at[0, core, kv], wcopy_sem.at[kv]) for kv in range(2)]
    for cp in wlocal:
        cp.start()

    def xcopy(ch):
        return pltpu.make_async_copy(x_hbm.at[pl.ds(ch * GROUP, GROUP)], xown.at[pl.ds(ch * GROUP, GROUP)], xcopy_sem.at[ch])

    for ch in range(2 * n_chunk):
        xcopy(ch).start()
    later = [pltpu.make_async_copy(src, dst, wcopy_sem.at[2 + i])
             for i, (src, dst) in enumerate(((wq_hbm, wq), (wo_hbm, wo), (wg_hbm, wg), (wu_hbm, wu), (wd_hbm, wd)))]
    for cp in later:
        cp.start()

    greet(me, n_dev)

    wsends = []
    for kv in range(2):
        wsends.append(remote(w_hbm[kv], wbuf.at[1, core, kv], wsend_sem.at[0, kv], wrecv_sem.at[1, core, kv], right * 2 + core))
        wsends.append(remote(w_hbm[kv], wbuf.at[2, core, kv], wsend_sem.at[1, kv], wrecv_sem.at[2, core, kv], left * 2 + core))
        wsends.append(remote(w_hbm[kv], wbuf.at[0, core, kv], wsend_sem.at[2, kv], wrecv_sem.at[0, core, kv], partner))
    for cp in wsends:
        cp.start()

    xsends = []

    def send_rows(ci):
        for side, aim in ((0, right), (1, left)):
            xsends.append(remote(x_hbm.at[pl.ds(side * half + ci * GROUP, GROUP)], xrecv.at[side, pl.ds(ci * GROUP, GROUP)],
                                 xsend_sem.at[side, ci], xrecv_sem.at[side, ci], aim * 2 + core))
            xsends[-1].start()

    def to_peers(src_of, dst, send_sem, recv_sem):
        for off in range(1, n_dev):
            peer = lax.rem(me + off, n_dev)
            remote(src_of(peer), dst, send_sem, recv_sem, peer).start()

    gain = gain_ref[...].astype(F32)

    def normalize(ref):
        for g in range(GROUP):
            ref[g] = rms_rows(ref[g].astype(F32), gain)

    def piece_of(unit, ci, dst, kv):
        start = pl.multiple_of(owners[unit] * seq_loc, seq_loc)
        return (stage.at[unit, dst, kv, pl.ds(ci * GROUP, GROUP)],
                outs[kv].at[pl.ds(firsts[unit] + ci * GROUP, GROUP), pl.ds(start, seq_loc)])

    def make_kv(rows_ref, unit, ci, slot, kcore, dst):
        mat = rows_ref[...].reshape(m_rows, d_model)
        start = pl.multiple_of(owners[unit] * seq_loc, seq_loc)
        cos_t = jnp.concatenate([cos_ref[pl.ds(start, seq_loc), :]] * GROUP, axis=0)
        sin_t = jnp.concatenate([sin_ref[pl.ds(start, seq_loc), :]] * GROUP, axis=0)
        for kv in range(2):
            acc = dot_f32(mat, wbuf[slot, kcore, kv])
            for h in range(2):
                head = acc[:, h * HEAD_DIM:(h + 1) * HEAD_DIM]
                if kv == 0:
                    head = rope_half(head, cos_t, sin_t)
                ktmp[pl.ds(h, m_rows, stride=2), :] = head
            piece, place = piece_of(unit, ci, dst, kv)
            piece.reshape(2 * m_rows, HEAD_DIM)[...] = ktmp[...].astype(BF16)
            if dst == 3:
                pltpu.make_async_copy(piece, place, kv_local_sem.at[kv]).start()
            elif dst == 2:
                remote(piece, place, kv_send_sem, kv_recv_sem.at[kv], partner).start()

    def own_rows(unit, ci):
        return xown.at[pl.ds(firsts[unit] + ci * GROUP, GROUP)]

    waiting = [(units, ci, kcore, kv) for units in ((0, 1), (3, 2)) for ci in range(n_chunk) for kcore in range(2) for kv in range(2)]

    def send_kv(count):
        for _ in range(min(count, len(waiting))):
            units, ci, kcore, kv = waiting.pop(0)
            for unit in units:
                piece, place = piece_of(unit, ci, kcore, kv)
                remote(piece, place, kv_send_sem, kv_recv_sem.at[kv], aims[unit] * 2 + kcore).start()

    for cp in wlocal:
        cp.wait()
    base = me * seq_loc
    for unit in range(2):
        @pl.loop(0, n_chunk)
        def _(ci):
            xcopy(unit * n_chunk + ci).wait()
            for g in range(GROUP):
                b = firsts[unit] + ci * GROUP + g
                hit = lax.broadcasted_iota(jnp.int32, (16, seq_loc), 1) == len_ref[b] - 1 - base
                row = dot_f32(jnp.where(hit, 1.0, 0.0).astype(BF16), xown[b])
                lfull[pl.ds(b, 1), :] = row[0:1]
            normalize(own_rows(unit, ci))
            make_kv(own_rows(unit, ci), unit, ci, 0, core, 3)

    to_peers(lambda peer: lfull.at[:, col(peer)], lrecv.at[me], l_send_sem.at[0], l_recv_sem.at[0])
    lrecv[me] = lfull[:, col(me)]
    for ci in range(n_chunk // 2):
        send_rows(ci)

    for kv in range(2):
        wait_bytes(wbuf.at[0, 1 - core, kv], wrecv_sem.at[0, 1 - core, kv])
    for unit in range(2):
        @pl.loop(0, n_chunk)
        def _(ci):
            make_kv(own_rows(unit, ci), unit, ci, 0, 1 - core, 2)

    far = 1 << 20
    shape = near.shape
    r_idx = lax.broadcasted_iota(jnp.int32, shape, 0)
    c_idx = lax.broadcasted_iota(jnp.int32, shape, 1)
    match = (c_idx // (2 * seq_loc) == lax.rem(r_idx, half)) & (lax.rem(c_idx, 2) == lax.rem(r_idx // half, 2))
    near[...] = jnp.where(match, lax.rem(c_idx // 2, seq_loc), far)

    fwds = []
    for kv in range(2):
        for slot in (1, 2):
            wait_bytes(wbuf.at[slot, core, kv], wrecv_sem.at[slot, core, kv])
            fwds.append(remote(wbuf.at[slot, core, kv], wbuf.at[slot, core, kv], wsend_sem.at[2 + slot, kv],
                               wrecv_sem.at[slot, core, kv], partner))
            fwds[-1].start()
    for slot in (1, 2):
        for kv in range(2):
            wait_bytes(wbuf.at[slot, 1 - core, kv], wrecv_sem.at[slot, 1 - core, kv])

    @pl.loop(0, n_chunk)
    def _(ci):
        for kcore in range(2):
            for unit in range(2):
                make_kv(own_rows(unit, ci), unit, ci, slots[unit], kcore, kcore)

    wait_bytes(lrecv.at[pl.ds(0, n_dev - 1)], l_recv_sem.at[0])
    lcols[me] = jnp.sum(lrecv[...], axis=0).astype(BF16)
    to_peers(lambda peer: lcols.at[me], lcols.at[me], l_send_sem.at[1], l_recv_sem.at[1])
    for ci in range(n_chunk // 2, n_chunk):
        send_rows(ci)

    def received(ci):
        for side in range(2):
            rows_ref = xrecv.at[side, pl.ds(ci * GROUP, GROUP)]
            wait_bytes(rows_ref, xrecv_sem.at[side, ci])
            normalize(rows_ref)
            for kcore in range(2):
                make_kv(rows_ref, 2 + side, ci, slots[2 + side], kcore, kcore)
            make_kv(rows_ref, 2 + side, ci, 0, 1 - core, 2)
            make_kv(rows_ref, 2 + side, ci, 0, core, 3)

    @pl.loop(0, n_chunk // 2)
    def _(ci):
        received(ci)

    wait_bytes(lcols.at[pl.ds(0, n_dev - 1)], l_recv_sem.at[1])
    later[0].wait()
    rows[0:n_batch, :] = tok_ref[...]
    for j in range(n_dev):
        rows[n_batch:2 * n_batch, j * width:(j + 1) * width] = lcols[j]
    for b in range(n_batch):
        for r in range(2):
            at = jnp.maximum(len_ref[b] - r, 0)
            crow[pl.ds(r * n_batch + b, 1), :] = cos_ref[pl.ds(at, 1), :]
            srow[pl.ds(r * n_batch + b, 1), :] = sin_ref[pl.ds(at, 1), :]
    rows_n = rms_rows(rows[...].astype(F32), gain)
    q_acc = dot_f32(rows_n, wq[...])
    for h in range(2):
        head = rope_half(q_acc[:, h * HEAD_DIM:(h + 1) * HEAD_DIM], crow[...], srow[...])
        for r in range(2):
            for s in range(2):
                qtmp[pl.ds(((s * 2 + r) * 2 + h) * half, half), :] = head[r * n_batch + s * half:r * n_batch + (s + 1) * half]
    qall[me] = qtmp[...].astype(BF16)
    to_peers(lambda peer: qall.at[me], qall.at[me], q_sem.at[0], q_sem.at[1])
    send_kv(6)
    kself[...] = jnp.zeros_like(kself)
    vself[...] = jnp.zeros_like(vself)
    news = []
    for kv, (new, own) in enumerate(((knew, kself), (vnew, vself))):
        acc = dot_f32(rows_n[0:n_batch], wbuf[0, core, kv])
        for h in range(2):
            head = acc[:, h * HEAD_DIM:(h + 1) * HEAD_DIM]
            if kv == 0:
                head = rope_half(head, crow[0:n_batch, :], srow[0:n_batch, :])
            ktmp[pl.ds(h, n_batch, stride=2), :] = head
            head = head.astype(BF16).astype(F32)
            for s in range(2):
                own[pl.ds((s * 4 + h) * half, half), :] = head[s * half:(s + 1) * half]
        new.reshape(2 * n_batch, HEAD_DIM)[...] = ktmp[0:2 * n_batch, :].astype(BF16)
        news.append(pltpu.make_async_copy(new, outs[kv].at[pl.ds(0, n_batch), seq_len], new_sem.at[kv]))
        news[-1].start()

    @pl.loop(n_chunk // 2, n_chunk)
    def _(ci):
        received(ci)

    wait_bytes(qall.at[pl.ds(0, n_dev - 1)], q_sem.at[1])
    n_q = 4 * half
    scale = HEAD_DIM ** -0.5
    lane = lax.broadcasted_iota(jnp.int32, (n_q, HEAD_DIM), 1)
    q_row = lax.broadcasted_iota(jnp.int32, (n_q, 1), 0)
    q_len = []
    for s in range(2):
        vec = jnp.zeros((n_q, 1), jnp.int32)
        for b in range(half):
            vec = jnp.where(lax.rem(q_row, half) == b, len_ref[s * half + b], vec)
        q_len.append(vec)

    def partial_att(unit, dst):
        s = unit % 2
        target = (aims[unit] * 2, aims[unit] * 2 + 1, partner, me)[dst]
        q32 = qall[target, s * n_q:(s + 1) * n_q, :]
        keys = stage.at[unit, dst, 0].reshape(2 * half * seq_loc, HEAD_DIM)[...]
        vals = stage.at[unit, dst, 1].reshape(2 * half * seq_loc, HEAD_DIM)[...]
        scores = lax.dot_general(q32, keys, (((1,), (1,)), ((), ())), preferred_element_type=F32) * scale
        scores = jnp.where(near[...] < q_len[s] - owners[unit] * seq_loc, scores, NEG_BIG)
        top = jnp.max(scores, axis=1, keepdims=True)
        prob = jnp.exp(scores - top)
        total = jnp.sum(prob, axis=1, keepdims=True)
        acc = dot_f32(prob.astype(BF16), vals)
        dest = prec.at[3, unit] if dst == 3 else psend.at[dst, unit]
        dest[0] = acc
        dest[1] = jnp.where(lane < HEAD_DIM // 2, top, total)
        if dst == 2:
            remote(psend.at[dst, unit], prec.at[2, unit], p_sem.at[0], p_sem.at[1], partner).start()
        elif dst < 2:
            remote(psend.at[dst, unit], prec.at[core, unit], p_sem.at[0], p_sem.at[1], target).start()

    for dst in range(4):
        for unit in range(4):
            partial_att(unit, dst)
        send_kv(2)

    wait_bytes(prec.at[pl.ds(0, 3)], p_sem.at[1])
    for s in range(2):
        q32 = qall[me, s * n_q:(s + 1) * n_q, :].astype(F32)
        is_new = q_row < n_q // 2
        self_score = jnp.sum(q32 * kself[s * n_q:(s + 1) * n_q, :], axis=1, keepdims=True) * scale
        tops = [jnp.where(is_new, self_score, NEG_BIG)]
        sums = [jnp.where(is_new, 1.0, 0.0)]
        accs = [vself[s * n_q:(s + 1) * n_q, :]]
        for unit in (s, s + 2):
            for src in range(4):
                stat = prec[src, unit, 1]
                tops.append(stat[:, 0:1])
                sums.append(stat[:, HEAD_DIM // 2:HEAD_DIM // 2 + 1])
                accs.append(prec[src, unit, 0])
        top = functools.reduce(jnp.maximum, tops)
        facs = [jnp.exp(t - top) for t in tops]
        total = sum(f * l for f, l in zip(facs, sums))
        merged = sum(f * a for f, a in zip(facs, accs)) / total
        for r in range(2):
            for h in range(2):
                att[r * n_batch + s * half:r * n_batch + (s + 1) * half, h * HEAD_DIM:(h + 1) * HEAD_DIM] = \
                    merged[(r * 2 + h) * half:(r * 2 + h + 1) * half]

    def add_partials(step, lot):
        to_peers(lambda peer: part.at[step, :, col(peer)], recv.at[step, me], r_send_sem.at[step], r_recv_sem.at[step])
        send_kv(lot)
        recv[step, me] = part[step, :, col(me)]
        mine = rows[:, col(me)].astype(F32)
        wait_bytes(recv.at[step, pl.ds(0, n_dev - 1)], r_recv_sem.at[step])
        hid[step, me] = (mine + jnp.sum(recv[step], axis=0)).astype(BF16)
        to_peers(lambda peer: hid.at[step, me], hid.at[step, me], h_send_sem.at[step], h_recv_sem.at[step])
        send_kv(lot)
        wait_bytes(hid.at[step, pl.ds(0, n_dev - 1)], h_recv_sem.at[step])

    later[1].wait()
    part[0] = dot_f32(att[...].astype(BF16), wo[...])
    add_partials(0, 4)
    for j in range(n_dev):
        rows[:, j * width:(j + 1) * width] = hid[0, j]
    for cp in later[2:]:
        cp.wait()
    rows_n = rms_rows(rows[...].astype(F32), gain2_ref[...].astype(F32))
    gate = dot_f32(rows_n, wg[...])
    mid = (gate * (1.0 / (1.0 + jnp.exp(-gate))) * dot_f32(rows_n, wu[...])).astype(BF16)
    part[1] = dot_f32(mid, wd[...])
    add_partials(1, 5)
    for j in range(n_dev):
        out_ref[:, j * width:(j + 1) * width] = hid[1, j]
    send_kv(len(waiting))

    quarter = n_batch // 4
    for kv in range(2):
        news[kv].wait()
        wait_bytes(outs[kv].at[pl.ds(0, quarter), pl.ds(0, seq_len)], kv_local_sem.at[kv])
        wait_bytes(outs[kv].at[pl.ds(0, 3 * quarter), pl.ds(0, seq_len)], kv_recv_sem.at[kv])
    for cp in wsends + fwds + xsends:
        cp.wait_send()
    wait_bytes(lrecv.at[pl.ds(0, n_dev - 1)], l_send_sem.at[0])
    wait_bytes(lcols.at[pl.ds(0, n_dev - 1)], l_send_sem.at[1])
    wait_bytes(qall.at[pl.ds(0, n_dev - 1)], q_sem.at[0])
    wait_bytes(psend, p_sem.at[0])
    for step in range(2):
        wait_bytes(recv.at[step, pl.ds(0, n_dev - 1)], r_send_sem.at[step])
        wait_bytes(hid.at[step, pl.ds(0, n_dev - 1)], h_send_sem.at[step])
    wait_bytes(stage.at[:, pl.ds(0, 3)], kv_send_sem)


def rotary_tables(n_pos):
    inv_freq = np.float32(10000.0) ** (-2.0 * np.arange(HEAD_DIM // 2, dtype=np.float32) / HEAD_DIM).astype(np.float32)
    angles = np.arange(n_pos, dtype=np.float32)[:, None] * inv_freq.astype(np.float32)
    cos, sin = np.cos(angles), np.sin(angles)
    return (np.concatenate([cos, cos], axis=1).astype(np.float32), np.concatenate([-sin, sin], axis=1).astype(np.float32))


def solution(mesh):
    n_dev = mesh.shape['model']
    seq_spec = P('replica', 'model', None)
    col_spec = P(None, None, 'model')
    row_spec = P(None, 'model', None)
    gain_spec = P(None, None)
    tok_spec = P('replica', None)
    cache_spec = P(None, 'replica', None, 'model', None)
    in_specs = (seq_spec, P('replica'), tok_spec, gain_spec, col_spec, col_spec, col_spec, row_spec, gain_spec, col_spec, col_spec, row_spec)
    out_specs = (tok_spec, tok_spec, cache_spec, cache_spec)
    hbm = pl.BlockSpec(memory_space=pl.ANY)
    vmem = pl.BlockSpec(memory_space=pltpu.VMEM)
    smem = pl.BlockSpec(memory_space=pltpu.SMEM)
    dma = pltpu.SemaphoreType.DMA

    def per_device(prompt, lengths, new_tok, norm_attn, w_q, w_k, w_v, w_o, norm_mlp, w_gate, w_up, w_down):
        n_batch, seq_loc, d_model = prompt.shape
        kv_width = w_k.shape[2]
        heads = kv_width // HEAD_DIM
        seq_len = seq_loc * n_dev
        half = n_batch // 2
        n_chunk = half // GROUP
        width = d_model // n_dev
        wq, wk, wv, wo, wg, wu, wd = w_q[0], w_k[0], w_v[0], w_o[0], w_gate[0], w_up[0], w_down[0]
        cos_tab, sin_tab = (jnp.asarray(t) for t in rotary_tables(seq_len + 8))

        ff = wg.shape[1]
        n_q = 4 * half
        cache = jax.ShapeDtypeStruct((n_batch, seq_len + 1, heads, HEAD_DIM), BF16)
        scratch = lambda *shape, dtype=F32: pltpu.VMEM(shape, dtype)
        key_cache, val_cache, out = pl.pallas_call(
            functools.partial(layer_kernel, n_dev),
            out_shape=(cache, cache, jax.ShapeDtypeStruct((2 * n_batch, d_model), BF16)),
            in_specs=[smem] + [hbm] * 8 + [vmem] * 5,
            out_specs=(hbm, hbm, vmem),
            scratch_shapes=[
                scratch(3, 2, 2, d_model, kv_width, dtype=BF16),
                scratch(d_model, kv_width, dtype=BF16),
                scratch(kv_width, d_model, dtype=BF16),
                scratch(d_model, ff, dtype=BF16), scratch(d_model, ff, dtype=BF16), scratch(ff, d_model, dtype=BF16),
                scratch(n_batch, seq_loc, d_model, dtype=BF16),
                scratch(2, half, seq_loc, d_model, dtype=BF16),
                scratch(4, 4, 2, half, seq_loc, heads, HEAD_DIM, dtype=BF16),
                scratch(2 * GROUP * seq_loc, HEAD_DIM),
                scratch(n_batch, d_model), scratch(n_dev, n_batch, width), scratch(n_dev, n_batch, width, dtype=BF16),
                scratch(2 * n_batch, HEAD_DIM), scratch(2 * n_batch, HEAD_DIM),
                scratch(2 * n_batch, d_model, dtype=BF16),
                scratch(2 * n_q, HEAD_DIM), scratch(n_dev, 2 * n_q, HEAD_DIM, dtype=BF16),
                scratch(n_batch, heads, HEAD_DIM, dtype=BF16), scratch(n_batch, heads, HEAD_DIM, dtype=BF16),
                scratch(2 * n_q, HEAD_DIM), scratch(2 * n_q, HEAD_DIM),
                scratch(n_q, 2 * half * seq_loc, dtype=jnp.int32),
                scratch(3, 4, 2, n_q, HEAD_DIM), scratch(4, 4, 2, n_q, HEAD_DIM),
                scratch(2 * n_batch, kv_width),
                scratch(2, 2 * n_batch, d_model), scratch(2, n_dev, 2 * n_batch, width),
                scratch(2, n_dev, 2 * n_batch, width, dtype=BF16),
                dma((2 * n_chunk,)), dma((7,)), dma((3, 2, 2)), dma((5, 2)), dma((2, n_chunk)), dma((2, n_chunk)),
                dma((2,)), dma(()), dma((2,)), dma((2,)), dma((2,)), dma((2,)), dma((2,)),
                dma((2,)), dma((2,)), dma((2,)), dma((2,)), dma((2,)),
            ],
            compiler_params=pltpu.CompilerParams(collective_id=0, has_side_effects=True, vmem_limit_bytes=63 * 2 ** 20),
            name='layer',
        )(lengths, prompt, wk, wv, wq, wo, wg, wu, wd, new_tok, norm_attn, norm_mlp, cos_tab, sin_tab)
        return out[:n_batch], out[n_batch:], key_cache[None], val_cache[None]

    return jax.shard_map(per_device, mesh=mesh, in_specs=in_specs, out_specs=out_specs, check_vma=False)
```

time: 243 us -> 215 us (0.88)
  Pallas kernels: 232 us -> 203 us
  local copies, waits for them, and re-layouts: 8.85 us -> 11.3 us
    pallas_call x3 -> x1, Pallas kernels: 232 us -> 203 us  [per_device(): pl.pallas_call(functools.partial(layer_kernel, n_dev), out_shape=(cache,...]
    unnamed x12 -> x6, local copies, waits for them, and re-layouts: 6.57 us -> 9.67 us
where the time goes in v3:
time: 215 us
  Pallas kernels  203 us (94%)
  local copies, waits for them, and re-layouts  11.3 us (5%)
    pallas_call x1, Pallas kernels, per_device(): pl.pallas_call(functools.partial(layer_kernel, n_dev), out_shape=(cache,...  203 us
    unnamed x6, local copies, waits for them, and re-layouts  9.67 us

profile of v3, /device:TPU:113, one launch (start us, length us, event | category | flops | bytes accessed | tf_op | source)
XLA Modules:
  0.0 215.2 jit_solution(15580364974228330270)
XLA Ops:
  0.6 203.2 %layer.1 = (bf16[16,769,2,128]{3,2,1,0:T(2,128)(2,1)}, bf16[16,769,2,128]{3,2,1,0:T(2,128)(2,1)}, bf16[32,2048]{1,0:T(8,128)(2,1)}) custom-call(s32[16]{0:T(128)} %len_ref.1, bf16[16,96,2048]{2,1,0:T(8,128)(2,1)} %x_hbm.1, bf16[2048,256]{1,0:T(8,128)(2,1)} %bitcast.16, bf16[2048,256]{1,0:T(8,128)(2,1)} %bitcast.17, bf16[2048,256]{1,0:T(8,128)(2,1)} %bitcast.18, ...), custom_call_target="tpu_custom_call" | custom-call | tf_op jit(solution)/shard_map/layer/pallas_call | solution.py:408
  203.9 0.0 slice-start
  203.9 1.7 fusion
  205.6 0.0 slice-start.1
  205.6 6.9 %copy.20 = bf16[1,16,769,2,128]{4,3,2,1,0:T(2,128)(2,1)} copy(bf16[1,16,769,2,128]{4,3,2,1,0:T(2,128)(2,1)} %bitcast.12) | data formatting | bytes 12599296
  212.5 0.0 slice-done
  212.5 0.0 slice-done.1
  212.5 2.7 %copy.21 = bf16[1,16,769,2,128]{4,3,2,1,0:T(2,128)(2,1)} copy(bf16[1,16,769,2,128]{4,3,2,1,0:T(2,128)(2,1)S(1)} %bitcast.11) | data formatting | bytes 12599296
  (1 shorter events, 0.0 us)
Async XLA Ops:
  203.9 8.6 %slice-start = ((s8[6299648]{0:T(1024)(128)(4,1)}), s8[4194304]{0:T(1024)(128)(4,1)S(1)}, s32[]{:S(2)}) async-start(s8[6299648]{0:T(1024)(128)(4,1)} %bitcast.9), calls=%async_computation | async-start | bytes 8388608
  205.6 7.0 %slice-start.1 = ((s8[6299648]{0:T(1024)(128)(4,1)}), s8[2105344]{0:T(1024)(128)(4,1)S(1)}, s32[]{:S(2)}) async-start(s8[6299648]{0:T(1024)(128)(4,1)} %bitcast.9), calls=%async_computation.1 | async-start | bytes 4210688

commit v4 on v3

v4 whole, which is shorter than its diff:
```python
import functools

import numpy as np

import jax
import jax.numpy as jnp
from jax import lax
from jax.experimental import pallas as pl
from jax.experimental.pallas import tpu as pltpu
from jax.sharding import PartitionSpec as P

HEAD_DIM = 128
NEG_BIG = -1e30
MESH = pl.DeviceIdType.MESH
GROUP = 2
LOTS = (5, 1, 2)
F32 = jnp.float32
BF16 = jnp.bfloat16


def dot_f32(lhs, rhs):
    return jnp.dot(lhs, rhs, preferred_element_type=F32)


def rms_rows(rows_f32, gain_f32):
    inv_rms = lax.rsqrt(jnp.mean(rows_f32 * rows_f32, axis=-1, keepdims=True) + 1e-5)
    return (rows_f32 * inv_rms * gain_f32).astype(BF16)


def rope_half(head_f32, cos_t, sin_t):
    return head_f32 * cos_t + pltpu.roll(head_f32, HEAD_DIM // 2, 1) * sin_t


def remote(src, dst, send_sem, recv_sem, dev):
    return pltpu.make_async_remote_copy(src_ref=src, dst_ref=dst, send_sem=send_sem, recv_sem=recv_sem,
                                        device_id={'model': dev}, device_id_type=MESH)


def wait_bytes(ref, sem):
    pltpu.make_async_copy(ref, ref, sem).wait()


def layer_kernel(n_dev, n_rep, len_ref, x_hbm, wk_hbm, wv_hbm, wq_hbm, wo_hbm, wg_hbm, wu_hbm, wd_hbm, tok_ref, gain_ref, gain2_ref, cos_ref, sin_ref,
                 kout, vout, dec_out, last_out,
                 wbuf, wq, wo, wg, wu, wd, xown, xrecv, stage, ktmp, lfull, lgot, lpair, lrecv, lcols, crow, srow,
                 rows, qtmp, qall, knew, vnew, kself, vself, near, psend, prec, att, part, got, pair, recv, hid,
                 xcopy_sem, wcopy_sem, wrecv_sem, wsend_sem, wown_sem, wfwd_sem, ysend_sem, yrecv_sem, xrecv_sem, xsend_sem,
                 kv_recv_sem, kv_send_sem, kv_local_sem, p_sem, new_sem, sum_sem, all_sem):
    n_batch, seq_loc, d_model = xown.shape
    n_chip = n_dev // 2
    half = n_batch // 2
    n_chunk = half // GROUP
    m_rows = GROUP * seq_loc
    seq_len = seq_loc * n_dev
    width = d_model // n_dev
    me = lax.axis_index('model')
    rep = lax.axis_index('replica')
    chip, core = me // 2, lax.rem(me, 2)
    left, right = lax.rem(chip + n_chip - 1, n_chip), lax.rem(chip + 1, n_chip)
    partner = chip * 2 + 1 - core
    w_hbm = (wk_hbm, wv_hbm)
    outs = (kout, vout)
    owners = (me, me, left * 2 + core, right * 2 + core)
    firsts = (0, half, 0, half)
    aims = (left, right, right, left)
    slots = (1, 2, 2, 1)

    def col(j):
        return pl.ds(pl.multiple_of(j * width, width), width)

    wlocal = [pltpu.make_async_copy(w_hbm[kv], wbuf.at[0, core, kv], wcopy_sem.at[kv]) for kv in range(2)]
    for cp in wlocal:
        cp.start()

    def xcopy(ch):
        return pltpu.make_async_copy(x_hbm.at[pl.ds(ch * GROUP, GROUP)], xown.at[pl.ds(ch * GROUP, GROUP)], xcopy_sem.at[ch])

    for ch in range(2 * n_chunk):
        xcopy(ch).start()
    later = [pltpu.make_async_copy(src, dst, wcopy_sem.at[2 + i])
             for i, (src, dst) in enumerate(((wq_hbm, wq), (wo_hbm, wo), (wg_hbm, wg), (wu_hbm, wu), (wd_hbm, wd)))]
    for cp in later:
        cp.start()

    barrier = pltpu.get_barrier_semaphore()
    for off in range(1, n_dev):
        pl.semaphore_signal(barrier, inc=1, device_id={'model': lax.rem(me + off, n_dev)}, device_id_type=MESH)

    @pl.loop(1, n_rep)
    def _(off):
        pl.semaphore_signal(barrier, inc=1, device_id={'replica': lax.rem(rep + off, n_rep)}, device_id_type=MESH)

    pl.semaphore_wait(barrier, n_dev + n_rep - 2)

    n_sub = 2
    slice_rows = d_model // n_rep
    sub_rows = slice_rows // n_sub

    def w_slice(h):
        return pl.ds(pl.multiple_of(rep * slice_rows + h * sub_rows, sub_rows), sub_rows)

    wsends = []
    for kv in range(2):
        for h in range(n_sub):
            for slot, aim in ((1, right), (2, left)):
                wsends.append(remote(w_hbm[kv].at[w_slice(h)], wbuf.at[slot, core, kv, w_slice(h)],
                                     wsend_sem.at[slot - 1, kv, h], wrecv_sem.at[slot - 1, kv, h], aim * 2 + core))
        wsends.append(remote(w_hbm[kv], wbuf.at[0, core, kv], wown_sem.at[0, kv], wown_sem.at[1, kv], partner))
    for cp in wsends:
        cp.start()

    def pass_on(kv, h):
        for slot in (1, 2):
            block = wbuf.at[slot, core, kv, w_slice(h)]
            wait_bytes(block, wrecv_sem.at[slot - 1, kv, h])

            @pl.loop(1, n_rep)
            def _(off):
                pltpu.make_async_remote_copy(src_ref=block, dst_ref=block, send_sem=ysend_sem, recv_sem=yrecv_sem.at[slot - 1, kv],
                                             device_id={'replica': lax.rem(rep + off, n_rep)}, device_id_type=MESH).start()

    xsends = []

    def send_rows(ci):
        for side, aim in ((0, right), (1, left)):
            xsends.append(remote(x_hbm.at[pl.ds(side * half + ci * GROUP, GROUP)], xrecv.at[side, pl.ds(ci * GROUP, GROUP)],
                                 xsend_sem.at[side, ci], xrecv_sem.at[side, ci], aim * 2 + core))
            xsends[-1].start()

    def other_chips():
        return [lax.rem(chip + off, n_chip) for off in range(1, n_chip)]

    def sum_pair(index, full, got_ref):
        for c in range(n_chip):
            remote(full.at[:, col(c * 2 + 1 - core)], got_ref.at[c], sum_sem.at[index, 0], sum_sem.at[index, 1], partner).start()

    def sum_chips(index, full, got_ref, pair_ref, recv_ref):
        wait_bytes(got_ref, sum_sem.at[index, 1])
        for c in range(n_chip):
            pair_ref[c] = full[:, col(c * 2 + core)] + got_ref[c]
        for c in other_chips():
            remote(pair_ref.at[c], recv_ref.at[chip], sum_sem.at[index, 2], sum_sem.at[index, 3], c * 2 + core).start()
        recv_ref[chip] = pair_ref[chip]

    def sum_end(index, recv_ref):
        wait_bytes(recv_ref.at[pl.ds(0, n_chip - 1)], sum_sem.at[index, 3])
        return jnp.sum(recv_ref[...], axis=0)

    def gather(index, buf):
        for c in other_chips():
            remote(buf.at[me], buf.at[me], all_sem.at[index, 0], all_sem.at[index, 1], c * 2 + core).start()
        remote(buf.at[me], buf.at[me], all_sem.at[index, 2], all_sem.at[index, 3], partner).start()

    def gather_pass(index, buf):
        wait_bytes(buf.at[pl.ds(0, n_chip - 1)], all_sem.at[index, 1])
        for c in other_chips():
            remote(buf.at[c * 2 + core], buf.at[c * 2 + core], all_sem.at[index, 2], all_sem.at[index, 3], partner).start()

    def gather_end(index, buf):
        wait_bytes(buf.at[pl.ds(0, n_chip)], all_sem.at[index, 3])

    gain = gain_ref[...].astype(F32)

    def normalize(ref):
        for g in range(GROUP):
            ref[g] = rms_rows(ref[g].astype(F32), gain)

    def make_kv(rows_ref, unit, ci, owner, b0, slot, kcore, dst):
        mat = rows_ref[...].reshape(m_rows, d_model)
        start = pl.multiple_of(owner * seq_loc, seq_loc)
        cos_t = jnp.concatenate([cos_ref[pl.ds(start, seq_loc), :]] * GROUP, axis=0)
        sin_t = jnp.concatenate([sin_ref[pl.ds(start, seq_loc), :]] * GROUP, axis=0)
        for kv in range(2):
            acc = dot_f32(mat, wbuf[slot, kcore, kv])
            for h in range(2):
                head = acc[:, h * HEAD_DIM:(h + 1) * HEAD_DIM]
                if kv == 0:
                    head = rope_half(head, cos_t, sin_t)
                ktmp[pl.ds(h, m_rows, stride=2), :] = head
            piece = stage.at[unit, dst, kv, pl.ds(ci * GROUP, GROUP)]
            piece.reshape(2 * m_rows, HEAD_DIM)[...] = ktmp[...].astype(BF16)
            place = outs[kv].at[pl.ds(b0, GROUP), pl.ds(start, seq_loc)]
            if slot == 0 and dst == 3:
                pltpu.make_async_copy(piece, place, kv_local_sem.at[kv]).start()
            elif slot == 0:
                remote(piece, place, kv_send_sem, kv_recv_sem.at[kv], partner).start()

    waiting = [(units, ci, kcore, kv) for units in ((0, 1), (3, 2)) for ci in range(n_chunk) for kcore in range(2) for kv in range(2)]

    def send_kv(count):
        for _ in range(min(count, len(waiting))):
            units, ci, kcore, kv = waiting.pop(0)
            for unit in units:
                start = pl.multiple_of(owners[unit] * seq_loc, seq_loc)
                remote(stage.at[unit, kcore, kv, pl.ds(ci * GROUP, GROUP)],
                       outs[kv].at[pl.ds(firsts[unit] + ci * GROUP, GROUP), pl.ds(start, seq_loc)],
                       kv_send_sem, kv_recv_sem.at[kv], aims[unit] * 2 + kcore).start()

    for cp in wlocal:
        cp.wait()
    base = me * seq_loc

    @pl.loop(0, 2 * n_chunk)
    def _(ch):
        xcopy(ch).wait()
        own = xown.at[pl.ds(ch * GROUP, GROUP)]
        for g in range(GROUP):
            b = ch * GROUP + g
            hit = lax.broadcasted_iota(jnp.int32, (16, seq_loc), 1) == len_ref[b] - 1 - base
            row = dot_f32(jnp.where(hit, 1.0, 0.0).astype(BF16), xown[b])
            lfull[pl.ds(b, 1), :] = row[0:1]
        normalize(own)
        make_kv(own, ch // n_chunk, lax.rem(ch, n_chunk), me, ch * GROUP, 0, core, 3)

    pass_on(0, 0)
    sum_pair(0, lfull, lgot)
    for kv in range(2):
        wait_bytes(wbuf.at[0, 1 - core, kv], wown_sem.at[1, kv])

    @pl.loop(0, 2 * n_chunk)
    def _(ch):
        make_kv(xown.at[pl.ds(ch * GROUP, GROUP)], ch // n_chunk, lax.rem(ch, n_chunk), me, ch * GROUP, 0, 1 - core, 2)

        @pl.when(ch == n_chunk - 1)
        def _():
            pass_on(0, 1)
            sum_chips(0, lfull, lgot, lpair, lrecv)

    send_rows(0)
    pass_on(1, 0)

    far = 1 << 20
    r_idx = lax.broadcasted_iota(jnp.int32, near.shape, 0)
    c_idx = lax.broadcasted_iota(jnp.int32, near.shape, 1)
    match = (c_idx // (2 * seq_loc) == lax.rem(r_idx, half)) & (lax.rem(c_idx, 2) == lax.rem(r_idx // half, 2))
    near[...] = jnp.where(match, lax.rem(c_idx // 2, seq_loc), far)

    pass_on(1, 1)
    lcols[me] = sum_end(0, lrecv).astype(BF16)
    gather(0, lcols)
    send_rows(1)

    rows[0:n_batch, :] = tok_ref[...]
    for b in range(n_batch):
        for r in range(2):
            at = jnp.maximum(len_ref[b] - r, 0)
            crow[pl.ds(r * n_batch + b, 1), :] = cos_ref[pl.ds(at, 1), :]
            srow[pl.ds(r * n_batch + b, 1), :] = sin_ref[pl.ds(at, 1), :]
    later[0].wait()
    gather_pass(0, lcols)
    gather_end(0, lcols)
    for j in range(n_dev):
        rows[n_batch:2 * n_batch, j * width:(j + 1) * width] = lcols[j]
    rows_n = rms_rows(rows[...].astype(F32), gain)
    q_acc = dot_f32(rows_n, wq[...])
    for h in range(2):
        head = rope_half(q_acc[:, h * HEAD_DIM:(h + 1) * HEAD_DIM], crow[...], srow[...])
        for r in range(2):
            for s in range(2):
                qtmp[pl.ds(((s * 2 + r) * 2 + h) * half, half), :] = head[r * n_batch + s * half:r * n_batch + (s + 1) * half]
    qall[me] = qtmp[...].astype(BF16)
    gather(1, qall)
    for ci in range(2, n_chunk):
        send_rows(ci)
    kself[...] = jnp.zeros_like(kself)
    vself[...] = jnp.zeros_like(vself)
    news = []
    for kv, (new, own) in enumerate(((knew, kself), (vnew, vself))):
        acc = dot_f32(rows_n[0:n_batch], wbuf[0, core, kv])
        for h in range(2):
            head = acc[:, h * HEAD_DIM:(h + 1) * HEAD_DIM]
            if kv == 0:
                head = rope_half(head, crow[0:n_batch, :], srow[0:n_batch, :])
            ktmp[pl.ds(h, n_batch, stride=2), :] = head
            head = head.astype(BF16).astype(F32)
            for s in range(2):
                own[pl.ds((s * 4 + h) * half, half), :] = head[s * half:(s + 1) * half]
        new.reshape(2 * n_batch, HEAD_DIM)[...] = ktmp[0:2 * n_batch, :].astype(BF16)
        news.append(pltpu.make_async_copy(new, outs[kv].at[pl.ds(0, n_batch), seq_len], new_sem.at[kv]))
        news[-1].start()

    fwds = []
    for kv in range(2):
        for slot in (1, 2):
            if n_rep > 1:
                wait_bytes(wbuf.at[slot, core, kv, pl.ds(0, d_model - slice_rows)], yrecv_sem.at[slot - 1, kv])
            fwds.append(remote(wbuf.at[slot, core, kv], wbuf.at[slot, core, kv], wfwd_sem.at[0, slot - 1, kv], wfwd_sem.at[1, slot - 1, kv], partner))
            fwds[-1].start()
    for kv in range(2):
        for slot in (1, 2):
            wait_bytes(wbuf.at[slot, 1 - core, kv], wfwd_sem.at[1, slot - 1, kv])

    @pl.loop(0, n_chunk)
    def _(ci):
        @pl.loop(0, 2)
        def _(kcore):
            for unit in range(2):
                make_kv(xown.at[pl.ds(firsts[unit] + ci * GROUP, GROUP)], unit, ci, me, firsts[unit] + ci * GROUP, slots[unit], kcore, kcore)

    gather_pass(1, qall)
    send_kv(LOTS[0])

    @pl.loop(0, n_chunk)
    def _(ci):
        for side in range(2):
            unit = 2 + side
            rows_ref = xrecv.at[side, pl.ds(ci * GROUP, GROUP)]
            b0 = firsts[unit] + ci * GROUP
            wait_bytes(rows_ref, xrecv_sem.at[side, ci])
            normalize(rows_ref)

            @pl.loop(0, 2)
            def _(kcore):
                make_kv(rows_ref, unit, ci, owners[unit], b0, slots[unit], kcore, kcore)

            make_kv(rows_ref, unit, ci, owners[unit], b0, 0, 1 - core, 2)
            make_kv(rows_ref, unit, ci, owners[unit], b0, 0, core, 3)

    gather_end(1, qall)
    n_q = 4 * half
    scale = HEAD_DIM ** -0.5
    lane = lax.broadcasted_iota(jnp.int32, (n_q, HEAD_DIM), 1)
    q_row = lax.broadcasted_iota(jnp.int32, (n_q, 1), 0)
    q_len = []
    for s in range(2):
        vec = jnp.zeros((n_q, 1), jnp.int32)
        for b in range(half):
            vec = jnp.where(lax.rem(q_row, half) == b, len_ref[s * half + b], vec)
        q_len.append(vec)

    def partial_att(unit, dst):
        s = unit % 2
        target = (aims[unit] * 2, aims[unit] * 2 + 1, partner, me)[dst]
        q32 = qall[target, s * n_q:(s + 1) * n_q, :]
        keys = stage.at[unit, dst, 0].reshape(2 * half * seq_loc, HEAD_DIM)[...]
        vals = stage.at[unit, dst, 1].reshape(2 * half * seq_loc, HEAD_DIM)[...]
        scores = lax.dot_general(q32, keys, (((1,), (1,)), ((), ())), preferred_element_type=F32) * scale
        scores = jnp.where(near[...] < q_len[s] - owners[unit] * seq_loc, scores, NEG_BIG)
        top = jnp.max(scores, axis=1, keepdims=True)
        prob = jnp.exp(scores - top)
        total = jnp.sum(prob, axis=1, keepdims=True)
        acc = dot_f32(prob.astype(BF16), vals)
        dest = prec.at[3, unit] if dst == 3 else psend.at[dst, unit]
        dest[0] = acc
        dest[1] = jnp.where(lane < HEAD_DIM // 2, top, total)
        if dst == 2:
            remote(psend.at[dst, unit], prec.at[2, unit], p_sem.at[0], p_sem.at[1], partner).start()
        elif dst < 2:
            remote(psend.at[dst, unit], prec.at[core, unit], p_sem.at[0], p_sem.at[1], target).start()

    for dst in range(4):
        for unit in range(4):
            partial_att(unit, dst)
        send_kv(LOTS[1])

    wait_bytes(prec.at[pl.ds(0, 3)], p_sem.at[1])
    for s in range(2):
        q32 = qall[me, s * n_q:(s + 1) * n_q, :].astype(F32)
        is_new = q_row < n_q // 2
        self_score = jnp.sum(q32 * kself[s * n_q:(s + 1) * n_q, :], axis=1, keepdims=True) * scale
        tops = [jnp.where(is_new, self_score, NEG_BIG)]
        sums = [jnp.where(is_new, 1.0, 0.0)]
        accs = [vself[s * n_q:(s + 1) * n_q, :]]
        for unit in (s, s + 2):
            for src in range(4):
                stat = prec[src, unit, 1]
                tops.append(stat[:, 0:1])
                sums.append(stat[:, HEAD_DIM // 2:HEAD_DIM // 2 + 1])
                accs.append(prec[src, unit, 0])
        top = functools.reduce(jnp.maximum, tops)
        facs = [jnp.exp(t - top) for t in tops]
        total = sum(f * l for f, l in zip(facs, sums))
        merged = sum(f * a for f, a in zip(facs, accs)) / total
        for r in range(2):
            for h in range(2):
                att[r * n_batch + s * half:r * n_batch + (s + 1) * half, h * HEAD_DIM:(h + 1) * HEAD_DIM] = \
                    merged[(r * 2 + h) * half:(r * 2 + h + 1) * half]

    def add_partials(step):
        sum_pair(1 + step, part.at[step], got.at[step])
        sum_chips(1 + step, part.at[step], got.at[step], pair.at[step], recv.at[step])
        send_kv(LOTS[2])
        mine = rows[:, col(me)].astype(F32)
        hid[step, me] = (mine + sum_end(1 + step, recv.at[step])).astype(BF16)
        gather(2 + step, hid.at[step])
        send_kv(LOTS[2])
        gather_pass(2 + step, hid.at[step])
        gather_end(2 + step, hid.at[step])

    later[1].wait()
    part[0] = dot_f32(att[...].astype(BF16), wo[...])
    add_partials(0)
    for j in range(n_dev):
        rows[:, j * width:(j + 1) * width] = hid[0, j]
    for cp in later[2:]:
        cp.wait()
    rows_n = rms_rows(rows[...].astype(F32), gain2_ref[...].astype(F32))
    gate = dot_f32(rows_n, wg[...])
    mid = (gate * (1.0 / (1.0 + jnp.exp(-gate))) * dot_f32(rows_n, wu[...])).astype(BF16)
    part[1] = dot_f32(mid, wd[...])
    add_partials(1)
    send_kv(len(waiting))
    for j in range(n_dev):
        dec_out[:, j * width:(j + 1) * width] = hid[1, j, 0:n_batch, :]
        last_out[:, j * width:(j + 1) * width] = hid[1, j, n_batch:2 * n_batch, :]

    for cp in wsends + fwds + xsends:
        cp.wait_send()
    if n_rep > 1:
        for slot in (1, 2):
            wait_bytes(wbuf.at[slot, 0, :, pl.ds(0, d_model - slice_rows)], ysend_sem)
    wait_bytes(psend, p_sem.at[0])
    for index, (got_ref, recv_ref) in enumerate(((lgot, lrecv), (got.at[0], recv.at[0]), (got.at[1], recv.at[1]))):
        wait_bytes(got_ref, sum_sem.at[index, 0])
        wait_bytes(recv_ref.at[pl.ds(0, n_chip - 1)], sum_sem.at[index, 2])
    for index, buf in enumerate((lcols, qall, hid.at[0], hid.at[1])):
        wait_bytes(buf.at[pl.ds(0, n_chip - 1)], all_sem.at[index, 0])
        wait_bytes(buf.at[pl.ds(0, n_chip)], all_sem.at[index, 2])
    quarter = n_batch // 4
    for kv in range(2):
        news[kv].wait()
        wait_bytes(outs[kv].at[pl.ds(0, quarter), pl.ds(0, seq_len)], kv_local_sem.at[kv])
        wait_bytes(outs[kv].at[pl.ds(0, 3 * quarter), pl.ds(0, seq_len)], kv_recv_sem.at[kv])
    wait_bytes(stage.at[:, pl.ds(0, 3)], kv_send_sem)


def rotary_tables(n_pos):
    inv_freq = np.float32(10000.0) ** (-2.0 * np.arange(HEAD_DIM // 2, dtype=np.float32) / HEAD_DIM).astype(np.float32)
    angles = np.arange(n_pos, dtype=np.float32)[:, None] * inv_freq.astype(np.float32)
    cos, sin = np.cos(angles), np.sin(angles)
    return (np.concatenate([cos, cos], axis=1).astype(np.float32), np.concatenate([-sin, sin], axis=1).astype(np.float32))


def solution(mesh):
    n_dev, n_rep = mesh.shape['model'], mesh.shape['replica']
    seq_spec = P('replica', 'model', None)
    col_spec = P(None, None, 'model')
    row_spec = P(None, 'model', None)
    gain_spec = P(None, None)
    tok_spec = P('replica', None)
    cache_spec = P(None, 'replica', None, 'model', None)
    in_specs = (seq_spec, P('replica'), tok_spec, gain_spec, col_spec, col_spec, col_spec, row_spec, gain_spec, col_spec, col_spec, row_spec)
    out_specs = (tok_spec, tok_spec, cache_spec, cache_spec)
    hbm = pl.BlockSpec(memory_space=pl.ANY)
    vmem = pl.BlockSpec(memory_space=pltpu.VMEM)
    smem = pl.BlockSpec(memory_space=pltpu.SMEM)
    dma = pltpu.SemaphoreType.DMA

    def per_device(prompt, lengths, new_tok, norm_attn, w_q, w_k, w_v, w_o, norm_mlp, w_gate, w_up, w_down):
        n_batch, seq_loc, d_model = prompt.shape
        kv_width = w_k.shape[2]
        heads = kv_width // HEAD_DIM
        seq_len = seq_loc * n_dev
        half = n_batch // 2
        n_chunk = half // GROUP
        width = d_model // n_dev
        wq, wk, wv, wo, wg, wu, wd = w_q[0], w_k[0], w_v[0], w_o[0], w_gate[0], w_up[0], w_down[0]
        cos_tab, sin_tab = (jnp.asarray(t) for t in rotary_tables(seq_len + 8))

        ff = wg.shape[1]
        n_q = 4 * half
        cache = jax.ShapeDtypeStruct((n_batch, seq_len + 1, heads, HEAD_DIM), BF16)
        scratch = lambda *shape, dtype=F32: pltpu.VMEM(shape, dtype)
        tail = jax.ShapeDtypeStruct((n_batch, d_model), BF16)
        n_chip = n_dev // 2
        key_cache, val_cache, dec, last = pl.pallas_call(
            functools.partial(layer_kernel, n_dev, n_rep),
            out_shape=(cache, cache, tail, tail),
            in_specs=[smem] + [hbm] * 8 + [vmem] * 5,
            out_specs=(hbm, hbm, vmem, vmem),
            scratch_shapes=[
                scratch(3, 2, 2, d_model, kv_width, dtype=BF16),
                scratch(d_model, kv_width, dtype=BF16),
                scratch(kv_width, d_model, dtype=BF16),
                scratch(d_model, ff, dtype=BF16), scratch(d_model, ff, dtype=BF16), scratch(ff, d_model, dtype=BF16),
                scratch(n_batch, seq_loc, d_model, dtype=BF16),
                scratch(2, half, seq_loc, d_model, dtype=BF16),
                scratch(4, 4, 2, half, seq_loc, heads, HEAD_DIM, dtype=BF16),
                scratch(2 * GROUP * seq_loc, HEAD_DIM),
                scratch(n_batch, d_model), scratch(n_chip, n_batch, width),
                scratch(n_chip, n_batch, width), scratch(n_chip, n_batch, width),
                scratch(n_dev, n_batch, width, dtype=BF16),
                scratch(2 * n_batch, HEAD_DIM), scratch(2 * n_batch, HEAD_DIM),
                scratch(2 * n_batch, d_model, dtype=BF16),
                scratch(2 * n_q, HEAD_DIM), scratch(n_dev, 2 * n_q, HEAD_DIM, dtype=BF16),
                scratch(n_batch, heads, HEAD_DIM, dtype=BF16), scratch(n_batch, heads, HEAD_DIM, dtype=BF16),
                scratch(2 * n_q, HEAD_DIM), scratch(2 * n_q, HEAD_DIM),
                scratch(n_q, 2 * half * seq_loc, dtype=jnp.int32),
                scratch(3, 4, 2, n_q, HEAD_DIM), scratch(4, 4, 2, n_q, HEAD_DIM),
                scratch(2 * n_batch, kv_width),
                scratch(2, 2 * n_batch, d_model), scratch(2, n_chip, 2 * n_batch, width),
                scratch(2, n_chip, 2 * n_batch, width), scratch(2, n_chip, 2 * n_batch, width),
                scratch(2, n_dev, 2 * n_batch, width, dtype=BF16),
                dma((2 * n_chunk,)), dma((7,)), dma((2, 2, 2)), dma((2, 2, 2)), dma((2, 2)), dma((2, 2, 2)), dma(()), dma((2, 2)),
                dma((2, n_chunk)), dma((2, n_chunk)),
                dma((2,)), dma(()), dma((2,)), dma((2,)), dma((2,)), dma((3, 4)), dma((4, 4)),
            ],
            compiler_params=pltpu.CompilerParams(collective_id=0, has_side_effects=True, vmem_limit_bytes=63 * 2 ** 20),
            name='layer',
        )(lengths, prompt, wk, wv, wq, wo, wg, wu, wd, new_tok, norm_attn, norm_mlp, cos_tab, sin_tab)
        return dec, last, key_cache[None], val_cache[None]

    return jax.shard_map(per_device, mesh=mesh, in_specs=in_specs, out_specs=out_specs, check_vma=False)
```

time: 215 us -> 193 us (0.90)
  Pallas kernels: 203 us -> 179 us
    pallas_call x1, Pallas kernels: 203 us -> 179 us  [per_device(): pl.pallas_call(functools.partial(layer_kernel, n_dev, n_rep), out_shape=(...]
    unnamed x6 -> x8, local copies, waits for them, and re-layouts: 9.67 us -> 12.8 us
where the time goes in v4:
time: 193 us
  Pallas kernels  179 us (93%)
  local copies, waits for them, and re-layouts  12.8 us (7%)
    pallas_call x1, Pallas kernels, per_device(): pl.pallas_call(functools.partial(layer_kernel, n_dev, n_rep), out_shape=(...  179 us
    unnamed x8, local copies, waits for them, and re-layouts  12.8 us

profile of v4, /device:TPU:113, one launch (start us, length us, event | category | flops | bytes accessed | tf_op | source)
XLA Modules:
  0.0 192.8 jit_solution(2430898510581432860)
XLA Ops:
  0.6 179.4 %layer.1 = (bf16[16,769,2,128]{3,2,1,0:T(2,128)(2,1)}, bf16[16,769,2,128]{3,2,1,0:T(2,128)(2,1)}, bf16[16,2048]{1,0:T(8,128)(2,1)}, bf16[16,2048]{1,0:T(8,128)(2,1)}) custom-call(s32[16]{0:T(128)} %len_ref.1, bf16[16,96,2048]{2,1,0:T(8,128)(2,1)} %x_hbm.1, bf16[2048,256]{1,0:T(8,128)(2,1)} %bitcast.16, bf16[2048,256]{1,0:T(8,128)(2,1)} %bitcast.17, ...), custom_call_target="tpu_custom_call" | custom-call | tf_op jit(solution)/shard_map/layer/pallas_call | solution.py:466
  180.0 1.5 copy.22
  181.5 0.0 slice-start
  181.5 1.6 copy.23
  183.1 0.0 slice-start.1
  183.1 6.9 %copy.24 = bf16[1,16,769,2,128]{4,3,2,1,0:T(2,128)(2,1)} copy(bf16[1,16,769,2,128]{4,3,2,1,0:T(2,128)(2,1)} %bitcast.12) | data formatting | bytes 12599296
  190.1 0.0 slice-done
  190.1 0.0 slice-done.1
  190.1 2.7 %copy.25 = bf16[1,16,769,2,128]{4,3,2,1,0:T(2,128)(2,1)} copy(bf16[1,16,769,2,128]{4,3,2,1,0:T(2,128)(2,1)S(1)} %bitcast.11) | data formatting | bytes 12599296
  (1 shorter events, 0.0 us)
Async XLA Ops:
  181.5 8.6 %slice-start = ((s8[6299648]{0:T(1024)(128)(4,1)}), s8[4194304]{0:T(1024)(128)(4,1)S(1)}, s32[]{:S(2)}) async-start(s8[6299648]{0:T(1024)(128)(4,1)} %bitcast.9), calls=%async_computation | async-start | bytes 8388608
  183.1 6.9 %slice-start.1 = ((s8[6299648]{0:T(1024)(128)(4,1)}), s8[2105344]{0:T(1024)(128)(4,1)S(1)}, s32[]{:S(2)}) async-start(s8[6299648]{0:T(1024)(128)(4,1)} %bitcast.9), calls=%async_computation.1 | async-start | bytes 4210688

commit v5 on v4

--- a/solution.py
+++ b/solution.py
@@ -13,7 +13,8 @@
 NEG_BIG = -1e30
 MESH = pl.DeviceIdType.MESH
 GROUP = 2
-LOTS = (5, 1, 2)
+VMEM_MIB = 49
+LOTS = (9, 1, 2)
 F32 = jnp.float32
 BF16 = jnp.bfloat16
 
@@ -42,10 +43,10 @@
 
 def layer_kernel(n_dev, n_rep, len_ref, x_hbm, wk_hbm, wv_hbm, wq_hbm, wo_hbm, wg_hbm, wu_hbm, wd_hbm, tok_ref, gain_ref, gain2_ref, cos_ref, sin_ref,
                  kout, vout, dec_out, last_out,
-                 wbuf, wq, wo, wg, wu, wd, xown, xrecv, stage, ktmp, lfull, lgot, lpair, lrecv, lcols, crow, srow,
+                 wbuf, wq, wo, xown, xrecv, stage, ktmp, lfull, lgot, lpair, lrecv, lcols, crow, srow,
                  rows, qtmp, qall, knew, vnew, kself, vself, near, psend, prec, att, part, got, pair, recv, hid,
                  xcopy_sem, wcopy_sem, wrecv_sem, wsend_sem, wown_sem, wfwd_sem, ysend_sem, yrecv_sem, xrecv_sem, xsend_sem,
-                 kv_recv_sem, kv_send_sem, kv_local_sem, p_sem, new_sem, sum_sem, all_sem):
+                 kv_recv_sem, kv_send_sem, p_sem, sum_sem, all_sem, mlp_sem):
     n_batch, seq_loc, d_model = xown.shape
     n_chip = n_dev // 2
     half = n_batch // 2
@@ -78,7 +79,7 @@
     for ch in range(2 * n_chunk):
         xcopy(ch).start()
     later = [pltpu.make_async_copy(src, dst, wcopy_sem.at[2 + i])
-             for i, (src, dst) in enumerate(((wq_hbm, wq), (wo_hbm, wo), (wg_hbm, wg), (wu_hbm, wu), (wd_hbm, wd)))]
+             for i, (src, dst) in enumerate(((wq_hbm, wq), (wo_hbm, wo)))]
     for cp in later:
         cp.start()
 
@@ -178,12 +179,14 @@
                     head = rope_half(head, cos_t, sin_t)
                 ktmp[pl.ds(h, m_rows, stride=2), :] = head
             piece = stage.at[unit, dst, kv, pl.ds(ci * GROUP, GROUP)]
-            piece.reshape(2 * m_rows, HEAD_DIM)[...] = ktmp[...].astype(BF16)
-            place = outs[kv].at[pl.ds(b0, GROUP), pl.ds(start, seq_loc)]
+            made = ktmp[...].astype(BF16)
+            piece.reshape(2 * m_rows, HEAD_DIM)[...] = made
             if slot == 0 and dst == 3:
-                pltpu.make_async_copy(piece, place, kv_local_sem.at[kv]).start()
+                for g in range(GROUP):
+                    outs[kv].at[b0 + g, pl.ds(start, seq_loc)].reshape(2 * seq_loc, HEAD_DIM)[...] = \
+                        made[g * 2 * seq_loc:(g + 1) * 2 * seq_loc]
             elif slot == 0:
-                remote(piece, place, kv_send_sem, kv_recv_sem.at[kv], partner).start()
+                remote(piece, outs[kv].at[pl.ds(b0, GROUP), pl.ds(start, seq_loc)], kv_send_sem, kv_recv_sem.at[kv], partner).start()
 
     waiting = [(units, ci, kcore, kv) for units in ((0, 1), (3, 2)) for ci in range(n_chunk) for kcore in range(2) for kv in range(2)]
 
@@ -264,7 +267,6 @@
         send_rows(ci)
     kself[...] = jnp.zeros_like(kself)
     vself[...] = jnp.zeros_like(vself)
-    news = []
     for kv, (new, own) in enumerate(((knew, kself), (vnew, vself))):
         acc = dot_f32(rows_n[0:n_batch], wbuf[0, core, kv])
         for h in range(2):
@@ -276,8 +278,8 @@
             for s in range(2):
                 own[pl.ds((s * 4 + h) * half, half), :] = head[s * half:(s + 1) * half]
         new.reshape(2 * n_batch, HEAD_DIM)[...] = ktmp[0:2 * n_batch, :].astype(BF16)
-        news.append(pltpu.make_async_copy(new, outs[kv].at[pl.ds(0, n_batch), seq_len], new_sem.at[kv]))
-        news[-1].start()
+        for b in range(n_batch):
+            outs[kv][b, seq_len] = new[b]
 
     fwds = []
     for kv in range(2):
@@ -315,6 +317,21 @@
 
             make_kv(rows_ref, unit, ci, owners[unit], b0, 0, 1 - core, 2)
             make_kv(rows_ref, unit, ci, owners[unit], b0, 0, core, 3)
+
+    for cp in wsends + fwds:
+        cp.wait_send()
+    if n_rep > 1:
+        for slot in (1, 2):
+            wait_bytes(wbuf.at[slot, 0, :, pl.ds(0, d_model - slice_rows)], ysend_sem)
+    ff, block = wd_hbm.shape[0], wbuf.shape[4]
+    places = [wbuf.at[i // 4, (i // 2) % 2, i % 2] for i in range(12)]
+    gate_w, up_w = places[0:4], places[4:8]
+    down_w = [places[8 + i // 2].at[pl.ds((i % 2) * ff, ff)] for i in range(8)]
+    mlp_copies = []
+    for i, (src, dsts) in enumerate(((wg_hbm, gate_w), (wu_hbm, up_w), (wd_hbm, down_w))):
+        for j, dst in enumerate(dsts):
+            mlp_copies.append(pltpu.make_async_copy(src.at[:, pl.ds(j * block, block)], dst, mlp_sem.at[i * 4 + j]))
+            mlp_copies[-1].start()
 
     gather_end(1, qall)
     n_q = 4 * half
@@ -392,23 +409,24 @@
     add_partials(0)
     for j in range(n_dev):
         rows[:, j * width:(j + 1) * width] = hid[0, j]
-    for cp in later[2:]:
+    for cp in mlp_copies:
         cp.wait()
     rows_n = rms_rows(rows[...].astype(F32), gain2_ref[...].astype(F32))
-    gate = dot_f32(rows_n, wg[...])
-    mid = (gate * (1.0 / (1.0 + jnp.exp(-gate))) * dot_f32(rows_n, wu[...])).astype(BF16)
-    part[1] = dot_f32(mid, wd[...])
+    mids = []
+    for g_ref, u_ref in zip(gate_w, up_w):
+        gate = dot_f32(rows_n, g_ref[...])
+        mids.append((gate * (1.0 / (1.0 + jnp.exp(-gate))) * dot_f32(rows_n, u_ref[...])).astype(BF16))
+    mid = jnp.concatenate(mids, axis=1)
+    for j, d_ref in enumerate(down_w):
+        part[1, :, j * block:(j + 1) * block] = dot_f32(mid, d_ref[...])
     add_partials(1)
     send_kv(len(waiting))
     for j in range(n_dev):
         dec_out[:, j * width:(j + 1) * width] = hid[1, j, 0:n_batch, :]
         last_out[:, j * width:(j + 1) * width] = hid[1, j, n_batch:2 * n_batch, :]
 
-    for cp in wsends + fwds + xsends:
+    for cp in xsends:
         cp.wait_send()
-    if n_rep > 1:
-        for slot in (1, 2):
-            wait_bytes(wbuf.at[slot, 0, :, pl.ds(0, d_model - slice_rows)], ysend_sem)
     wait_bytes(psend, p_sem.at[0])
     for index, (got_ref, recv_ref) in enumerate(((lgot, lrecv), (got.at[0], recv.at[0]), (got.at[1], recv.at[1]))):
         wait_bytes(got_ref, sum_sem.at[index, 0])
@@ -416,12 +434,18 @@
     for index, buf in enumerate((lcols, qall, hid.at[0], hid.at[1])):
         wait_bytes(buf.at[pl.ds(0, n_chip - 1)], all_sem.at[index, 0])
         wait_bytes(buf.at[pl.ds(0, n_chip)], all_sem.at[index, 2])
-    quarter = n_batch // 4
     for kv in range(2):
-        news[kv].wait()
-        wait_bytes(outs[kv].at[pl.ds(0, quarter), pl.ds(0, seq_len)], kv_local_sem.at[kv])
-        wait_bytes(outs[kv].at[pl.ds(0, 3 * quarter), pl.ds(0, seq_len)], kv_recv_sem.at[kv])
+        wait_bytes(outs[kv].at[pl.ds(0, 3 * n_batch // 4), pl.ds(0, seq_len)], kv_recv_sem.at[kv])
     wait_bytes(stage.at[:, pl.ds(0, 3)], kv_send_sem)
+
+
+def deliver_kernel(k_in, v_in, d_in, l_in, k_out, v_out, d_out, l_out, sem):
+    copies = [pltpu.make_async_copy(src, dst, sem.at[i])
+              for i, (src, dst) in enumerate(((k_in, k_out), (v_in, v_out), (d_in, d_out), (l_in, l_out)))]
+    for cp in copies:
+        cp.start()
+    for cp in copies:
+        cp.wait()
 
 
 def rotary_tables(n_pos):
@@ -461,18 +485,18 @@
         n_q = 4 * half
         cache = jax.ShapeDtypeStruct((n_batch, seq_len + 1, heads, HEAD_DIM), BF16)
         scratch = lambda *shape, dtype=F32: pltpu.VMEM(shape, dtype)
+        held = pltpu.VMEM(cache.shape, BF16)
         tail = jax.ShapeDtypeStruct((n_batch, d_model), BF16)
         n_chip = n_dev // 2
         key_cache, val_cache, dec, last = pl.pallas_call(
             functools.partial(layer_kernel, n_dev, n_rep),
-            out_shape=(cache, cache, tail, tail),
+            out_shape=(held, held, pltpu.VMEM(tail.shape, BF16), pltpu.VMEM(tail.shape, BF16)),
             in_specs=[smem] + [hbm] * 8 + [vmem] * 5,
-            out_specs=(hbm, hbm, vmem, vmem),
+            out_specs=(vmem,) * 4,
             scratch_shapes=[
                 scratch(3, 2, 2, d_model, kv_width, dtype=BF16),
                 scratch(d_model, kv_width, dtype=BF16),
                 scratch(kv_width, d_model, dtype=BF16),
-                scratch(d_model, ff, dtype=BF16), scratch(d_model, ff, dtype=BF16), scratch(ff, d_model, dtype=BF16),
                 scratch(n_batch, seq_loc, d_model, dtype=BF16),
                 scratch(2, half, seq_loc, d_model, dtype=BF16),
                 scratch(4, 4, 2, half, seq_loc, heads, HEAD_DIM, dtype=BF16),
@@ -491,13 +515,19 @@
                 scratch(2, 2 * n_batch, d_model), scratch(2, n_chip, 2 * n_batch, width),
                 scratch(2, n_chip, 2 * n_batch, width), scratch(2, n_chip, 2 * n_batch, width),
                 scratch(2, n_dev, 2 * n_batch, width, dtype=BF16),
-                dma((2 * n_chunk,)), dma((7,)), dma((2, 2, 2)), dma((2, 2, 2)), dma((2, 2)), dma((2, 2, 2)), dma(()), dma((2, 2)),
+                dma((2 * n_chunk,)), dma((4,)), dma((2, 2, 2)), dma((2, 2, 2)), dma((2, 2)), dma((2, 2, 2)), dma(()), dma((2, 2)),
                 dma((2, n_chunk)), dma((2, n_chunk)),
-                dma((2,)), dma(()), dma((2,)), dma((2,)), dma((2,)), dma((3, 4)), dma((4, 4)),
+                dma((2,)), dma(()), dma((2,)), dma((3, 4)), dma((4, 4)), dma((16,)),
             ],
-            compiler_params=pltpu.CompilerParams(collective_id=0, has_side_effects=True, vmem_limit_bytes=63 * 2 ** 20),
+            compiler_params=pltpu.CompilerParams(collective_id=0, has_side_effects=True, vmem_limit_bytes=VMEM_MIB * 2 ** 20),
             name='layer',
-        )(lengths, prompt, wk, wv, wq, wo, wg, wu, wd, new_tok, norm_attn, norm_mlp, cos_tab, sin_tab)
+        )(*(pltpu.with_memory_space_constraint(a, pltpu.HBM) for a in
+            (lengths, prompt, wk, wv, wq, wo, wg, wu, wd, new_tok, norm_attn, norm_mlp, cos_tab, sin_tab)))
+        key_cache, val_cache, dec, last = pl.pallas_call(
+            deliver_kernel, out_shape=(cache, cache, tail, tail), in_specs=[vmem] * 4, out_specs=(hbm,) * 4,
+            scratch_shapes=[dma((4,))], name='deliver',
+            compiler_params=pltpu.CompilerParams(vmem_limit_bytes=14 * 2 ** 20),
+        )(key_cache, val_cache, dec, last)
         return dec, last, key_cache[None], val_cache[None]
 
     return jax.shard_map(per_device, mesh=mesh, in_specs=in_specs, out_specs=out_specs, check_vma=False)

time: 193 us -> 184 us (0.953)
  local copies, waits for them, and re-layouts: 12.8 us -> 0 us
  Pallas kernels: 179 us -> 183 us
    unnamed x8 -> x0, local copies, waits for them, and re-layouts: 12.8 us -> none
    pallas_call x0 -> x1, Pallas kernels: none -> 4.82 us  [per_device(): pl.pallas_call(deliver_kernel, out_shape=(cache, cache, tail, tail), in_s...]
where the time goes in v5:
time: 184 us
  Pallas kernels  183 us (99%)
    pallas_call x1, Pallas kernels, per_device(): pl.pallas_call(functools.partial(layer_kernel, n_dev, n_rep), out_shape=(...  178 us
    pallas_call x1, Pallas kernels, per_device(): pl.pallas_call(deliver_kernel, out_shape=(cache, cache, tail, tail), in_s...  4.82 us

profile of v5, /device:TPU:113, one launch (start us, length us, event | category | flops | bytes accessed | tf_op | source)
XLA Modules:
  0.0 183.7 jit_solution(13876994105650032068)
XLA Ops:
  0.6 178.1 %layer.1 = (bf16[16,769,2,128]{3,2,1,0:T(2,128)(2,1)S(1)}, bf16[16,769,2,128]{3,2,1,0:T(2,128)(2,1)S(1)}, bf16[16,2048]{1,0:T(8,128)(2,1)S(1)}, bf16[16,2048]{1,0:T(8,128)(2,1)S(1)}) custom-call(s32[16]{0:T(128)} %len_ref.1, bf16[16,96,2048]{2,1,0:T(8,128)(2,1)} %x_hbm.1, bf16[2048,256]{1,0:T(8,128)(2,1)} %bitcast.12, bf16[2048,256]{1,0:T(8,128)(2,1)} %bitcast.13, ...), custom_call_target="tpu_custom_call" | custom-call | tf_op jit(solution)/shard_map/layer/pallas_call | solution.py:491
  178.7 4.8 %deliver.1 = (bf16[16,769,2,128]{3,2,1,0:T(2,128)(2,1)}, bf16[16,769,2,128]{3,2,1,0:T(2,128)(2,1)}, bf16[16,2048]{1,0:T(8,128)(2,1)}, bf16[16,2048]{1,0:T(8,128)(2,1)}) custom-call(bf16[16,769,2,128]{3,2,1,0:T(2,128)(2,1)S(1)} %get-tuple-element.12.k_in, bf16[16,769,2,128]{3,2,1,0:T(2,128)(2,1)S(1)} %get-tuple-element.13.v_in, ...), custom_call_target="tpu_custom_call" | custom-call | tf_op jit(solution)/shard_map/deliver/pallas_call | solution.py:526

commit v6 on v5

--- a/solution.py
+++ b/solution.py
@@ -14,7 +14,7 @@
 MESH = pl.DeviceIdType.MESH
 GROUP = 2
 VMEM_MIB = 49
-LOTS = (9, 1, 2)
+LOTS = (8, 1, 3, 2)
 F32 = jnp.float32
 BF16 = jnp.bfloat16
 
@@ -41,12 +41,12 @@
     pltpu.make_async_copy(ref, ref, sem).wait()
 
 
-def layer_kernel(n_dev, n_rep, len_ref, x_hbm, wk_hbm, wv_hbm, wq_hbm, wo_hbm, wg_hbm, wu_hbm, wd_hbm, tok_ref, gain_ref, gain2_ref, cos_ref, sin_ref,
+def layer_kernel(n_dev, n_rep, len_ref, x_hbm, wk_hbm, wv_hbm, wq_hbm, wo_hbm, wg_hbm, wu_hbm, wd_hbm, tok_hbm, gain_hbm, gain2_hbm, cos_hbm, sin_hbm,
                  kout, vout, dec_out, last_out,
                  wbuf, wq, wo, xown, xrecv, stage, ktmp, lfull, lgot, lpair, lrecv, lcols, crow, srow,
-                 rows, qtmp, qall, knew, vnew, kself, vself, near, psend, prec, att, part, got, pair, recv, hid,
+                 rows, qtmp, qall, knew, vnew, kself, vself, near, psend, prec, att, part, got, pair, far_got, comb, recv, hid, tok_ref, gain_ref, gain2_ref, cos_ref, sin_ref,
                  xcopy_sem, wcopy_sem, wrecv_sem, wsend_sem, wown_sem, wfwd_sem, ysend_sem, yrecv_sem, xrecv_sem, xsend_sem,
-                 kv_recv_sem, kv_send_sem, p_sem, sum_sem, all_sem, mlp_sem):
+                 kv_recv_sem, kv_send_sem, p_sem, sum_sem, all_sem, mlp_sem, small_sem):
     n_batch, seq_loc, d_model = xown.shape
     n_chip = n_dev // 2
     half = n_batch // 2
@@ -69,6 +69,18 @@
     def col(j):
         return pl.ds(pl.multiple_of(j * width, width), width)
 
+    barrier = pltpu.get_barrier_semaphore()
+    for off in range(1, n_dev):
+        pl.semaphore_signal(barrier, inc=1, device_id={'model': lax.rem(me + off, n_dev)}, device_id_type=MESH)
+
+    @pl.loop(1, n_rep)
+    def _(off):
+        pl.semaphore_signal(barrier, inc=1, device_id={'replica': lax.rem(rep + off, n_rep)}, device_id_type=MESH)
+
+    small = [pltpu.make_async_copy(src, dst, small_sem.at[i])
+             for i, (src, dst) in enumerate(((tok_hbm, tok_ref), (gain_hbm, gain_ref), (gain2_hbm, gain2_ref), (cos_hbm, cos_ref), (sin_hbm, sin_ref)))]
+    for cp in small:
+        cp.start()
     wlocal = [pltpu.make_async_copy(w_hbm[kv], wbuf.at[0, core, kv], wcopy_sem.at[kv]) for kv in range(2)]
     for cp in wlocal:
         cp.start()
@@ -82,14 +94,6 @@
              for i, (src, dst) in enumerate(((wq_hbm, wq), (wo_hbm, wo)))]
     for cp in later:
         cp.start()
-
-    barrier = pltpu.get_barrier_semaphore()
-    for off in range(1, n_dev):
-        pl.semaphore_signal(barrier, inc=1, device_id={'model': lax.rem(me + off, n_dev)}, device_id_type=MESH)
-
-    @pl.loop(1, n_rep)
-    def _(off):
-        pl.semaphore_signal(barrier, inc=1, device_id={'replica': lax.rem(rep + off, n_rep)}, device_id_type=MESH)
 
     pl.semaphore_wait(barrier, n_dev + n_rep - 2)
 
@@ -128,38 +132,78 @@
                                  xsend_sem.at[side, ci], xrecv_sem.at[side, ci], aim * 2 + core))
             xsends[-1].start()
 
-    def other_chips():
-        return [lax.rem(chip + off, n_chip) for off in range(1, n_chip)]
+    opposite = lax.rem(chip + 2, n_chip)
+    lane_half = (pl.ds(0, width // 2), pl.ds(width // 2, width // 2))
 
     def sum_pair(index, full, got_ref):
         for c in range(n_chip):
             remote(full.at[:, col(c * 2 + 1 - core)], got_ref.at[c], sum_sem.at[index, 0], sum_sem.at[index, 1], partner).start()
 
-    def sum_chips(index, full, got_ref, pair_ref, recv_ref):
+    def other_chips():
+        return [lax.rem(chip + off, n_chip) for off in range(1, n_chip)]
+
+    def sum_direct(full, got_ref, pair_ref, recv_ref):
+        wait_bytes(got_ref, sum_sem.at[0, 1])
+        for c in range(n_chip):
+            pair_ref[c] = full[:, col(c * 2 + core)] + got_ref[c]
+        for c in other_chips():
+            remote(pair_ref.at[c], recv_ref.at[chip], sum_sem.at[0, 2], sum_sem.at[0, 3], c * 2 + core).start()
+        recv_ref[chip] = pair_ref[chip]
+
+    def gather_direct(buf):
+        for c in other_chips():
+            remote(buf.at[me], buf.at[me], all_sem.at[0, 0], all_sem.at[0, 1], c * 2 + core).start()
+        remote(buf.at[me], buf.at[me], all_sem.at[0, 2], all_sem.at[0, 3], partner).start()
+
+    def gather_direct_end(buf):
+        wait_bytes(buf.at[pl.ds(0, n_chip - 1)], all_sem.at[0, 1])
+        for c in other_chips():
+            remote(buf.at[c * 2 + core], buf.at[c * 2 + core], all_sem.at[0, 2], all_sem.at[0, 3], partner).start()
+        wait_bytes(buf.at[pl.ds(0, n_chip)], all_sem.at[0, 3])
+
+    def sum_far(index, full, got_ref, pair_ref, far_ref):
         wait_bytes(got_ref, sum_sem.at[index, 1])
         for c in range(n_chip):
             pair_ref[c] = full[:, col(c * 2 + core)] + got_ref[c]
-        for c in other_chips():
-            remote(pair_ref.at[c], recv_ref.at[chip], sum_sem.at[index, 2], sum_sem.at[index, 3], c * 2 + core).start()
-        recv_ref[chip] = pair_ref[chip]
-
-    def sum_end(index, recv_ref):
-        wait_bytes(recv_ref.at[pl.ds(0, n_chip - 1)], sum_sem.at[index, 3])
-        return jnp.sum(recv_ref[...], axis=0)
+        for side, aim in ((0, right), (1, left)):
+            remote(pair_ref.at[opposite, :, lane_half[side]], far_ref.at[side], sum_sem.at[index, 2], sum_sem.at[index, 3], aim * 2 + core).start()
+
+    def sum_near(index, pair_ref, far_ref, comb_ref, recv_ref):
+        wait_bytes(far_ref, sum_sem.at[index, 3])
+        for side, aim in ((0, right), (1, left)):
+            comb_ref[side] = pair_ref[aim]
+            comb_ref[side, :, lane_half[side]] = pair_ref[aim, :, lane_half[side]] + far_ref[side]
+            remote(comb_ref.at[side], recv_ref.at[side], sum_sem.at[index, 4], sum_sem.at[index, 5], aim * 2 + core).start()
+
+    def sum_end(index, pair_ref, recv_ref):
+        wait_bytes(recv_ref, sum_sem.at[index, 5])
+        return pair_ref[chip] + recv_ref[0] + recv_ref[1]
+
+    def half_of(ref, side):
+        if ref.shape[1] == width:
+            return ref.at[:, lane_half[side]]
+        return ref.at[pl.ds(side * (ref.shape[0] // 2), ref.shape[0] // 2)]
 
     def gather(index, buf):
-        for c in other_chips():
-            remote(buf.at[me], buf.at[me], all_sem.at[index, 0], all_sem.at[index, 1], c * 2 + core).start()
+        for aim in (right, left):
+            remote(buf.at[me], buf.at[me], all_sem.at[index, 0], all_sem.at[index, 1], aim * 2 + core).start()
         remote(buf.at[me], buf.at[me], all_sem.at[index, 2], all_sem.at[index, 3], partner).start()
 
     def gather_pass(index, buf):
-        wait_bytes(buf.at[pl.ds(0, n_chip - 1)], all_sem.at[index, 1])
-        for c in other_chips():
-            remote(buf.at[c * 2 + core], buf.at[c * 2 + core], all_sem.at[index, 2], all_sem.at[index, 3], partner).start()
+        wait_bytes(buf.at[pl.ds(0, 2)], all_sem.at[index, 1])
+        for side, (source, aim) in enumerate(((left, right), (right, left))):
+            slot = buf.at[source * 2 + core]
+            remote(half_of(slot, side), half_of(slot, side), all_sem.at[index, 4], all_sem.at[index, 5], aim * 2 + core).start()
+            remote(slot, slot, all_sem.at[index, 2], all_sem.at[index, 3], partner).start()
 
     def gather_end(index, buf):
+        wait_bytes(buf.at[0], all_sem.at[index, 5])
+        slot = buf.at[opposite * 2 + core]
+        remote(slot, slot, all_sem.at[index, 2], all_sem.at[index, 3], partner).start()
         wait_bytes(buf.at[pl.ds(0, n_chip)], all_sem.at[index, 3])
 
+    for cp in small:
+        cp.wait()
     gain = gain_ref[...].astype(F32)
 
     def normalize(ref):
@@ -227,7 +271,7 @@
         @pl.when(ch == n_chunk - 1)
         def _():
             pass_on(0, 1)
-            sum_chips(0, lfull, lgot, lpair, lrecv)
+            sum_direct(lfull, lgot, lpair, lrecv)
 
     send_rows(0)
     pass_on(1, 0)
@@ -239,9 +283,58 @@
     near[...] = jnp.where(match, lax.rem(c_idx // 2, seq_loc), far)
 
     pass_on(1, 1)
-    lcols[me] = sum_end(0, lrecv).astype(BF16)
-    gather(0, lcols)
+    wait_bytes(lrecv.at[pl.ds(0, n_chip - 1)], sum_sem.at[0, 3])
+    lcols[me] = jnp.sum(lrecv[...], axis=0).astype(BF16)
+    gather_direct(lcols)
     send_rows(1)
+
+    def received_own(ci):
+        for side in range(2):
+            unit = 2 + side
+            rows_ref = xrecv.at[side, pl.ds(ci * GROUP, GROUP)]
+            wait_bytes(rows_ref, xrecv_sem.at[side, ci])
+            normalize(rows_ref)
+            make_kv(rows_ref, unit, ci, owners[unit], firsts[unit] + ci * GROUP, 0, 1 - core, 2)
+            make_kv(rows_ref, unit, ci, owners[unit], firsts[unit] + ci * GROUP, 0, core, 3)
+
+    def received_far(ci):
+        for side in range(2):
+            unit = 2 + side
+
+            @pl.loop(0, 2)
+            def _(kcore):
+                make_kv(xrecv.at[side, pl.ds(ci * GROUP, GROUP)], unit, ci, owners[unit], firsts[unit] + ci * GROUP, slots[unit], kcore, kcore)
+
+    n_q = 4 * half
+    scale = HEAD_DIM ** -0.5
+    lane = lax.broadcasted_iota(jnp.int32, (n_q, HEAD_DIM), 1)
+    q_row = lax.broadcasted_iota(jnp.int32, (n_q, 1), 0)
+    q_len = []
+    for s in range(2):
+        vec = jnp.zeros((n_q, 1), jnp.int32)
+        for b in range(half):
+            vec = jnp.where(lax.rem(q_row, half) == b, len_ref[s * half + b], vec)
+        q_len.append(vec)
+
+    def partial_att(unit, dst):
+        s = unit % 2
+        target = (aims[unit] * 2, aims[unit] * 2 + 1, partner, me)[dst]
+        q32 = qall[target, s * n_q:(s + 1) * n_q, :]
+        keys = stage.at[unit, dst, 0].reshape(2 * half * seq_loc, HEAD_DIM)[...]
+        vals = stage.at[unit, dst, 1].reshape(2 * half * seq_loc, HEAD_DIM)[...]
+        scores = lax.dot_general(q32, keys, (((1,), (1,)), ((), ())), preferred_element_type=F32) * scale
+        scores = jnp.where(near[...] < q_len[s] - owners[unit] * seq_loc, scores, NEG_BIG)
+        top = jnp.max(scores, axis=1, keepdims=True)
+        prob = jnp.exp(scores - top)
+        total = jnp.sum(prob, axis=1, keepdims=True)
+        acc = dot_f32((prob / total).astype(BF16), vals)
+        dest = prec.at[3, unit] if dst == 3 else psend.at[dst, unit]
+        dest[0] = acc
+        dest[1] = jnp.where(lane < HEAD_DIM // 2, top, total)
+        if dst == 2:
+            remote(psend.at[dst, unit], prec.at[2, unit], p_sem.at[0], p_sem.at[1], partner).start()
+        elif dst < 2:
+            remote(psend.at[dst, unit], prec.at[core, unit], p_sem.at[0], p_sem.at[1], target).start()
 
     rows[0:n_batch, :] = tok_ref[...]
     for b in range(n_batch):
@@ -250,8 +343,8 @@
             crow[pl.ds(r * n_batch + b, 1), :] = cos_ref[pl.ds(at, 1), :]
             srow[pl.ds(r * n_batch + b, 1), :] = sin_ref[pl.ds(at, 1), :]
     later[0].wait()
-    gather_pass(0, lcols)
-    gather_end(0, lcols)
+    received_own(0)
+    gather_direct_end(lcols)
     for j in range(n_dev):
         rows[n_batch:2 * n_batch, j * width:(j + 1) * width] = lcols[j]
     rows_n = rms_rows(rows[...].astype(F32), gain)
@@ -263,7 +356,7 @@
                 qtmp[pl.ds(((s * 2 + r) * 2 + h) * half, half), :] = head[r * n_batch + s * half:r * n_batch + (s + 1) * half]
     qall[me] = qtmp[...].astype(BF16)
     gather(1, qall)
-    for ci in range(2, n_chunk):
+    for ci in range(2, n_chunk - 1):
         send_rows(ci)
     kself[...] = jnp.zeros_like(kself)
     vself[...] = jnp.zeros_like(vself)
@@ -300,23 +393,22 @@
                 make_kv(xown.at[pl.ds(firsts[unit] + ci * GROUP, GROUP)], unit, ci, me, firsts[unit] + ci * GROUP, slots[unit], kcore, kcore)
 
     gather_pass(1, qall)
+    send_rows(n_chunk - 1)
     send_kv(LOTS[0])
 
-    @pl.loop(0, n_chunk)
+    received_far(0)
+
+    @pl.loop(1, n_chunk)
     def _(ci):
-        for side in range(2):
-            unit = 2 + side
-            rows_ref = xrecv.at[side, pl.ds(ci * GROUP, GROUP)]
-            b0 = firsts[unit] + ci * GROUP
-            wait_bytes(rows_ref, xrecv_sem.at[side, ci])
-            normalize(rows_ref)
-
-            @pl.loop(0, 2)
-            def _(kcore):
-                make_kv(rows_ref, unit, ci, owners[unit], b0, slots[unit], kcore, kcore)
-
-            make_kv(rows_ref, unit, ci, owners[unit], b0, 0, 1 - core, 2)
-            make_kv(rows_ref, unit, ci, owners[unit], b0, 0, core, 3)
+        @pl.when(ci == n_chunk - 1)
+        def _():
+            gather_end(1, qall)
+            for dst in range(4):
+                for unit in range(2):
+                    partial_att(unit, dst)
+
+        received_own(ci)
+        received_far(ci)
 
     for cp in wsends + fwds:
         cp.wait_send()
@@ -333,40 +425,8 @@
             mlp_copies.append(pltpu.make_async_copy(src.at[:, pl.ds(j * block, block)], dst, mlp_sem.at[i * 4 + j]))
             mlp_copies[-1].start()
 
-    gather_end(1, qall)
-    n_q = 4 * half
-    scale = HEAD_DIM ** -0.5
-    lane = lax.broadcasted_iota(jnp.int32, (n_q, HEAD_DIM), 1)
-    q_row = lax.broadcasted_iota(jnp.int32, (n_q, 1), 0)
-    q_len = []
-    for s in range(2):
-        vec = jnp.zeros((n_q, 1), jnp.int32)
-        for b in range(half):
-            vec = jnp.where(lax.rem(q_row, half) == b, len_ref[s * half + b], vec)
-        q_len.append(vec)
-
-    def partial_att(unit, dst):
-        s = unit % 2
-        target = (aims[unit] * 2, aims[unit] * 2 + 1, partner, me)[dst]
-        q32 = qall[target, s * n_q:(s + 1) * n_q, :]
-        keys = stage.at[unit, dst, 0].reshape(2 * half * seq_loc, HEAD_DIM)[...]
-        vals = stage.at[unit, dst, 1].reshape(2 * half * seq_loc, HEAD_DIM)[...]
-        scores = lax.dot_general(q32, keys, (((1,), (1,)), ((), ())), preferred_element_type=F32) * scale
-        scores = jnp.where(near[...] < q_len[s] - owners[unit] * seq_loc, scores, NEG_BIG)
-        top = jnp.max(scores, axis=1, keepdims=True)
-        prob = jnp.exp(scores - top)
-        total = jnp.sum(prob, axis=1, keepdims=True)
-        acc = dot_f32(prob.astype(BF16), vals)
-        dest = prec.at[3, unit] if dst == 3 else psend.at[dst, unit]
-        dest[0] = acc
-        dest[1] = jnp.where(lane < HEAD_DIM // 2, top, total)
-        if dst == 2:
-            remote(psend.at[dst, unit], prec.at[2, unit], p_sem.at[0], p_sem.at[1], partner).start()
-        elif dst < 2:
-            remote(psend.at[dst, unit], prec.at[core, unit], p_sem.at[0], p_sem.at[1], target).start()
-
     for dst in range(4):
-        for unit in range(4):
+        for unit in range(2, 4):
             partial_att(unit, dst)
         send_kv(LOTS[1])
 
@@ -386,8 +446,9 @@
                 accs.append(prec[src, unit, 0])
         top = functools.reduce(jnp.maximum, tops)
         facs = [jnp.exp(t - top) for t in tops]
-        total = sum(f * l for f, l in zip(facs, sums))
-        merged = sum(f * a for f, a in zip(facs, accs)) / total
+        facs = [f * l for f, l in zip(facs, sums)]
+        total = sum(facs)
+        merged = sum((f / total) * a for f, a in zip(facs, accs))
         for r in range(2):
             for h in range(2):
                 att[r * n_batch + s * half:r * n_batch + (s + 1) * half, h * HEAD_DIM:(h + 1) * HEAD_DIM] = \
@@ -395,13 +456,16 @@
 
     def add_partials(step):
         sum_pair(1 + step, part.at[step], got.at[step])
-        sum_chips(1 + step, part.at[step], got.at[step], pair.at[step], recv.at[step])
-        send_kv(LOTS[2])
+        sum_far(1 + step, part.at[step], got.at[step], pair.at[step], far_got.at[step])
+        send_kv(LOTS[2 + step])
+        sum_near(1 + step, pair.at[step], far_got.at[step], comb.at[step], recv.at[step])
+        send_kv(LOTS[2 + step])
         mine = rows[:, col(me)].astype(F32)
-        hid[step, me] = (mine + sum_end(1 + step, recv.at[step])).astype(BF16)
+        hid[step, me] = (mine + sum_end(1 + step, pair.at[step], recv.at[step])).astype(BF16)
         gather(2 + step, hid.at[step])
-        send_kv(LOTS[2])
+        send_kv(LOTS[2 + step])
         gather_pass(2 + step, hid.at[step])
+        send_kv(LOTS[2 + step])
         gather_end(2 + step, hid.at[step])
 
     later[1].wait()
@@ -428,12 +492,14 @@
     for cp in xsends:
         cp.wait_send()
     wait_bytes(psend, p_sem.at[0])
-    for index, (got_ref, recv_ref) in enumerate(((lgot, lrecv), (got.at[0], recv.at[0]), (got.at[1], recv.at[1]))):
-        wait_bytes(got_ref, sum_sem.at[index, 0])
-        wait_bytes(recv_ref.at[pl.ds(0, n_chip - 1)], sum_sem.at[index, 2])
+    for index, refs in enumerate(((lgot, lrecv.at[pl.ds(0, n_chip - 1)]), (got.at[0], far_got.at[0], comb.at[0]), (got.at[1], far_got.at[1], comb.at[1]))):
+        for i, ref in enumerate(refs):
+            wait_bytes(ref, sum_sem.at[index, 2 * i])
     for index, buf in enumerate((lcols, qall, hid.at[0], hid.at[1])):
-        wait_bytes(buf.at[pl.ds(0, n_chip - 1)], all_sem.at[index, 0])
+        wait_bytes(buf.at[pl.ds(0, 2 if index else n_chip - 1)], all_sem.at[index, 0])
         wait_bytes(buf.at[pl.ds(0, n_chip)], all_sem.at[index, 2])
+        if index:
+            wait_bytes(buf.at[0], all_sem.at[index, 4])
     for kv in range(2):
         wait_bytes(outs[kv].at[pl.ds(0, 3 * n_batch // 4), pl.ds(0, seq_len)], kv_recv_sem.at[kv])
     wait_bytes(stage.at[:, pl.ds(0, 3)], kv_send_sem)
@@ -491,7 +557,7 @@
         key_cache, val_cache, dec, last = pl.pallas_call(
             functools.partial(layer_kernel, n_dev, n_rep),
             out_shape=(held, held, pltpu.VMEM(tail.shape, BF16), pltpu.VMEM(tail.shape, BF16)),
-            in_specs=[smem] + [hbm] * 8 + [vmem] * 5,
+            in_specs=[smem] + [hbm] * 13,
             out_specs=(vmem,) * 4,
             scratch_shapes=[
                 scratch(3, 2, 2, d_model, kv_width, dtype=BF16),
@@ -513,11 +579,14 @@
                 scratch(3, 4, 2, n_q, HEAD_DIM), scratch(4, 4, 2, n_q, HEAD_DIM),
                 scratch(2 * n_batch, kv_width),
                 scratch(2, 2 * n_batch, d_model), scratch(2, n_chip, 2 * n_batch, width),
-                scratch(2, n_chip, 2 * n_batch, width), scratch(2, n_chip, 2 * n_batch, width),
+                scratch(2, n_chip, 2 * n_batch, width), scratch(2, 2, 2 * n_batch, width // 2),
+                scratch(2, 2, 2 * n_batch, width), scratch(2, 2, 2 * n_batch, width),
                 scratch(2, n_dev, 2 * n_batch, width, dtype=BF16),
+                scratch(n_batch, d_model, dtype=BF16), scratch(1, d_model, dtype=BF16), scratch(1, d_model, dtype=BF16),
+                scratch(seq_len + 8, HEAD_DIM), scratch(seq_len + 8, HEAD_DIM),
                 dma((2 * n_chunk,)), dma((4,)), dma((2, 2, 2)), dma((2, 2, 2)), dma((2, 2)), dma((2, 2, 2)), dma(()), dma((2, 2)),
                 dma((2, n_chunk)), dma((2, n_chunk)),
-                dma((2,)), dma(()), dma((2,)), dma((3, 4)), dma((4, 4)), dma((16,)),
+                dma((2,)), dma(()), dma((2,)), dma((3, 6)), dma((4, 6)), dma((16,)), dma((5,)),
             ],
             compiler_params=pltpu.CompilerParams(collective_id=0, has_side_effects=True, vmem_limit_bytes=VMEM_MIB * 2 ** 20),
             name='layer',

time: 184 us -> 180 us (0.978)
  Pallas kernels: 183 us -> 179 us
    pallas_call x1, Pallas kernels: 178 us -> 174 us  [per_device(): pl.pallas_call(functools.partial(layer_kernel, n_dev, n_rep), out_shape=(...]
where the time goes in v6:
time: 180 us
  Pallas kernels  179 us (99%)
    pallas_call x1, Pallas kernels, per_device(): pl.pallas_call(functools.partial(layer_kernel, n_dev, n_rep), out_shape=(...  174 us
    pallas_call x1, Pallas kernels, per_device(): pl.pallas_call(deliver_kernel, out_shape=(cache, cache, tail, tail), in_s...  4.82 us

profile of v6, /device:TPU:113, one launch (start us, length us, event | category | flops | bytes accessed | tf_op | source)
XLA Modules:
  0.0 179.5 jit_solution(7157756365868213839)
XLA Ops:
  0.6 173.9 %layer.1 = (bf16[16,769,2,128]{3,2,1,0:T(2,128)(2,1)S(1)}, bf16[16,769,2,128]{3,2,1,0:T(2,128)(2,1)S(1)}, bf16[16,2048]{1,0:T(8,128)(2,1)S(1)}, bf16[16,2048]{1,0:T(8,128)(2,1)S(1)}) custom-call(s32[16]{0:T(128)} %len_ref.1, bf16[16,96,2048]{2,1,0:T(8,128)(2,1)} %x_hbm.1, bf16[2048,256]{1,0:T(8,128)(2,1)} %bitcast.12, bf16[2048,256]{1,0:T(8,128)(2,1)} %bitcast.13, ...), custom_call_target="tpu_custom_call" | custom-call | tf_op jit(solution)/shard_map/layer/pallas_call | solution.py:557
  174.5 4.8 %deliver.1 = (bf16[16,769,2,128]{3,2,1,0:T(2,128)(2,1)}, bf16[16,769,2,128]{3,2,1,0:T(2,128)(2,1)}, bf16[16,2048]{1,0:T(8,128)(2,1)}, bf16[16,2048]{1,0:T(8,128)(2,1)}) custom-call(bf16[16,769,2,128]{3,2,1,0:T(2,128)(2,1)S(1)} %get-tuple-element.12.k_in, bf16[16,769,2,128]{3,2,1,0:T(2,128)(2,1)S(1)} %get-tuple-element.13.v_in, ...), custom_call_target="tpu_custom_call" | custom-call | tf_op jit(solution)/shard_map/deliver/pallas_call | solution.py:595

commit v7 on v6

--- a/solution.py
+++ b/solution.py
@@ -13,8 +13,10 @@
 NEG_BIG = -1e30
 MESH = pl.DeviceIdType.MESH
 GROUP = 2
+PARTS = 4
 VMEM_MIB = 49
 LOTS = (8, 1, 3, 2)
+BOTH = (0, 1)
 F32 = jnp.float32
 BF16 = jnp.bfloat16
 
@@ -51,20 +53,29 @@
     n_chip = n_dev // 2
     half = n_batch // 2
     n_chunk = half // GROUP
+    n_all = xcopy_sem.shape[0]
     m_rows = GROUP * seq_loc
+    n_row, n_units = rows.shape[0], stage.shape[0]
     seq_len = seq_loc * n_dev
     width = d_model // n_dev
     me = lax.axis_index('model')
     rep = lax.axis_index('replica')
     chip, core = me // 2, lax.rem(me, 2)
     left, right = lax.rem(chip + n_chip - 1, n_chip), lax.rem(chip + 1, n_chip)
-    partner = chip * 2 + 1 - core
+    other = 1 - core
+    partner = chip * 2 + other
+
+    def same(c):
+        return c * 2 + core
+
     w_hbm = (wk_hbm, wv_hbm)
     outs = (kout, vout)
-    owners = (me, me, left * 2 + core, right * 2 + core)
+    owners = (me, me, same(left), same(right))
     firsts = (0, half, 0, half)
     aims = (left, right, right, left)
     slots = (1, 2, 2, 1)
+    hops = ((1, right), (2, left))
+    sides = ((0, right), (1, left))
 
     def col(j):
         return pl.ds(pl.multiple_of(j * width, width), width)
@@ -81,14 +92,14 @@
              for i, (src, dst) in enumerate(((tok_hbm, tok_ref), (gain_hbm, gain_ref), (gain2_hbm, gain2_ref), (cos_hbm, cos_ref), (sin_hbm, sin_ref)))]
     for cp in small:
         cp.start()
-    wlocal = [pltpu.make_async_copy(w_hbm[kv], wbuf.at[0, core, kv], wcopy_sem.at[kv]) for kv in range(2)]
+    wlocal = [pltpu.make_async_copy(w_hbm[kv], wbuf.at[0, core, kv], wcopy_sem.at[kv]) for kv in BOTH]
     for cp in wlocal:
         cp.start()
 
     def xcopy(ch):
         return pltpu.make_async_copy(x_hbm.at[pl.ds(ch * GROUP, GROUP)], xown.at[pl.ds(ch * GROUP, GROUP)], xcopy_sem.at[ch])
 
-    for ch in range(2 * n_chunk):
+    for ch in range(n_all):
         xcopy(ch).start()
     later = [pltpu.make_async_copy(src, dst, wcopy_sem.at[2 + i])
              for i, (src, dst) in enumerate(((wq_hbm, wq), (wo_hbm, wo)))]
@@ -105,17 +116,17 @@
         return pl.ds(pl.multiple_of(rep * slice_rows + h * sub_rows, sub_rows), sub_rows)
 
     wsends = []
-    for kv in range(2):
+    for kv in BOTH:
         for h in range(n_sub):
-            for slot, aim in ((1, right), (2, left)):
+            for slot, aim in hops:
                 wsends.append(remote(w_hbm[kv].at[w_slice(h)], wbuf.at[slot, core, kv, w_slice(h)],
-                                     wsend_sem.at[slot - 1, kv, h], wrecv_sem.at[slot - 1, kv, h], aim * 2 + core))
+                                     wsend_sem.at[slot - 1, kv, h], wrecv_sem.at[slot - 1, kv, h], same(aim)))
         wsends.append(remote(w_hbm[kv], wbuf.at[0, core, kv], wown_sem.at[0, kv], wown_sem.at[1, kv], partner))
     for cp in wsends:
         cp.start()
 
     def pass_on(kv, h):
-        for slot in (1, 2):
+        for slot, _ in hops:
             block = wbuf.at[slot, core, kv, w_slice(h)]
             wait_bytes(block, wrecv_sem.at[slot - 1, kv, h])
 
@@ -127,9 +138,9 @@
     xsends = []
 
     def send_rows(ci):
-        for side, aim in ((0, right), (1, left)):
+        for side, aim in sides:
             xsends.append(remote(x_hbm.at[pl.ds(side * half + ci * GROUP, GROUP)], xrecv.at[side, pl.ds(ci * GROUP, GROUP)],
-                                 xsend_sem.at[side, ci], xrecv_sem.at[side, ci], aim * 2 + core))
+                                 xsend_sem.at[side, ci], xrecv_sem.at[side, ci], same(aim)))
             xsends[-1].start()
 
     opposite = lax.rem(chip + 2, n_chip)
@@ -137,7 +148,7 @@
 
     def sum_pair(index, full, got_ref):
         for c in range(n_chip):
-            remote(full.at[:, col(c * 2 + 1 - core)], got_ref.at[c], sum_sem.at[index, 0], sum_sem.at[index, 1], partner).start()
+            remote(full.at[:, col(c * 2 + other)], got_ref.at[c], sum_sem.at[index, 0], sum_sem.at[index, 1], partner).start()
 
     def other_chips():
         return [lax.rem(chip + off, n_chip) for off in range(1, n_chip)]
@@ -145,35 +156,35 @@
     def sum_direct(full, got_ref, pair_ref, recv_ref):
         wait_bytes(got_ref, sum_sem.at[0, 1])
         for c in range(n_chip):
-            pair_ref[c] = full[:, col(c * 2 + core)] + got_ref[c]
+            pair_ref[c] = full[:, col(same(c))] + got_ref[c]
         for c in other_chips():
-            remote(pair_ref.at[c], recv_ref.at[chip], sum_sem.at[0, 2], sum_sem.at[0, 3], c * 2 + core).start()
+            remote(pair_ref.at[c], recv_ref.at[chip], sum_sem.at[0, 2], sum_sem.at[0, 3], same(c)).start()
         recv_ref[chip] = pair_ref[chip]
 
     def gather_direct(buf):
         for c in other_chips():
-            remote(buf.at[me], buf.at[me], all_sem.at[0, 0], all_sem.at[0, 1], c * 2 + core).start()
+            remote(buf.at[me], buf.at[me], all_sem.at[0, 0], all_sem.at[0, 1], same(c)).start()
         remote(buf.at[me], buf.at[me], all_sem.at[0, 2], all_sem.at[0, 3], partner).start()
 
     def gather_direct_end(buf):
         wait_bytes(buf.at[pl.ds(0, n_chip - 1)], all_sem.at[0, 1])
         for c in other_chips():
-            remote(buf.at[c * 2 + core], buf.at[c * 2 + core], all_sem.at[0, 2], all_sem.at[0, 3], partner).start()
+            remote(buf.at[same(c)], buf.at[same(c)], all_sem.at[0, 2], all_sem.at[0, 3], partner).start()
         wait_bytes(buf.at[pl.ds(0, n_chip)], all_sem.at[0, 3])
 
     def sum_far(index, full, got_ref, pair_ref, far_ref):
         wait_bytes(got_ref, sum_sem.at[index, 1])
         for c in range(n_chip):
-            pair_ref[c] = full[:, col(c * 2 + core)] + got_ref[c]
-        for side, aim in ((0, right), (1, left)):
-            remote(pair_ref.at[opposite, :, lane_half[side]], far_ref.at[side], sum_sem.at[index, 2], sum_sem.at[index, 3], aim * 2 + core).start()
+            pair_ref[c] = full[:, col(same(c))] + got_ref[c]
+        for side, aim in sides:
+            remote(pair_ref.at[opposite, :, lane_half[side]], far_ref.at[side], sum_sem.at[index, 2], sum_sem.at[index, 3], same(aim)).start()
 
     def sum_near(index, pair_ref, far_ref, comb_ref, recv_ref):
         wait_bytes(far_ref, sum_sem.at[index, 3])
-        for side, aim in ((0, right), (1, left)):
+        for side, aim in sides:
             comb_ref[side] = pair_ref[aim]
             comb_ref[side, :, lane_half[side]] = pair_ref[aim, :, lane_half[side]] + far_ref[side]
-            remote(comb_ref.at[side], recv_ref.at[side], sum_sem.at[index, 4], sum_sem.at[index, 5], aim * 2 + core).start()
+            remote(comb_ref.at[side], recv_ref.at[side], sum_sem.at[index, 4], sum_sem.at[index, 5], same(aim)).start()
 
     def sum_end(index, pair_ref, recv_ref):
         wait_bytes(recv_ref, sum_sem.at[index, 5])
@@ -186,19 +197,19 @@
 
     def gather(index, buf):
         for aim in (right, left):
-            remote(buf.at[me], buf.at[me], all_sem.at[index, 0], all_sem.at[index, 1], aim * 2 + core).start()
+            remote(buf.at[me], buf.at[me], all_sem.at[index, 0], all_sem.at[index, 1], same(aim)).start()
         remote(buf.at[me], buf.at[me], all_sem.at[index, 2], all_sem.at[index, 3], partner).start()
 
     def gather_pass(index, buf):
         wait_bytes(buf.at[pl.ds(0, 2)], all_sem.at[index, 1])
         for side, (source, aim) in enumerate(((left, right), (right, left))):
-            slot = buf.at[source * 2 + core]
-            remote(half_of(slot, side), half_of(slot, side), all_sem.at[index, 4], all_sem.at[index, 5], aim * 2 + core).start()
+            slot = buf.at[same(source)]
+            remote(half_of(slot, side), half_of(slot, side), all_sem.at[index, 4], all_sem.at[index, 5], same(aim)).start()
             remote(slot, slot, all_sem.at[index, 2], all_sem.at[index, 3], partner).start()
 
     def gather_end(index, buf):
         wait_bytes(buf.at[0], all_sem.at[index, 5])
-        slot = buf.at[opposite * 2 + core]
+        slot = buf.at[same(opposite)]
         remote(slot, slot, all_sem.at[index, 2], all_sem.at[index, 3], partner).start()
         wait_bytes(buf.at[pl.ds(0, n_chip)], all_sem.at[index, 3])
 
@@ -215,16 +226,16 @@
         start = pl.multiple_of(owner * seq_loc, seq_loc)
         cos_t = jnp.concatenate([cos_ref[pl.ds(start, seq_loc), :]] * GROUP, axis=0)
         sin_t = jnp.concatenate([sin_ref[pl.ds(start, seq_loc), :]] * GROUP, axis=0)
-        for kv in range(2):
+        for kv in BOTH:
             acc = dot_f32(mat, wbuf[slot, kcore, kv])
-            for h in range(2):
+            for h in BOTH:
                 head = acc[:, h * HEAD_DIM:(h + 1) * HEAD_DIM]
                 if kv == 0:
                     head = rope_half(head, cos_t, sin_t)
                 ktmp[pl.ds(h, m_rows, stride=2), :] = head
             piece = stage.at[unit, dst, kv, pl.ds(ci * GROUP, GROUP)]
             made = ktmp[...].astype(BF16)
-            piece.reshape(2 * m_rows, HEAD_DIM)[...] = made
+            piece.reshape(ktmp.shape[0], HEAD_DIM)[...] = made
             if slot == 0 and dst == 3:
                 for g in range(GROUP):
                     outs[kv].at[b0 + g, pl.ds(start, seq_loc)].reshape(2 * seq_loc, HEAD_DIM)[...] = \
@@ -232,7 +243,7 @@
             elif slot == 0:
                 remote(piece, outs[kv].at[pl.ds(b0, GROUP), pl.ds(start, seq_loc)], kv_send_sem, kv_recv_sem.at[kv], partner).start()
 
-    waiting = [(units, ci, kcore, kv) for units in ((0, 1), (3, 2)) for ci in range(n_chunk) for kcore in range(2) for kv in range(2)]
+    waiting = [(units, ci, kcore, kv) for units in ((0, 1), (3, 2)) for ci in range(n_chunk) for kcore in BOTH for kv in BOTH]
 
     def send_kv(count):
         for _ in range(min(count, len(waiting))):
@@ -247,7 +258,7 @@
         cp.wait()
     base = me * seq_loc
 
-    @pl.loop(0, 2 * n_chunk)
+    @pl.loop(0, n_all)
     def _(ch):
         xcopy(ch).wait()
         own = xown.at[pl.ds(ch * GROUP, GROUP)]
@@ -261,12 +272,12 @@
 
     pass_on(0, 0)
     sum_pair(0, lfull, lgot)
-    for kv in range(2):
-        wait_bytes(wbuf.at[0, 1 - core, kv], wown_sem.at[1, kv])
-
-    @pl.loop(0, 2 * n_chunk)
+    for kv in BOTH:
+        wait_bytes(wbuf.at[0, other, kv], wown_sem.at[1, kv])
+
+    @pl.loop(0, n_all)
     def _(ch):
-        make_kv(xown.at[pl.ds(ch * GROUP, GROUP)], ch // n_chunk, lax.rem(ch, n_chunk), me, ch * GROUP, 0, 1 - core, 2)
+        make_kv(xown.at[pl.ds(ch * GROUP, GROUP)], ch // n_chunk, lax.rem(ch, n_chunk), me, ch * GROUP, 0, other, 2)
 
         @pl.when(ch == n_chunk - 1)
         def _():
@@ -289,16 +300,16 @@
     send_rows(1)
 
     def received_own(ci):
-        for side in range(2):
+        for side in BOTH:
             unit = 2 + side
             rows_ref = xrecv.at[side, pl.ds(ci * GROUP, GROUP)]
             wait_bytes(rows_ref, xrecv_sem.at[side, ci])
             normalize(rows_ref)
-            make_kv(rows_ref, unit, ci, owners[unit], firsts[unit] + ci * GROUP, 0, 1 - core, 2)
+            make_kv(rows_ref, unit, ci, owners[unit], firsts[unit] + ci * GROUP, 0, other, 2)
             make_kv(rows_ref, unit, ci, owners[unit], firsts[unit] + ci * GROUP, 0, core, 3)
 
     def received_far(ci):
-        for side in range(2):
+        for side in BOTH:
             unit = 2 + side
 
             @pl.loop(0, 2)
@@ -310,7 +321,7 @@
     lane = lax.broadcasted_iota(jnp.int32, (n_q, HEAD_DIM), 1)
     q_row = lax.broadcasted_iota(jnp.int32, (n_q, 1), 0)
     q_len = []
-    for s in range(2):
+    for s in BOTH:
         vec = jnp.zeros((n_q, 1), jnp.int32)
         for b in range(half):
             vec = jnp.where(lax.rem(q_row, half) == b, len_ref[s * half + b], vec)
@@ -338,7 +349,7 @@
 
     rows[0:n_batch, :] = tok_ref[...]
     for b in range(n_batch):
-        for r in range(2):
+        for r in BOTH:
             at = jnp.maximum(len_ref[b] - r, 0)
             crow[pl.ds(r * n_batch + b, 1), :] = cos_ref[pl.ds(at, 1), :]
             srow[pl.ds(r * n_batch + b, 1), :] = sin_ref[pl.ds(at, 1), :]
@@ -346,13 +357,13 @@
     received_own(0)
     gather_direct_end(lcols)
     for j in range(n_dev):
-        rows[n_batch:2 * n_batch, j * width:(j + 1) * width] = lcols[j]
+        rows[n_batch:n_row, j * width:(j + 1) * width] = lcols[j]
     rows_n = rms_rows(rows[...].astype(F32), gain)
     q_acc = dot_f32(rows_n, wq[...])
-    for h in range(2):
+    for h in BOTH:
         head = rope_half(q_acc[:, h * HEAD_DIM:(h + 1) * HEAD_DIM], crow[...], srow[...])
-        for r in range(2):
-            for s in range(2):
+        for r in BOTH:
+            for s in BOTH:
                 qtmp[pl.ds(((s * 2 + r) * 2 + h) * half, half), :] = head[r * n_batch + s * half:r * n_batch + (s + 1) * half]
     qall[me] = qtmp[...].astype(BF16)
     gather(1, qall)
@@ -362,34 +373,34 @@
     vself[...] = jnp.zeros_like(vself)
     for kv, (new, own) in enumerate(((knew, kself), (vnew, vself))):
         acc = dot_f32(rows_n[0:n_batch], wbuf[0, core, kv])
-        for h in range(2):
+        for h in BOTH:
             head = acc[:, h * HEAD_DIM:(h + 1) * HEAD_DIM]
             if kv == 0:
                 head = rope_half(head, crow[0:n_batch, :], srow[0:n_batch, :])
             ktmp[pl.ds(h, n_batch, stride=2), :] = head
             head = head.astype(BF16).astype(F32)
-            for s in range(2):
+            for s in BOTH:
                 own[pl.ds((s * 4 + h) * half, half), :] = head[s * half:(s + 1) * half]
-        new.reshape(2 * n_batch, HEAD_DIM)[...] = ktmp[0:2 * n_batch, :].astype(BF16)
+        new.reshape(n_row, HEAD_DIM)[...] = ktmp[0:n_row, :].astype(BF16)
         for b in range(n_batch):
             outs[kv][b, seq_len] = new[b]
 
     fwds = []
-    for kv in range(2):
-        for slot in (1, 2):
+    for kv in BOTH:
+        for slot, _ in hops:
             if n_rep > 1:
                 wait_bytes(wbuf.at[slot, core, kv, pl.ds(0, d_model - slice_rows)], yrecv_sem.at[slot - 1, kv])
             fwds.append(remote(wbuf.at[slot, core, kv], wbuf.at[slot, core, kv], wfwd_sem.at[0, slot - 1, kv], wfwd_sem.at[1, slot - 1, kv], partner))
             fwds[-1].start()
-    for kv in range(2):
-        for slot in (1, 2):
-            wait_bytes(wbuf.at[slot, 1 - core, kv], wfwd_sem.at[1, slot - 1, kv])
+    for kv in BOTH:
+        for slot, _ in hops:
+            wait_bytes(wbuf.at[slot, other, kv], wfwd_sem.at[1, slot - 1, kv])
 
     @pl.loop(0, n_chunk)
     def _(ci):
         @pl.loop(0, 2)
         def _(kcore):
-            for unit in range(2):
+            for unit in BOTH:
                 make_kv(xown.at[pl.ds(firsts[unit] + ci * GROUP, GROUP)], unit, ci, me, firsts[unit] + ci * GROUP, slots[unit], kcore, kcore)
 
     gather_pass(1, qall)
@@ -403,8 +414,8 @@
         @pl.when(ci == n_chunk - 1)
         def _():
             gather_end(1, qall)
-            for dst in range(4):
-                for unit in range(2):
+            for dst in range(n_units):
+                for unit in BOTH:
                     partial_att(unit, dst)
 
         received_own(ci)
@@ -413,7 +424,7 @@
     for cp in wsends + fwds:
         cp.wait_send()
     if n_rep > 1:
-        for slot in (1, 2):
+        for slot, _ in hops:
             wait_bytes(wbuf.at[slot, 0, :, pl.ds(0, d_model - slice_rows)], ysend_sem)
     ff, block = wd_hbm.shape[0], wbuf.shape[4]
     places = [wbuf.at[i // 4, (i // 2) % 2, i % 2] for i in range(12)]
@@ -425,13 +436,13 @@
             mlp_copies.append(pltpu.make_async_copy(src.at[:, pl.ds(j * block, block)], dst, mlp_sem.at[i * 4 + j]))
             mlp_copies[-1].start()
 
-    for dst in range(4):
+    for dst in range(n_units):
         for unit in range(2, 4):
             partial_att(unit, dst)
         send_kv(LOTS[1])
 
     wait_bytes(prec.at[pl.ds(0, 3)], p_sem.at[1])
-    for s in range(2):
+    for s in BOTH:
         q32 = qall[me, s * n_q:(s + 1) * n_q, :].astype(F32)
         is_new = q_row < n_q // 2
         self_score = jnp.sum(q32 * kself[s * n_q:(s + 1) * n_q, :], axis=1, keepdims=True) * scale
@@ -439,7 +450,7 @@
         sums = [jnp.where(is_new, 1.0, 0.0)]
         accs = [vself[s * n_q:(s + 1) * n_q, :]]
         for unit in (s, s + 2):
-            for src in range(4):
+            for src in range(n_units):
                 stat = prec[src, unit, 1]
                 tops.append(stat[:, 0:1])
                 sums.append(stat[:, HEAD_DIM // 2:HEAD_DIM // 2 + 1])
@@ -449,8 +460,8 @@
         facs = [f * l for f, l in zip(facs, sums)]
         total = sum(facs)
         merged = sum((f / total) * a for f, a in zip(facs, accs))
-        for r in range(2):
-            for h in range(2):
+        for r in BOTH:
+            for h in BOTH:
                 att[r * n_batch + s * half:r * n_batch + (s + 1) * half, h * HEAD_DIM:(h + 1) * HEAD_DIM] = \
                     merged[(r * 2 + h) * half:(r * 2 + h + 1) * half]
 
@@ -487,7 +498,7 @@
     send_kv(len(waiting))
     for j in range(n_dev):
         dec_out[:, j * width:(j + 1) * width] = hid[1, j, 0:n_batch, :]
-        last_out[:, j * width:(j + 1) * width] = hid[1, j, n_batch:2 * n_batch, :]
+        last_out[:, j * width:(j + 1) * width] = hid[1, j, n_batch:n_row, :]
 
     for cp in xsends:
         cp.wait_send()
@@ -500,14 +511,15 @@
         wait_bytes(buf.at[pl.ds(0, n_chip)], all_sem.at[index, 2])
         if index:
             wait_bytes(buf.at[0], all_sem.at[index, 4])
-    for kv in range(2):
+    for kv in BOTH:
         wait_bytes(outs[kv].at[pl.ds(0, 3 * n_batch // 4), pl.ds(0, seq_len)], kv_recv_sem.at[kv])
     wait_bytes(stage.at[:, pl.ds(0, 3)], kv_send_sem)
 
 
 def deliver_kernel(k_in, v_in, d_in, l_in, k_out, v_out, d_out, l_out, sem):
-    copies = [pltpu.make_async_copy(src, dst, sem.at[i])
-              for i, (src, dst) in enumerate(((k_in, k_out), (v_in, v_out), (d_in, d_out), (l_in, l_out)))]
+    part = k_in.shape[0] // PARTS
+    pairs = [(src.at[pl.ds(i * part, part)], dst.at[pl.ds(i * part, part)]) for i in range(PARTS) for src, dst in ((k_in, k_out), (v_in, v_out))]
+    copies = [pltpu.make_async_copy(src, dst, sem.at[i]) for i, (src, dst) in enumerate(pairs + [(d_in, d_out), (l_in, l_out)])]
     for cp in copies:
         cp.start()
     for cp in copies:
@@ -548,8 +560,9 @@
         cos_tab, sin_tab = (jnp.asarray(t) for t in rotary_tables(seq_len + 8))
 
         ff = wg.shape[1]
-        n_q = 4 * half
+        n_q, n_row, two = 4 * half, 2 * n_batch, dma((2,))
         cache = jax.ShapeDtypeStruct((n_batch, seq_len + 1, heads, HEAD_DIM), BF16)
+        cube, square, chunked = dma((2, 2, 2)), dma((2, 2)), dma((2, n_chunk))
         scratch = lambda *shape, dtype=F32: pltpu.VMEM(shape, dtype)
         held = pltpu.VMEM(cache.shape, BF16)
         tail = jax.ShapeDtypeStruct((n_batch, d_model), BF16)
@@ -570,23 +583,23 @@
                 scratch(n_batch, d_model), scratch(n_chip, n_batch, width),
                 scratch(n_chip, n_batch, width), scratch(n_chip, n_batch, width),
                 scratch(n_dev, n_batch, width, dtype=BF16),
-                scratch(2 * n_batch, HEAD_DIM), scratch(2 * n_batch, HEAD_DIM),
-                scratch(2 * n_batch, d_model, dtype=BF16),
+                scratch(n_row, HEAD_DIM), scratch(n_row, HEAD_DIM),
+                scratch(n_row, d_model, dtype=BF16),
                 scratch(2 * n_q, HEAD_DIM), scratch(n_dev, 2 * n_q, HEAD_DIM, dtype=BF16),
                 scratch(n_batch, heads, HEAD_DIM, dtype=BF16), scratch(n_batch, heads, HEAD_DIM, dtype=BF16),
                 scratch(2 * n_q, HEAD_DIM), scratch(2 * n_q, HEAD_DIM),
                 scratch(n_q, 2 * half * seq_loc, dtype=jnp.int32),
                 scratch(3, 4, 2, n_q, HEAD_DIM), scratch(4, 4, 2, n_q, HEAD_DIM),
-                scratch(2 * n_batch, kv_width),
-                scratch(2, 2 * n_batch, d_model), scratch(2, n_chip, 2 * n_batch, width),
-                scratch(2, n_chip, 2 * n_batch, width), scratch(2, 2, 2 * n_batch, width // 2),
-                scratch(2, 2, 2 * n_batch, width), scratch(2, 2, 2 * n_batch, width),
-                scratch(2, n_dev, 2 * n_batch, width, dtype=BF16),
+                scratch(n_row, kv_width),
+                scratch(2, n_row, d_model), scratch(2, n_chip, n_row, width),
+                scratch(2, n_chip, n_row, width), scratch(2, 2, n_row, width // 2),
+                scratch(2, 2, n_row, width), scratch(2, 2, n_row, width),
+                scratch(2, n_dev, n_row, width, dtype=BF16),
                 scratch(n_batch, d_model, dtype=BF16), scratch(1, d_model, dtype=BF16), scratch(1, d_model, dtype=BF16),
                 scratch(seq_len + 8, HEAD_DIM), scratch(seq_len + 8, HEAD_DIM),
-                dma((2 * n_chunk,)), dma((4,)), dma((2, 2, 2)), dma((2, 2, 2)), dma((2, 2)), dma((2, 2, 2)), dma(()), dma((2, 2)),
-                dma((2, n_chunk)), dma((2, n_chunk)),
-                dma((2,)), dma(()), dma((2,)), dma((3, 6)), dma((4, 6)), dma((16,)), dma((5,)),
+                dma((2 * n_chunk,)), dma((4,)), cube, cube, square, cube, dma(()), square,
+                chunked, chunked,
+                two, dma(()), two, dma((3, 6)), dma((4, 6)), dma((16,)), dma((5,)),
             ],
             compiler_params=pltpu.CompilerParams(collective_id=0, has_side_effects=True, vmem_limit_bytes=VMEM_MIB * 2 ** 20),
             name='layer',
@@ -594,7 +607,7 @@
             (lengths, prompt, wk, wv, wq, wo, wg, wu, wd, new_tok, norm_attn, norm_mlp, cos_tab, sin_tab)))
         key_cache, val_cache, dec, last = pl.pallas_call(
             deliver_kernel, out_shape=(cache, cache, tail, tail), in_specs=[vmem] * 4, out_specs=(hbm,) * 4,
-            scratch_shapes=[dma((4,))], name='deliver',
+            scratch_shapes=[dma((2 * PARTS + 2,))], name='deliver',
             compiler_params=pltpu.CompilerParams(vmem_limit_bytes=14 * 2 ** 20),
         )(key_cache, val_cache, dec, last)
         return dec, last, key_cache[None], val_cache[None]

time: 180 us -> 179 us (level)
  no operation moved by 1% of the time
where the time goes in v7:
time: 179 us
  Pallas kernels  179 us (100%)
    pallas_call x1, Pallas kernels, per_device(): pl.pallas_call(functools.partial(layer_kernel, n_dev, n_rep), out_shape=(...  174 us
    pallas_call x1, Pallas kernels, per_device(): pl.pallas_call(deliver_kernel, out_shape=(cache, cache, tail, tail), in_s...  4.69 us

profile of v7, /device:TPU:113, one launch (start us, length us, event | category | flops | bytes accessed | tf_op | source)
XLA Modules:
  0.0 179.4 jit_solution(11877695778132252122)
XLA Ops:
  0.6 173.9 %layer.1 = (bf16[16,769,2,128]{3,2,1,0:T(2,128)(2,1)S(1)}, bf16[16,769,2,128]{3,2,1,0:T(2,128)(2,1)S(1)}, bf16[16,2048]{1,0:T(8,128)(2,1)S(1)}, bf16[16,2048]{1,0:T(8,128)(2,1)S(1)}) custom-call(s32[16]{0:T(128)} %len_ref.1, bf16[16,96,2048]{2,1,0:T(8,128)(2,1)} %x_hbm.1, bf16[2048,256]{1,0:T(8,128)(2,1)} %bitcast.12, bf16[2048,256]{1,0:T(8,128)(2,1)} %bitcast.13, ...), custom_call_target="tpu_custom_call" | custom-call | tf_op jit(solution)/shard_map/layer/pallas_call | solution.py:570
  174.5 4.7 %deliver.1 = (bf16[16,769,2,128]{3,2,1,0:T(2,128)(2,1)}, bf16[16,769,2,128]{3,2,1,0:T(2,128)(2,1)}, bf16[16,2048]{1,0:T(8,128)(2,1)}, bf16[16,2048]{1,0:T(8,128)(2,1)}) custom-call(bf16[16,769,2,128]{3,2,1,0:T(2,128)(2,1)S(1)} %get-tuple-element.12.k_in, bf16[16,769,2,128]{3,2,1,0:T(2,128)(2,1)S(1)} %get-tuple-element.13.v_in, ...), custom_call_target="tpu_custom_call" | custom-call | tf_op jit(solution)/shard_map/deliver/pallas_call | solution.py:608

commit v8 on v7

--- a/solution.py
+++ b/solution.py
@@ -43,7 +43,7 @@
     pltpu.make_async_copy(ref, ref, sem).wait()
 
 
-def layer_kernel(n_dev, n_rep, len_ref, x_hbm, wk_hbm, wv_hbm, wq_hbm, wo_hbm, wg_hbm, wu_hbm, wd_hbm, tok_hbm, gain_hbm, gain2_hbm, cos_hbm, sin_hbm,
+def layer_kernel(n_dev, n_pair, len_ref, x_hbm, wk_hbm, wv_hbm, wq_hbm, wo_hbm, wg_hbm, wu_hbm, wd_hbm, tok_hbm, gain_hbm, gain2_hbm, cos_hbm, sin_hbm,
                  kout, vout, dec_out, last_out,
                  wbuf, wq, wo, xown, xrecv, stage, ktmp, lfull, lgot, lpair, lrecv, lcols, crow, srow,
                  rows, qtmp, qall, knew, vnew, kself, vself, near, psend, prec, att, part, got, pair, far_got, comb, recv, hid, tok_ref, gain_ref, gain2_ref, cos_ref, sin_ref,
@@ -60,6 +60,8 @@
     width = d_model // n_dev
     me = lax.axis_index('model')
     rep = lax.axis_index('replica')
+    turn = lax.rem(rep, n_pair)
+    twin = rep + 1 - 2 * turn
     chip, core = me // 2, lax.rem(me, 2)
     left, right = lax.rem(chip + n_chip - 1, n_chip), lax.rem(chip + 1, n_chip)
     other = 1 - core
@@ -84,9 +86,8 @@
     for off in range(1, n_dev):
         pl.semaphore_signal(barrier, inc=1, device_id={'model': lax.rem(me + off, n_dev)}, device_id_type=MESH)
 
-    @pl.loop(1, n_rep)
-    def _(off):
-        pl.semaphore_signal(barrier, inc=1, device_id={'replica': lax.rem(rep + off, n_rep)}, device_id_type=MESH)
+    if n_pair > 1:
+        pl.semaphore_signal(barrier, inc=1, device_id={'replica': twin}, device_id_type=MESH)
 
     small = [pltpu.make_async_copy(src, dst, small_sem.at[i])
              for i, (src, dst) in enumerate(((tok_hbm, tok_ref), (gain_hbm, gain_ref), (gain2_hbm, gain2_ref), (cos_hbm, cos_ref), (sin_hbm, sin_ref)))]
@@ -106,14 +107,14 @@
     for cp in later:
         cp.start()
 
-    pl.semaphore_wait(barrier, n_dev + n_rep - 2)
+    pl.semaphore_wait(barrier, n_dev + n_pair - 2)
 
     n_sub = 2
-    slice_rows = d_model // n_rep
+    slice_rows = d_model // n_pair
     sub_rows = slice_rows // n_sub
 
     def w_slice(h):
-        return pl.ds(pl.multiple_of(rep * slice_rows + h * sub_rows, sub_rows), sub_rows)
+        return pl.ds(pl.multiple_of(turn * slice_rows + h * sub_rows, sub_rows), sub_rows)
 
     wsends = []
     for kv in BOTH:
@@ -130,10 +131,9 @@
             block = wbuf.at[slot, core, kv, w_slice(h)]
             wait_bytes(block, wrecv_sem.at[slot - 1, kv, h])
 
-            @pl.loop(1, n_rep)
-            def _(off):
+            if n_pair > 1:
                 pltpu.make_async_remote_copy(src_ref=block, dst_ref=block, send_sem=ysend_sem, recv_sem=yrecv_sem.at[slot - 1, kv],
-                                             device_id={'replica': lax.rem(rep + off, n_rep)}, device_id_type=MESH).start()
+                                             device_id={'replica': twin}, device_id_type=MESH).start()
 
     xsends = []
 
@@ -388,7 +388,7 @@
     fwds = []
     for kv in BOTH:
         for slot, _ in hops:
-            if n_rep > 1:
+            if n_pair > 1:
                 wait_bytes(wbuf.at[slot, core, kv, pl.ds(0, d_model - slice_rows)], yrecv_sem.at[slot - 1, kv])
             fwds.append(remote(wbuf.at[slot, core, kv], wbuf.at[slot, core, kv], wfwd_sem.at[0, slot - 1, kv], wfwd_sem.at[1, slot - 1, kv], partner))
             fwds[-1].start()
@@ -423,7 +423,7 @@
 
     for cp in wsends + fwds:
         cp.wait_send()
-    if n_rep > 1:
+    if n_pair > 1:
         for slot, _ in hops:
             wait_bytes(wbuf.at[slot, 0, :, pl.ds(0, d_model - slice_rows)], ysend_sem)
     ff, block = wd_hbm.shape[0], wbuf.shape[4]
@@ -534,7 +534,8 @@
 
 
 def solution(mesh):
-    n_dev, n_rep = mesh.shape['model'], mesh.shape['replica']
+    n_dev = mesh.shape['model']
+    n_pair = 1 + (mesh.shape['replica'] + 1) % 2
     seq_spec = P('replica', 'model', None)
     col_spec = P(None, None, 'model')
     row_spec = P(None, 'model', None)
@@ -568,7 +569,7 @@
         tail = jax.ShapeDtypeStruct((n_batch, d_model), BF16)
         n_chip = n_dev // 2
         key_cache, val_cache, dec, last = pl.pallas_call(
-            functools.partial(layer_kernel, n_dev, n_rep),
+            functools.partial(layer_kernel, n_dev, n_pair),
             out_shape=(held, held, pltpu.VMEM(tail.shape, BF16), pltpu.VMEM(tail.shape, BF16)),
             in_specs=[smem] + [hbm] * 13,
             out_specs=(vmem,) * 4,

time: 179 us -> 179 us (level)
  no operation moved by 1% of the time
where the time goes in v8:
time: 179 us
  Pallas kernels  179 us (100%)
    pallas_call x1, Pallas kernels, per_device(): pl.pallas_call(functools.partial(layer_kernel, n_dev, n_pair), out_shape=...  174 us
    pallas_call x1, Pallas kernels, per_device(): pl.pallas_call(deliver_kernel, out_shape=(cache, cache, tail, tail), in_s...  4.69 us

profile of v8, /device:TPU:113, one launch (start us, length us, event | category | flops | bytes accessed | tf_op | source)
XLA Modules:
  0.0 179.4 jit_solution(11983527773152346054)
XLA Ops:
  0.6 173.9 %layer.1 = (bf16[16,769,2,128]{3,2,1,0:T(2,128)(2,1)S(1)}, bf16[16,769,2,128]{3,2,1,0:T(2,128)(2,1)S(1)}, bf16[16,2048]{1,0:T(8,128)(2,1)S(1)}, bf16[16,2048]{1,0:T(8,128)(2,1)S(1)}) custom-call(s32[16]{0:T(128)} %len_ref.1, bf16[16,96,2048]{2,1,0:T(8,128)(2,1)} %x_hbm.1, bf16[2048,256]{1,0:T(8,128)(2,1)} %bitcast.12, bf16[2048,256]{1,0:T(8,128)(2,1)} %bitcast.13, ...), custom_call_target="tpu_custom_call" | custom-call | tf_op jit(solution)/shard_map/layer/pallas_call | solution.py:571
  174.5 4.7 %deliver.1 = (bf16[16,769,2,128]{3,2,1,0:T(2,128)(2,1)}, bf16[16,769,2,128]{3,2,1,0:T(2,128)(2,1)}, bf16[16,2048]{1,0:T(8,128)(2,1)}, bf16[16,2048]{1,0:T(8,128)(2,1)}) custom-call(bf16[16,769,2,128]{3,2,1,0:T(2,128)(2,1)S(1)} %get-tuple-element.12.k_in, bf16[16,769,2,128]{3,2,1,0:T(2,128)(2,1)S(1)} %get-tuple-element.13.v_in, ...), custom_call_target="tpu_custom_call" | custom-call | tf_op jit(solution)/shard_map/deliver/pallas_call | solution.py:609
